TPU v7x, 768 devices: a whole 4x8x12 slice. The times are simulated.
768 devices in a mesh: grp: 32 (over x_lo, y, core), tp: 24 (over x_hi, z).
Axes of the slice: x: 4 (x_hi: 2, x_lo: 2; x = x_hi * 2 + x_lo), y: 8, z: 12, core: 2. Of those that a mesh axis runs over, the one named last changes fastest.
Arguments:
- queries: bfloat16 [128, 2, 4096], P('grp'), may hold values from -8 to 8
- cache_keys: bfloat16 [128, 3072, 512], P('grp', 'tp'), may hold values from -8 to 8
- cache_values: bfloat16 [128, 3072, 512], P('grp', 'tp'), may hold values from -6 to 6
- new_keys: bfloat16 [128, 2, 512], P('grp'), may hold values from -6 to 6
- new_values: bfloat16 [128, 2, 512], P('grp'), may hold values from -6 to 6
- lengths: int32 [128], P('grp'), may hold values from 2 to 3072
- residual: bfloat16 [128, 2, 4096], P('grp'), may hold values from -0.1796875 to 0.1796875
- norm_gain: float32 [4096], replicated, may hold values from 0.25 to 1.75
- w_gate: float32 [4096, 14400], P('grp', 'tp'), may hold values from -0.09375 to 0.09375
- w_down: float32 [4096, 14400], P('grp', 'tp'), may hold values from -0.046875 to 0.046875
Outputs:
- mixed: bfloat16 [128, 2, 4096], P('grp')
All inputs are finite; a program needn't handle non-finite values.
Results may differ from a plain program's by a relative error of at most 0.028.
Values may be sent and summed in bfloat16 or wider, within the bound.
No kernel may reach another device: no remote copies, remote signals or barrier semaphores. Data moves between devices by JAX's collectives and lax.ppermute only.
A program may use at most 32 MiB of HBM per device.

v0:
```python
import jax
import jax.numpy as jnp
from jax import lax
from jax.sharding import Mesh
from jax.sharding import PartitionSpec as P

HD = 128
KVH = 4
TP = ("tp_0", "tp_1")


masked_score = -1e30


def gathered_once(shard, axis):
    leaves = jax.tree.leaves(shard)
    sequence = sorted(range(len(leaves)), key=lambda k: -leaves[k].size)
    width = (1, *leaves[sequence[0]].shape)[-1]
    lines = [
        jnp.pad(leaves[k].reshape(-1), (0, -leaves[k].size % width)).reshape(-1, width)
        for k in sequence
    ]
    both, at, found = (lax.all_gather(jnp.concatenate(lines), axis), 0, {})
    for k, line in zip(sequence, lines):
        slab = both[:, at : at + len(line)].reshape(len(both), -1)
        found[k] = slab[:, : leaves[k].size].reshape(-1, *leaves[k].shape)
        at += len(line)
    numbers = iter(range(len(leaves)))
    return jax.tree.map(lambda _: found[next(numbers)], shard)


def joined_all(shard, axes, combine):
    for axis in axes:
        pieces = gathered_once(
            jax.tree.map(
                lambda part, kind: part.astype(kind),
                shard,
                jax.tree.map(lambda a: jnp.bfloat16 if a.dtype == jnp.float32 else a.dtype, shard),
            ),
            axis,
        )
        widened = [
            jax.tree.map(lambda part, own: part[k].astype(own.dtype), pieces, shard)
            for k in range(lax.axis_size(axis))
        ]
        shard = widened[0]
        for partner_block in widened[1:]:
            shard = combine(shard, partner_block)
    return shard


def split_up(shard, dim, count):
    dims = shard.shape
    parts = shard.reshape(*dims[:dim], count, dims[dim] // count, *dims[dim + 1 :])
    return jnp.moveaxis(parts, dim, 0)


def summed_on_arrival(shard, axis, dim):
    parts = split_up(shard, dim, lax.axis_size(axis))
    arrived = lax.all_to_all(parts, axis, split_axis=0, concat_axis=0, tiled=True)
    return arrived.astype(jnp.float32).sum(axis=0)


def copy_for_each(shard, axis):
    copies = jnp.broadcast_to(shard, (lax.axis_size(axis), *shard.shape))
    return lax.all_to_all(copies, axis, split_axis=0, concat_axis=0, tiled=True)


def joined_along(parts, dim):
    parts = jnp.moveaxis(parts, 0, dim)
    dims = parts.shape
    return parts.reshape(*dims[:dim], dims[dim] * dims[dim + 1], *dims[dim + 2 :])


def gather_directly(shard, axis, dim):
    parts = copy_for_each(shard, axis)
    return joined_along(parts, dim)


def taken_together(shard, axis):
    return copy_for_each(shard, axis).astype(jnp.float32).sum(axis=0)


def combine_parts(earlier, later):
    first_max, first_total, first_accum = earlier
    second_max, second_total, second_accum = later
    joint_max = jnp.maximum(first_max, second_max)
    first_factor = jnp.exp(first_max - joint_max)
    second_factor = jnp.exp(second_max - joint_max)
    joint_total = first_total * first_factor + second_total * second_factor
    joint_accum = first_accum * first_factor[..., None] + second_accum * second_factor[..., None]
    return (joint_max, joint_total, joint_accum)


def partial_softmax(scores, visible, value_heads, formula):
    scores = jnp.where(visible, scores, masked_score)
    highest = jnp.max(scores, axis=-1)
    weights = jnp.where(visible, jnp.exp(scores - highest[..., None]), 0.0)
    totals = jnp.sum(weights, axis=-1)
    accum = jnp.einsum(
        formula, weights.astype(jnp.bfloat16), value_heads, preferred_element_type=jnp.float32
    )
    return (highest, totals, accum)


def shards(
    queries,
    cache_keys,
    cache_values,
    new_keys,
    new_values,
    lengths,
    residual,
    norm_gain,
    w_gate,
    w_down,
):
    row_count, step_count, features = queries.shape
    positions = cache_keys.shape[1]
    per_group = features // (KVH * HD)
    inv_root = HD ** (-0.5)
    query_heads = queries.reshape(row_count, step_count, KVH, per_group, HD)
    key_heads = cache_keys.reshape(row_count, positions, KVH, HD)
    value_heads = cache_values.reshape(row_count, positions, KVH, HD)
    cached_scores = (
        jnp.einsum("rsjgd,rcjd->rsjgc", query_heads, key_heads, preferred_element_type=jnp.float32)
        * inv_root
    )
    offset = lax.axis_index(TP) * positions
    places = offset + lax.broadcasted_iota(jnp.int32, (row_count, positions), 1)
    visible = (places < lengths[:, None])[:, None, None, None, :]
    local_part = partial_softmax(cached_scores, visible, value_heads, "rsjgc,rcjd->rsjgd")
    merged = joined_all(local_part, TP, combine_parts)
    fresh_key_heads = new_keys.reshape(row_count, step_count, KVH, HD)
    fresh_value_heads = new_values.reshape(row_count, step_count, KVH, HD)
    fresh_scores = (
        jnp.einsum(
            "rsjgd,rtjd->rsjgt", query_heads, fresh_key_heads, preferred_element_type=jnp.float32
        )
        * inv_root
    )
    causal = lax.broadcasted_iota(jnp.int32, (step_count, step_count), 0) >= lax.broadcasted_iota(
        jnp.int32, (step_count, step_count), 1
    )
    causal = causal[None, :, None, None, :]
    fresh_part = partial_softmax(fresh_scores, causal, fresh_value_heads, "rsjgt,rtjd->rsjgd")
    joint_max, joint_total, joint_accum = combine_parts(merged, fresh_part)
    context = (joint_accum / joint_total[..., None]).reshape(row_count, step_count, features)
    summed = residual.astype(jnp.float32) + context
    mean_square = jnp.mean(summed * summed, axis=-1, keepdims=True)
    normed = (summed * lax.rsqrt(mean_square + 1e-05) * norm_gain).astype(jnp.bfloat16)
    flat = normed.reshape(row_count * step_count, features)
    spread_rows = lax.all_to_all(flat, "grp", split_axis=1, concat_axis=0, tiled=True)
    gate_local = w_gate.astype(jnp.bfloat16)
    gate = summed_on_arrival(
        jnp.dot(spread_rows, gate_local, preferred_element_type=jnp.float32).astype(jnp.bfloat16),
        "grp",
        0,
    )
    hidden = jax.nn.silu(gate).astype(jnp.bfloat16)
    down_local = w_down.astype(jnp.bfloat16)
    feature_terms = lax.dot_general(
        gather_directly(hidden, "grp", 0),
        down_local,
        (((1,), (1,)), ((), ())),
        preferred_element_type=jnp.float32,
    )
    partial_sum = lax.all_to_all(
        feature_terms.astype(jnp.bfloat16), "grp", split_axis=0, concat_axis=1, tiled=True
    ).astype(feature_terms.dtype)
    mlp = taken_together(partial_sum.astype(jnp.bfloat16), TP).astype(jnp.float32)
    return (summed + mlp.reshape(row_count, step_count, features)).astype(jnp.bfloat16)


def solution(mesh):
    finer = Mesh(mesh.devices.reshape(mesh.shape["grp"], 2, 12), ("grp", "tp_0", "tp_1"))
    return jax.shard_map(
        shards,
        mesh=finer,
        in_specs=(
            P("grp", None, None),
            P("grp", TP, None),
            P("grp", TP, None),
            P("grp", None, None),
            P("grp", None, None),
            P("grp"),
            P("grp", None, None),
            P(),
            P("grp", TP),
            P("grp", TP),
        ),
        out_specs=P("grp", None, None),
        check_vma=False,
    )
```

profile of v0, /device:TPU:8, one launch (start us, length us, event | category | flops | bytes accessed | tf_op | source)
XLA Modules:
  0.0 183.1 jit_solution(9272845764433794585)
XLA Ops:
  0.0 1.0 reshape.1062
  1.0 1.2 reshape.1061
  2.2 0.7 broadcast_compare_fusion
  2.9 0.5 fusion.71
  3.4 0.2 fusion.38
  4.0 0.3 fusion.6
  4.3 6.5 %all-gather.2 = bf16[2,260,128]{2,1,0:T(8,128)(2,1)S(1)} all-gather(bf16[1,260,128]{2,1,0:T(8,128)(2,1)S(1)} %maximum_bitcast_fusion), channel_id=2, replica_groups=mesh['grp'=32,'tp_0'=2,'tp_1'=12] {'tp_0'}, dimensions={0}, use_global_device_ids=true | all-gather | bytes 199680 | tf_op jit(solution)/shard_map/all_gather | solution.py:23
  10.8 0.1 fusion.15
  11.0 37.0 %all-gather.3 = bf16[12,260,128]{2,1,0:T(8,128)(2,1)S(1)} all-gather(bf16[1,260,128]{2,1,0:T(8,128)(2,1)S(1)} %maximum_bitcast_fusion.1), channel_id=3, replica_groups=mesh['grp'=32,'tp_0'=2,'tp_1'=12] {'tp_1'}, dimensions={0}, use_global_device_ids=true | all-gather | bytes 865280 | tf_op jit(solution)/shard_map/all_gather | solution.py:23
  50.5 0.4 fusion.72
  51.1 0.2 fusion.49
  51.8 1.4 fusion.4
  53.3 0.2 multiply_reduce_fusion
  53.7 16.3 %all_to_all.53 = bf16[8,32,128]{2,0,1:T(8,128)(2,1)S(1)} all-to-all(bf16[8,32,128]{2,0,1:T(8,128)(2,1)S(1)} %copy.295), channel_id=1, replica_groups=mesh['grp'=32,'tp_0'=2,'tp_1'=12] {'grp'}, dimensions={1} | all-to-all | bytes 131072 | tf_op jit(solution)/shard_map/all_to_all | solution.py:153
  70.0 0.3 convolution_convert_fusion
  70.3 0.2 copy.296
  70.5 17.7 %all_to_all.54 = bf16[32,8,600]{2,1,0:T(8,128)(2,1)S(1)} all-to-all(bf16[32,8,600]{2,1,0:T(8,128)(2,1)S(1)} %bitcast.187), channel_id=1, replica_groups=mesh['grp'=32,'tp_0'=2,'tp_1'=12] {'grp'}, dimensions={0} | all-to-all | bytes 614400 | tf_op jit(solution)/shard_map/all_to_all | solution.py:60
  88.3 17.5 %all_to_all.55 = bf16[32,8,600]{2,1,0:T(8,128)(2,1)S(1)} all-to-all(bf16[32,8,600]{2,1,0:T(8,128)(2,1)S(1)} %broadcast_in_dim.51), channel_id=1, replica_groups=mesh['grp'=32,'tp_0'=2,'tp_1'=12] {'grp'}, dimensions={0} | all-to-all | bytes 614400 | tf_op jit(solution)/shard_map/all_to_all | solution.py:66
  105.8 0.2 fusion.5
  106.0 11.8 %all_to_all.56 = bf16[32,8,128]{2,1,0:T(8,128)(2,1)S(1)} all-to-all(bf16[32,8,128]{2,1,0:T(8,128)(2,1)S(1)} %fusion.5), channel_id=1, replica_groups=mesh['grp'=32,'tp_0'=2,'tp_1'=12] {'grp'}, dimensions={0} | all-to-all | bytes 131072 | tf_op jit(solution)/shard_map/all_to_all | solution.py:168
  117.8 0.2 broadcast_in_dim.88
  118.0 64.0 %all_to_all.57 = bf16[24,8,4096]{2,1,0:T(8,128)(2,1)S(1)} all-to-all(bf16[24,8,4096]{2,1,0:T(8,128)(2,1)S(1)} %broadcast_in_dim.88), channel_id=1, replica_groups=mesh['grp'=32,'tp_0'=2,'tp_1'=12] {'tp_0','tp_1'}, dimensions={0} | all-to-all | bytes 3145728 | tf_op jit(solution)/shard_map/all_to_all | solution.py:66
  182.0 0.2 convert_reduce_fusion
  182.4 0.7 add_convert_fusion
  (91 shorter events, 3.7 us)
Async XLA Ops:
  0.0 51.7 %copy-start = (bf16[4,2,512]{2,1,0:T(2,128)(2,1)S(1)}, bf16[4,2,512]{2,1,0:T(2,128)(2,1)}, u32[]{:S(2)}) copy-start(bf16[4,2,512]{2,1,0:T(2,128)(2,1)} %param.14) | copy-start | bytes 24580
  0.0 3.8 %copy-start.2 = (bf16[4,128,512]{2,1,0:T(8,128)(2,1)S(1)}, bf16[4,128,512]{2,1,0:T(8,128)(2,1)}, u32[]{:S(2)}) copy-start(bf16[4,128,512]{2,1,0:T(8,128)(2,1)} %param.12) | copy-start | bytes 1572868
  10.9 39.5 %copy-start.6 = (bf16[4,2,512]{2,1,0:T(2,128)(2,1)S(1)}, bf16[4,2,512]{2,1,0:T(2,128)(2,1)}, u32[]{:S(2)}) copy-start(bf16[4,2,512]{2,1,0:T(2,128)(2,1)} %param.13) | copy-start | bytes 24580
  51.7 1.5 copy-start.1
  51.8 1.7 copy-start.5
  53.1 16.9 %copy-start.3 = (f32[128,600]{0,1:T(8,128)S(1)}, f32[128,600]{0,1:T(8,128)}, u32[]{:S(2)}) copy-start(f32[128,600]{0,1:T(8,128)} %param.18) | copy-start | bytes 921604
  70.0 35.7 %copy-start.4 = (f32[128,600]{0,1:T(8,128)S(1)}, f32[128,600]{0,1:T(8,128)}, u32[]{:S(2)}) copy-start(f32[128,600]{0,1:T(8,128)} %param.19) | copy-start | bytes 921604
where the time goes:
time: 183 us
  blocking collectives  171 us (93%)
  local copies, waits for them, and re-layouts  5.75 us (3%)
  matrix products  3.06 us (2%)
  other arithmetic  2.89 us (2%)
    all_to_all x2, blocking collectives, copy_for_each(): return lax.all_to_all(copies, axis, split_axis=0, concat_axis=0, tiled=True)  81.5 us
    all_gather x2, blocking collectives, gathered_once(): both, at, found = (lax.all_gather(jnp.concatenate(lines), axis), 0, {})  43.4 us
    all_to_all x1, blocking collectives, summed_on_arrival(): lax.all_to_all(parts, axis, split_axis=0, concat_axis=0, tiled=True)  17.7 us
    all_to_all x1, blocking collectives, shards(): lax.all_to_all(flat, 'grp', split_axis=1, concat_axis=0, tiled=True)  16.3 us
    all_to_all x1, blocking collectives, shards(): lax.all_to_all(feature_terms.astype(jnp.bfloat16), 'grp', split_axis=0, c...  11.8 us

commit v1 on v0

v1 whole, which is shorter than its diff:
```python
import jax
import jax.numpy as jnp
from jax import lax
from jax.sharding import Mesh
from jax.sharding import PartitionSpec as P

HD = 128
KVH = 4
HQ = 32
GRP = ("xl", "y", "c")
TP = ("xh", "z")
WIDE = ("xl", "y", "c", "xh")
CHUNK = 20
NEAR = 24
masked_score = -1e30


def exchange(parts, axis):
    return lax.all_to_all(parts, axis, split_axis=0, concat_axis=0, tiled=True)


def copies(part, axis):
    return exchange(jnp.broadcast_to(part, (lax.axis_size(axis), *part.shape)), axis)


def two_words(value):
    high = value.astype(jnp.bfloat16)
    return high, (value - high.astype(jnp.float32)).astype(jnp.bfloat16)


def pad_to(array, axis, size):
    widths = [(0, 0)] * array.ndim
    widths[axis] = (0, size - array.shape[axis])
    return jnp.pad(array, widths)


def resharded(w_gate, w_down, groups, slices, per_slice):
    stacked = jnp.stack([w_gate.T, w_down.T]).astype(jnp.bfloat16)
    stacked = pad_to(stacked, 1, groups * CHUNK)
    parts = jnp.moveaxis(stacked.reshape(2, groups, CHUNK, HD), 0, 1)
    heads = exchange(parts, GRP)
    heads = pad_to(heads, 0, slices * per_slice)
    arrived = exchange(heads.reshape(slices, per_slice, 2, CHUNK, HD), "z")
    both = jnp.transpose(arrived, (2, 0, 3, 1, 4)).reshape(2, slices * CHUNK, per_slice * HD)
    return both[0], both[1]


def shards(
    queries,
    cache_keys,
    cache_values,
    new_keys,
    new_values,
    lengths,
    residual,
    norm_gain,
    w_gate,
    w_down,
):
    rows, steps, features = queries.shape
    positions = cache_keys.shape[1]
    groups, slices, halves = lax.axis_size(GRP), lax.axis_size("z"), lax.axis_size("xh")
    per_slice = -(-HQ // slices)
    slots = slices * per_slice
    wide = per_slice * HD
    tokens = rows * steps
    share = tokens // halves
    total_tokens = groups * tokens
    gate_weights, down_weights = resharded(w_gate, w_down, groups, slices, per_slice)

    per_group = HQ // KVH
    inv_root = HD ** (-0.5)
    here = lax.axis_index(TP)
    query_heads = queries.reshape(rows, steps, KVH, per_group, HD)
    key_heads = cache_keys.reshape(rows, positions, KVH, HD)
    value_heads = cache_values.reshape(rows, positions, KVH, HD)
    scores = jnp.einsum("rsjgd,rcjd->rsjgc", query_heads, key_heads, preferred_element_type=jnp.float32) * inv_root
    places = here * positions + lax.broadcasted_iota(jnp.int32, (rows, positions), 1)
    visible = (places < lengths[:, None])[:, None, None, None, :]
    scores = jnp.where(visible, scores, masked_score)
    fresh = jnp.einsum(
        "rsjgd,rtjd->rsjgt", query_heads, new_keys.reshape(rows, steps, KVH, HD), preferred_element_type=jnp.float32
    ) * inv_root
    causal = lax.broadcasted_iota(jnp.int32, (steps, steps), 0) >= lax.broadcasted_iota(jnp.int32, (steps, steps), 1)
    causal = (causal & (here == 0))[None, :, None, None, :]
    fresh = jnp.where(causal, fresh, masked_score)
    highest = jnp.maximum(jnp.max(scores, axis=-1), jnp.max(fresh, axis=-1))
    shift = highest.astype(jnp.bfloat16)
    shift_wide = lax.reduce_precision(highest, 8, 7)[..., None]
    weights = jnp.where(visible, jnp.exp(scores - shift_wide), 0.0)
    fresh_weights = jnp.where(causal, jnp.exp(fresh - shift_wide), 0.0)
    totals = jnp.sum(weights, axis=-1) + jnp.sum(fresh_weights, axis=-1)
    accum = jnp.einsum(
        "rsjgc,rcjd->rsjgd", weights.astype(jnp.bfloat16), value_heads, preferred_element_type=jnp.float32
    ) + jnp.einsum(
        "rsjgt,rtjd->rsjgd",
        fresh_weights.astype(jnp.bfloat16),
        new_values.reshape(rows, steps, KVH, HD),
        preferred_element_type=jnp.float32,
    )

    def by_target(array):
        array = pad_to(array.reshape(halves, share, HQ, -1), 2, slots)
        array = array.reshape(halves, share, slices, per_slice, -1)
        return jnp.transpose(array, (0, 2, 1, 3, 4)).reshape(halves * slices, share * per_slice, -1)

    high, low = two_words(totals)
    stats = by_target(jnp.stack([shift, high, low], axis=-1))
    stats = pad_to(pad_to(jnp.swapaxes(stats, 1, 2), 2, HD), 1, 4)
    sent = jnp.concatenate([by_target(accum.astype(jnp.bfloat16)), stats], axis=1)
    pieces = exchange(sent, TP)

    lines = share * per_slice
    stats = pieces[:, lines:, :lines].astype(jnp.float32)
    joint = jnp.max(stats[:, 0], axis=0)
    factor = jnp.exp(stats[:, 0] - joint)
    total = jnp.sum(factor * (stats[:, 1] + stats[:, 2]), axis=0)
    total = jnp.where(total > 0, total, 1.0)
    context = jnp.sum(factor[..., None] * pieces[:, :lines].astype(jnp.float32), axis=0) / total[:, None]

    half, at = lax.axis_index("xh"), lax.axis_index("z")
    mine = pad_to(residual.reshape(tokens, features), 1, slots * HD)
    mine = lax.dynamic_slice(mine, (half * share, at * wide), (share, wide))
    gain = lax.dynamic_slice(jnp.pad(norm_gain, (0, slots * HD - features), constant_values=1.0), (at * wide,), (wide,))
    summed = mine.astype(jnp.float32) + context.reshape(share, wide)
    gained = copies((summed * gain).astype(jnp.bfloat16), WIDE).reshape(total_tokens, wide)

    unscaled = gained.astype(jnp.float32) / gain
    squares = jnp.stack(two_words(jnp.sum(unscaled * unscaled, axis=-1)), axis=-1)
    gate = lax.dot_general(gained, gate_weights, (((1,), (1,)), ((), ())), preferred_element_type=jnp.float32)
    sent = jnp.concatenate([gate.astype(jnp.bfloat16), squares], axis=-1)
    sent = pad_to(sent, 0, slices * NEAR).reshape(slices, NEAR, -1)
    arrived = exchange(sent, "z").astype(jnp.float32).sum(axis=0)
    units = gate_weights.shape[0]
    mean_square = (arrived[:, units] + arrived[:, units + 1]) / features
    gate = arrived[:, :units] * lax.rsqrt(mean_square + 1e-05)[:, None]
    hidden = jax.nn.silu(gate).astype(jnp.bfloat16)
    hidden = copies(hidden, "z").reshape(slices * NEAR, units)[:total_tokens]
    terms = jnp.dot(hidden, down_weights, preferred_element_type=jnp.float32).astype(jnp.bfloat16)
    mlp = exchange(terms.reshape(groups * halves, share, wide), WIDE).astype(jnp.float32).sum(axis=0)
    mixed = copies((summed + mlp).astype(jnp.bfloat16), TP)
    mixed = jnp.swapaxes(mixed.reshape(halves, slices, share, wide), 1, 2)
    return mixed.reshape(rows, steps, slots * HD)[..., :features]


def solution(mesh):
    fine = Mesh(mesh.devices.reshape(2, 8, 2, 2, 12), ("xl", "y", "c", "xh", "z"))
    return jax.shard_map(
        shards,
        mesh=fine,
        in_specs=(
            P(GRP, None, None),
            P(GRP, TP, None),
            P(GRP, TP, None),
            P(GRP, None, None),
            P(GRP, None, None),
            P(GRP),
            P(GRP, None, None),
            P(),
            P(GRP, TP),
            P(GRP, TP),
        ),
        out_specs=P(GRP, None, None),
        check_vma=False,
    )
```

time: 183 us -> 168 us (0.918)
  blocking collectives: 171 us -> 47.1 us
  waiting for transfers between devices: 0 us -> 67.1 us
  starting transfers between devices: 0 us -> 37.9 us
  local copies, waits for them, and re-layouts: 5.75 us -> 11.3 us
    all_to_all x5 -> x3, blocking collectives: 127 us -> 47.1 us  [exchange(): return lax.all_to_all(parts, axis, split_axis=0, concat_axis=0, tiled=True)]
    all_to_all x0 -> x5, waiting for transfers between devices: none -> 67.1 us  [exchange(): return lax.all_to_all(parts, axis, split_axis=0, concat_axis=0, tiled=True)]
    all_gather x2 -> x0, blocking collectives: 43.4 us -> none  [gathered_once(): both, at, found = (lax.all_gather(jnp.concatenate(lines), axis), 0, {})]
    all_to_all x0 -> x5, starting transfers between devices: none -> 37.9 us  [exchange(): return lax.all_to_all(parts, axis, split_axis=0, concat_axis=0, tiled=True)]
    convert_element_type x30 -> x3, local copies, waits for them, and re-layouts: 2.72 us -> 0.11 us  [the longest x2 0.09 us: shards(): shift = highest.astype(jnp.bfloat16)]
    unnamed x14 -> x20, local copies, waits for them, and re-layouts: 0.04 us -> 2.06 us
    pad x0 -> x5, local copies, waits for them, and re-layouts: none -> 2.01 us  [pad_to(): return jnp.pad(array, widths)]
  transfers between devices with their start and end apart: 0 -> 5, of which waited for: 0 -> 5; matrix products, arithmetic and copies ran while one was open for 0% -> 2% of each run, Pallas kernels for 0% -> 0%
where the time goes in v1:
time: 168 us; the launch traced here: 167 us
  waiting for transfers between devices  67.1 us (40%)
  blocking collectives  47.1 us (28%)
  starting transfers between devices  37.9 us (23%)
  local copies, waits for them, and re-layouts  11.3 us (7%)
  matrix products  1.94 us (1%)
    all_to_all x5, waiting for transfers between devices, exchange(): return lax.all_to_all(parts, axis, split_axis=0, concat_axis=0, tiled=True)  67.1 us
    all_to_all x3, blocking collectives, exchange(): return lax.all_to_all(parts, axis, split_axis=0, concat_axis=0, tiled=True)  47.1 us
    all_to_all x5, starting transfers between devices, exchange(): return lax.all_to_all(parts, axis, split_axis=0, concat_axis=0, tiled=True)  37.9 us
  transfers between devices with their start and end apart: 5, of which 5 were waited for; matrix products, arithmetic and copies ran while one was open for 2% of the time, Pallas kernels for 0%

profile of v1, /device:TPU:8, one launch (start us, length us, event | category | flops | bytes accessed | tf_op | source)
XLA Modules:
  0.0 167.2 jit_solution(235606570160495786)
XLA Ops:
  0.0 0.9 reshape.234
  0.9 1.2 reshape.233
  2.1 0.6 copy-done.7
  6.2 0.7 copy.169
  6.8 17.8 %all-to-all-start = ((bf16[24,16,128]{2,1,0:T(8,128)(2,1)}), bf16[24,16,128]{2,1,0:T(8,128)(2,1)S(1)}, u32[]{:S(2)}, u32[]{:S(2)}) async-start(bf16[24,16,128]{2,1,0:T(8,128)(2,1)} %copy.169), calls=%async_computation | async-start | bytes 196608 | tf_op jit(solution)/shard_map/all_to_all | solution.py:19
  24.8 0.8 copy-done.4
  25.9 1.0 pad.42.clone
  26.9 11.1 %all-to-all-done = bf16[24,16,128]{2,1,0:T(8,128)(2,1)S(1)} async-done(((bf16[24,16,128]{2,1,0:T(8,128)(2,1)}), bf16[24,16,128]{2,1,0:T(8,128)(2,1)S(1)}, u32[]{:S(2)}, u32[]{:S(2)}) %all-to-all-start) | async-done | bytes 98336 | tf_op jit(solution)/shard_map/all_to_all | solution.py:19
  38.0 7.7 %all-to-all-start.2 = ((bf16[32,2,20,128]{3,1,2,0:T(2,128)(2,1)}), bf16[32,2,20,128]{3,1,2,0:T(2,128)(2,1)S(1)}, u32[]{:S(2)}, u32[]{:S(2)}) async-start(bf16[32,2,20,128]{3,1,2,0:T(2,128)(2,1)} %bitcast.24), calls=%async_computation.2 | async-start | bytes 655360 | tf_op jit(solution)/shard_map/all_to_all | solution.py:19
  46.2 13.0 %all-to-all-done.2 = bf16[32,2,20,128]{3,1,2,0:T(2,128)(2,1)S(1)} async-done(((bf16[32,2,20,128]{3,1,2,0:T(2,128)(2,1)}), bf16[32,2,20,128]{3,1,2,0:T(2,128)(2,1)S(1)}, u32[]{:S(2)}, u32[]{:S(2)}) %all-to-all-start.2) | async-done | bytes 327712 | tf_op jit(solution)/shard_map/all_to_all | solution.py:19
  59.2 0.7 broadcast_in_dim.69
  60.0 5.3 %all-to-all-start.1 = ((bf16[64,4,384]{2,1,0:T(4,128)(2,1)}), bf16[64,4,384]{2,1,0:T(4,128)(2,1)S(1)}, u32[]{:S(2)}, u32[]{:S(2)}) async-start(bf16[64,4,384]{2,1,0:T(4,128)(2,1)} %broadcast_in_dim.69), calls=%async_computation.1 | async-start | bytes 393216 | tf_op jit(solution)/shard_map/all_to_all | solution.py:19
  65.2 1.0 pad.43
  66.2 10.7 %all-to-all-done.1 = bf16[64,4,384]{2,1,0:T(4,128)(2,1)S(1)} async-done(((bf16[64,4,384]{2,1,0:T(4,128)(2,1)}), bf16[64,4,384]{2,1,0:T(4,128)(2,1)S(1)}, u32[]{:S(2)}, u32[]{:S(2)}) %all-to-all-start.1) | async-done | bytes 196640 | tf_op jit(solution)/shard_map/all_to_all | solution.py:19
  77.0 3.6 %all-to-all-start.3 = ((bf16[12,3,2,20,128]{4,2,3,1,0:T(2,128)(2,1)}), bf16[12,3,2,20,128]{4,2,3,1,0:T(2,128)(2,1)S(1)}, u32[]{:S(2)}, u32[]{:S(2)}) async-start(bf16[12,3,2,20,128]{4,2,3,1,0:T(2,128)(2,1)} %bitcast.25), calls=%async_computation.3 | async-start | bytes 737280 | tf_op jit(solution)/shard_map/all_to_all | solution.py:19
  80.9 20.1 %all-to-all-done.3 = bf16[12,3,2,20,128]{4,2,3,1,0:T(2,128)(2,1)S(1)} async-done(((bf16[12,3,2,20,128]{4,2,3,1,0:T(2,128)(2,1)}), bf16[12,3,2,20,128]{4,2,3,1,0:T(2,128)(2,1)S(1)}, u32[]{:S(2)}, u32[]{:S(2)}) %all-to-all-start.3) | async-done | bytes 368672 | tf_op jit(solution)/shard_map/all_to_all | solution.py:19
  101.1 0.5 fusion.36
  102.1 14.5 %all_to_all.40 = bf16[12,24,242]{2,1,0:T(8,128)(2,1)S(1)} all-to-all(bf16[12,24,242]{2,1,0:T(8,128)(2,1)S(1)} %bitcast.82), channel_id=1, replica_groups=mesh['xl'=2,'y'=8,'c'=2,'xh'=2,'z'=12] {'z'}, dimensions={0} | all-to-all | bytes 278784 | tf_op jit(solution)/shard_map/all_to_all | solution.py:19
  117.0 0.7 broadcast_in_dim.70
  117.6 3.5 %all-to-all-start.5 = ((bf16[12,24,240]{2,1,0:T(8,128)(2,1)}), bf16[12,24,240]{2,1,0:T(8,128)(2,1)S(1)}, u32[]{:S(2)}, u32[]{:S(2)}) async-start(bf16[12,24,240]{2,1,0:T(8,128)(2,1)} %broadcast_in_dim.70), calls=%async_computation.5 | async-start | bytes 294912 | tf_op jit(solution)/shard_map/all_to_all | solution.py:19
  121.3 12.2 %all-to-all-done.5 = bf16[12,24,240]{2,1,0:T(8,128)(2,1)S(1)} async-done(((bf16[12,24,240]{2,1,0:T(8,128)(2,1)}), bf16[12,24,240]{2,1,0:T(8,128)(2,1)S(1)}, u32[]{:S(2)}, u32[]{:S(2)}) %all-to-all-start.5) | async-done | bytes 138272 | tf_op jit(solution)/shard_map/all_to_all | solution.py:19
  133.8 16.5 %all_to_all.41 = bf16[64,4,384]{2,1,0:T(4,128)(2,1)S(1)} all-to-all(bf16[64,4,384]{2,1,0:T(4,128)(2,1)S(1)} %reshape.248), channel_id=1, replica_groups=mesh['xl'=2,'y'=8,'c'=2,'xh'=2,'z'=12] {'xl','y','c','xh'}, dimensions={0} | all-to-all | bytes 393216 | tf_op jit(solution)/shard_map/all_to_all | solution.py:19
  150.5 16.0 %all_to_all.42 = bf16[24,4,384]{2,1,0:T(4,128)(2,1)S(1)} all-to-all(bf16[24,4,384]{2,1,0:T(4,128)(2,1)S(1)} %broadcast_in_dim.71), channel_id=1, replica_groups=mesh['xl'=2,'y'=8,'c'=2,'xh'=2,'z'=12] {'xh','z'}, dimensions={0} | all-to-all | bytes 147456 | tf_op jit(solution)/shard_map/all_to_all | solution.py:19
  166.6 0.7 slice.62
  (81 shorter events, 6.0 us)
Async XLA Ops:
  0.0 5.2 %copy-start = (bf16[4,2,512]{2,1,0:T(2,128)(2,1)S(1)}, bf16[4,2,512]{2,1,0:T(2,128)(2,1)}, u32[]{:S(2)}) copy-start(bf16[4,2,512]{2,1,0:T(2,128)(2,1)} %param.14) | copy-start | bytes 24580
  2.1 0.7 copy-start.7
  2.8 0.7 copy-start.6
  4.0 1.6 copy-start.1
  6.1 18.6 %copy-start.3 = (f32[128,600]{0,1:T(8,128)S(1)}, f32[128,600]{0,1:T(8,128)}, u32[]{:S(2)}) copy-start(f32[128,600]{0,1:T(8,128)} %param.18) | copy-start | bytes 921604
  6.2 18.5 %copy-start.2 = (f32[128,600]{0,1:T(8,128)S(1)}, f32[128,600]{0,1:T(8,128)}, u32[]{:S(2)}) copy-start(f32[128,600]{0,1:T(8,128)} %param.19) | copy-start | bytes 921604
  6.8 31.1 %all-to-all-start = ((bf16[24,16,128]{2,1,0:T(8,128)(2,1)}), bf16[24,16,128]{2,1,0:T(8,128)(2,1)S(1)}, u32[]{:S(2)}, u32[]{:S(2)}) async-start(bf16[24,16,128]{2,1,0:T(8,128)(2,1)} %copy.169), calls=%async_computation | async-start | bytes 196608 | tf_op jit(solution)/shard_map/all_to_all | solution.py:19
  24.7 0.8 copy-start.4
  25.9 1.0 copy-start.5
  38.0 21.3 %all-to-all-start.2 = ((bf16[32,2,20,128]{3,1,2,0:T(2,128)(2,1)}), bf16[32,2,20,128]{3,1,2,0:T(2,128)(2,1)S(1)}, u32[]{:S(2)}, u32[]{:S(2)}) async-start(bf16[32,2,20,128]{3,1,2,0:T(2,128)(2,1)} %bitcast.24), calls=%async_computation.2 | async-start | bytes 655360 | tf_op jit(solution)/shard_map/all_to_all | solution.py:19
  60.0 17.0 %all-to-all-start.1 = ((bf16[64,4,384]{2,1,0:T(4,128)(2,1)}), bf16[64,4,384]{2,1,0:T(4,128)(2,1)S(1)}, u32[]{:S(2)}, u32[]{:S(2)}) async-start(bf16[64,4,384]{2,1,0:T(4,128)(2,1)} %broadcast_in_dim.69), calls=%async_computation.1 | async-start | bytes 393216 | tf_op jit(solution)/shard_map/all_to_all | solution.py:19
  77.0 24.1 %all-to-all-start.3 = ((bf16[12,3,2,20,128]{4,2,3,1,0:T(2,128)(2,1)}), bf16[12,3,2,20,128]{4,2,3,1,0:T(2,128)(2,1)S(1)}, u32[]{:S(2)}, u32[]{:S(2)}) async-start(bf16[12,3,2,20,128]{4,2,3,1,0:T(2,128)(2,1)} %bitcast.25), calls=%async_computation.3 | async-start | bytes 737280 | tf_op jit(solution)/shard_map/all_to_all | solution.py:19
  117.6 15.8 %all-to-all-start.5 = ((bf16[12,24,240]{2,1,0:T(8,128)(2,1)}), bf16[12,24,240]{2,1,0:T(8,128)(2,1)S(1)}, u32[]{:S(2)}, u32[]{:S(2)}) async-start(bf16[12,24,240]{2,1,0:T(8,128)(2,1)} %broadcast_in_dim.70), calls=%async_computation.5 | async-start | bytes 294912 | tf_op jit(solution)/shard_map/all_to_all | solution.py:19

commit v2 on v1

v2 whole, which is shorter than its diff:
```python
import jax
import jax.numpy as jnp
from jax import lax
from jax.sharding import Mesh
from jax.sharding import PartitionSpec as P

HD = 128
KVH = 4
HQ = 32
GRP = ("xl", "ya", "yb", "c")
TP = ("xh", "z2", "z1")
WIDE = ("xl", "ya", "yb", "c", "xh")
DEEP = ("xl", "c", "z1")
HALF = 304
masked_score = -1e30


def exchange(parts, axis):
    return lax.all_to_all(parts, axis, split_axis=0, concat_axis=0, tiled=True)


def copies(part, axis):
    return exchange(jnp.broadcast_to(part, (lax.axis_size(axis), *part.shape)), axis)


def two_words(value):
    high = value.astype(jnp.bfloat16)
    return high, (value - high.astype(jnp.float32)).astype(jnp.bfloat16)


def pad_to(array, axis, size):
    widths = [(0, 0)] * array.ndim
    widths[axis] = (0, size - array.shape[axis])
    return jnp.pad(array, widths)


def traded(halves, other):
    near = lax.axis_size("ya")
    moves = []
    for row in range(near):
        for pair in range(2):
            for deep in range(near):
                target = (deep * 2 + (pair ^ other)) * near + row
                moves.append(((row * 2 + pair) * near + deep, target))
    at = lax.axis_index("yb") ^ other
    return lax.ppermute(lax.dynamic_index_in_dim(halves, at, 1, False), ("ya", "yb", "z1"), moves)


def shards(
    queries,
    cache_keys,
    cache_values,
    new_keys,
    new_values,
    lengths,
    residual,
    norm_gain,
    w_gate,
    w_down,
):
    rows, steps, features = queries.shape
    positions = cache_keys.shape[1]
    groups, halves = lax.axis_size(GRP), lax.axis_size("xh")
    tokens = rows * steps
    share = tokens // halves
    total_tokens = groups * tokens
    near = lax.axis_size("z1")
    far = lax.axis_size("z2")

    stacked = jnp.stack([w_gate.T, w_down.T]).astype(jnp.bfloat16)
    stacked = pad_to(stacked, 1, 2 * HALF).reshape(2, 2, HALF, HD)
    own, other = traded(stacked, 0), traded(stacked, 1)

    per_group = HQ // KVH
    inv_root = HD ** (-0.5)
    here = lax.axis_index(TP)
    query_heads = queries.reshape(rows, steps, KVH, per_group, HD)
    key_heads = cache_keys.reshape(rows, positions, KVH, HD)
    value_heads = cache_values.reshape(rows, positions, KVH, HD)
    scores = jnp.einsum("rsjgd,rcjd->rsjgc", query_heads, key_heads, preferred_element_type=jnp.float32) * inv_root
    places = here * positions + lax.broadcasted_iota(jnp.int32, (rows, positions), 1)
    visible = (places < lengths[:, None])[:, None, None, None, :]
    scores = jnp.where(visible, scores, masked_score)
    fresh = jnp.einsum(
        "rsjgd,rtjd->rsjgt", query_heads, new_keys.reshape(rows, steps, KVH, HD), preferred_element_type=jnp.float32
    ) * inv_root
    causal = lax.broadcasted_iota(jnp.int32, (steps, steps), 0) >= lax.broadcasted_iota(jnp.int32, (steps, steps), 1)
    causal = (causal & (here == 0))[None, :, None, None, :]
    fresh = jnp.where(causal, fresh, masked_score)
    highest = jnp.maximum(jnp.max(scores, axis=-1), jnp.max(fresh, axis=-1))
    shift = highest.astype(jnp.bfloat16)
    shift_wide = lax.reduce_precision(highest, 8, 7)[..., None]
    weights = jnp.where(visible, jnp.exp(scores - shift_wide), 0.0)
    fresh_weights = jnp.where(causal, jnp.exp(fresh - shift_wide), 0.0)
    totals = jnp.sum(weights, axis=-1) + jnp.sum(fresh_weights, axis=-1)
    accum = jnp.einsum(
        "rsjgc,rcjd->rsjgd", weights.astype(jnp.bfloat16), value_heads, preferred_element_type=jnp.float32
    ) + jnp.einsum(
        "rsjgt,rtjd->rsjgd",
        fresh_weights.astype(jnp.bfloat16),
        new_values.reshape(rows, steps, KVH, HD),
        preferred_element_type=jnp.float32,
    )

    lines = share * 2 * 4

    def by_target(array):
        array = array.reshape(halves, share, 2, near, 4, -1)
        return jnp.transpose(array, (0, 3, 1, 2, 4, 5)).reshape(halves, near, lines, -1)

    high, low = two_words(totals)
    stats = by_target(jnp.stack([shift, high, low], axis=-1))
    stats = pad_to(jnp.swapaxes(stats, 2, 3).reshape(halves, near, 1, 3 * lines), 3, HD)
    sent = jnp.concatenate([by_target(accum.astype(jnp.bfloat16)), stats], axis=2)
    sent = jnp.broadcast_to(sent[:, None], (halves, far, near, lines + 1, HD))
    pieces = exchange(sent.reshape(halves * far * near, lines + 1, HD), TP)

    stats = pieces[:, lines, : 3 * lines].astype(jnp.float32).reshape(-1, 3, lines)
    joint = jnp.max(stats[:, 0], axis=0)
    factor = jnp.exp(stats[:, 0] - joint)
    total = jnp.sum(factor * (stats[:, 1] + stats[:, 2]), axis=0)
    context = jnp.sum(factor[..., None] * pieces[:, :lines].astype(jnp.float32), axis=0) / total[:, None]

    half, deep = lax.axis_index("xh"), lax.axis_index("z1")
    mine = residual.reshape(halves, share, 2, near, 4, HD)
    mine = lax.dynamic_index_in_dim(lax.dynamic_index_in_dim(mine, half, 0, False), deep, 2, False)
    gain = lax.dynamic_index_in_dim(norm_gain.reshape(2, near, 4, HD), deep, 1, False)
    summed = mine.astype(jnp.float32) + context.reshape(share, 2, 4, HD)
    gained = (summed * gain).astype(jnp.bfloat16).reshape(share, 2, 2, 2, HD)
    gained = jnp.transpose(gained, (1, 3, 0, 2, 4))
    ordered = jnp.stack([gained, gained[:, :, :, ::-1]], axis=1)
    ordered = jnp.broadcast_to(ordered[:, None, :, :, None], (2, near, 2, 2, halves, share, 2, HD))
    arrived = exchange(ordered.reshape(groups * halves, share, 2 * HD), WIDE).reshape(total_tokens, 2 * HD)

    pair = lax.axis_index("yb")
    gain = gain.reshape(2, 2, 2, HD)[lax.axis_index("xl"), :, lax.axis_index("c")]
    gain = jnp.where(pair == 0, gain, gain[::-1]).reshape(2 * HD)
    unscaled = arrived.astype(jnp.float32) / gain
    squares = jnp.stack(two_words(jnp.sum(unscaled * unscaled, axis=-1)), axis=-1)
    turned = (((1,), (1,)), ((), ()))
    gate = lax.dot_general(arrived[:, :HD], own[0], turned, preferred_element_type=jnp.float32)
    gate = gate + lax.dot_general(arrived[:, HD:], other[0], turned, preferred_element_type=jnp.float32)
    sent = jnp.concatenate([gate.astype(jnp.bfloat16), squares], axis=-1)
    depth = lax.axis_size(DEEP)
    sums = exchange(sent.reshape(depth, total_tokens // depth, -1), DEEP).astype(jnp.float32).sum(axis=0)
    mean_square = (sums[:, HALF] + sums[:, HALF + 1]) / features
    gate = sums[:, :HALF] * lax.rsqrt(mean_square + 1e-05)[:, None]
    hidden = copies(jax.nn.silu(gate).astype(jnp.bfloat16), DEEP).reshape(total_tokens, HALF)
    terms = jnp.concatenate(
        [jnp.dot(hidden, w[1], preferred_element_type=jnp.float32).astype(jnp.bfloat16) for w in (own, other)], axis=-1
    )
    partial = exchange(terms.reshape(groups * halves, share, 2 * HD), WIDE)
    partial = partial.reshape(2, near, 2, 2, halves, share, 2, HD).astype(jnp.float32).sum(axis=(1, 4))
    mlp = partial[:, 0] + partial[:, 1, :, :, ::-1]
    mlp = jnp.transpose(mlp, (2, 0, 3, 1, 4)).reshape(share, 2, 4, HD)
    mixed = mlp + jnp.where(lax.axis_index("z2") == 0, summed, 0.0)
    mixed = copies(mixed.astype(jnp.bfloat16).reshape(share, 8 * HD), TP)
    mixed = mixed.reshape(halves, far, near, share, 2, 4, HD).astype(jnp.float32).sum(axis=1)
    mixed = jnp.transpose(mixed, (0, 2, 3, 1, 4, 5))
    return mixed.astype(jnp.bfloat16).reshape(rows, steps, features)


def solution(mesh):
    fine = Mesh(mesh.devices.reshape(2, 4, 2, 2, 2, 3, 4), ("xl", "ya", "yb", "c", "xh", "z2", "z1"))
    return jax.shard_map(
        shards,
        mesh=fine,
        in_specs=(
            P(GRP, None, None),
            P(GRP, TP, None),
            P(GRP, TP, None),
            P(GRP, None, None),
            P(GRP, None, None),
            P(GRP),
            P(GRP, None, None),
            P(),
            P(GRP, TP),
            P(GRP, TP),
        ),
        out_specs=P(GRP, None, None),
        check_vma=False,
    )
```

time: 168 us -> 135 us (0.80)
  waiting for transfers between devices: 67.1 us -> 34.4 us
  local copies, waits for them, and re-layouts: 11.3 us -> 8.77 us
    all_to_all x5 -> x3, waiting for transfers between devices: 67.1 us -> 34.4 us  [exchange(): return lax.all_to_all(parts, axis, split_axis=0, concat_axis=0, tiled=True)]
    ppermute x0 -> x2, starting transfers between devices: none -> 3.03 us  [traded(): lax.ppermute(lax.dynamic_index_in_dim(halves, at, 1, False), ('ya', 'yb',...]
    all_to_all x5 -> x3, starting transfers between devices: 37.9 us -> 35.8 us  [exchange(): return lax.all_to_all(parts, axis, split_axis=0, concat_axis=0, tiled=True)]
    pad x5 -> x0, local copies, waits for them, and re-layouts: 2.01 us -> none  [pad_to(): return jnp.pad(array, widths)]
    reshape x8 -> x7, local copies, waits for them, and re-layouts: 0.52 us -> 2.34 us  [the longest x1 0.73 us: shards(): ordered.reshape(groups * halves, share, 2 * HD)]
  transfers between devices with their start and end apart: 5 -> 5, of which waited for: 5 -> 3; matrix products, arithmetic and copies ran while one was open for 2% -> 2% of each run, Pallas kernels for 0% -> 0%
where the time goes in v2:
time: 135 us
  blocking collectives  47.9 us (35%)
  starting transfers between devices  38.9 us (29%)
  waiting for transfers between devices  34.4 us (25%)
  local copies, waits for them, and re-layouts  8.77 us (6%)
  matrix products  2.32 us (2%)
  other arithmetic  1.92 us (1%)
    all_to_all x3, blocking collectives, exchange(): return lax.all_to_all(parts, axis, split_axis=0, concat_axis=0, tiled=True)  47.9 us
    all_to_all x3, starting transfers between devices, exchange(): return lax.all_to_all(parts, axis, split_axis=0, concat_axis=0, tiled=True)  35.8 us
    all_to_all x3, waiting for transfers between devices, exchange(): return lax.all_to_all(parts, axis, split_axis=0, concat_axis=0, tiled=True)  34.4 us
    ppermute x2, starting transfers between devices, traded(): lax.ppermute(lax.dynamic_index_in_dim(halves, at, 1, False), ('ya', 'yb',...  3.03 us
  transfers between devices with their start and end apart: 5, of which 3 were waited for; matrix products, arithmetic and copies ran while one was open for 2% of the time, Pallas kernels for 0%

profile of v2, /device:TPU:8, one launch (start us, length us, event | category | flops | bytes accessed | tf_op | source)
XLA Modules:
  0.0 134.8 jit_solution(5919645285271176033)
XLA Ops:
  0.0 0.9 reshape.270
  0.9 1.2 reshape.269
  2.1 0.6 copy-done.7
  2.9 0.5 fusion.39
  3.6 0.4 fusion.40
  4.9 0.6 copy-done.5
  5.5 0.3 fusion.26
  6.0 0.3 fusion.4
  6.3 0.7 broadcast_in_dim.76
  7.1 18.0 %all-to-all-start = ((bf16[24,33,128]{2,1,0:T(8,128)(2,1)}), bf16[24,33,128]{2,1,0:T(8,128)(2,1)S(1)}, u32[]{:S(2)}, u32[]{:S(2)}) async-start(bf16[24,33,128]{2,1,0:T(8,128)(2,1)} %bitcast.17), calls=%async_computation | async-start | bytes 491520 | tf_op jit(solution)/shard_map/all_to_all | solution.py:19
  25.2 2.4 %collective-permute-start.1 = (bf16[2,304,128]{2,1,0:T(8,128)(2,1)S(1)}, bf16[2,304,128]{2,1,0:T(8,128)(2,1)S(1)}, u32[]{:S(2)}, u32[]{:S(2)}) collective-permute-start(bf16[2,304,128]{2,1,0:T(8,128)(2,1)S(1)} %get-tuple-element.12), channel_id=1, source_target_pairs={{0,48},{1,144},{2,240},{3,336},{48,0},{49,96},{50,192},{51,288},{9... | collective-permute-start | bytes 466952 | tf_op jit(solution)/shard_map/ppermute | solution.py:46
  27.6 0.7 collective-permute-start
  28.4 14.1 %all-to-all-done = bf16[24,33,128]{2,1,0:T(8,128)(2,1)S(1)} async-done(((bf16[24,33,128]{2,1,0:T(8,128)(2,1)}), bf16[24,33,128]{2,1,0:T(8,128)(2,1)S(1)}, u32[]{:S(2)}, u32[]{:S(2)}) %all-to-all-start) | async-done | bytes 202784 | tf_op jit(solution)/shard_map/all_to_all | solution.py:19
  43.3 0.7 reshape.280
  44.0 9.4 %all-to-all-start.1 = ((bf16[64,4,256]{2,1,0:T(4,128)(2,1)}), bf16[64,4,256]{2,1,0:T(4,128)(2,1)S(1)}, u32[]{:S(2)}, u32[]{:S(2)}) async-start(bf16[64,4,256]{2,1,0:T(4,128)(2,1)} %reshape.280), calls=%async_computation.1 | async-start | bytes 262144 | tf_op jit(solution)/shard_map/all_to_all | solution.py:19
  53.4 10.2 %all-to-all-done.1 = bf16[64,4,256]{2,1,0:T(4,128)(2,1)S(1)} async-done(((bf16[64,4,256]{2,1,0:T(4,128)(2,1)}), bf16[64,4,256]{2,1,0:T(4,128)(2,1)S(1)}, u32[]{:S(2)}, u32[]{:S(2)}) %all-to-all-start.1) | async-done | bytes 131104 | tf_op jit(solution)/shard_map/all_to_all | solution.py:19
  65.1 12.7 %all_to_all.30 = bf16[16,16,306]{2,1,0:T(8,128)(2,1)S(1)} all-to-all(bf16[16,16,306]{2,1,0:T(8,128)(2,1)S(1)} %pad_maximum_fusion), channel_id=1, replica_groups=mesh['xl'=2,'ya'=4,'yb'=2,'c'=2,'xh'=2,'z2'=3,'z1'=4] {'xl','c','z1'}, dimensions={0} | all-to-all | bytes 313344 | tf_op jit(solution)/shard_map/all_to_all | solution.py:19
  78.2 11.8 %all_to_all.31 = bf16[16,16,304]{2,1,0:T(8,128)(2,1)S(1)} all-to-all(bf16[16,16,304]{2,1,0:T(8,128)(2,1)S(1)} %broadcast_in_dim.78), channel_id=1, replica_groups=mesh['xl'=2,'ya'=4,'yb'=2,'c'=2,'xh'=2,'z2'=3,'z1'=4] {'xl','c','z1'}, dimensions={0} | all-to-all | bytes 311296 | tf_op jit(solution)/shard_map/all_to_all | solution.py:19
  90.2 0.2 convolution_convert_fusion.1
  90.5 0.7 reshape.284
  91.2 8.5 %all-to-all-start.4 = ((bf16[64,4,256]{2,1,0:T(4,128)(2,1)}), bf16[64,4,256]{2,1,0:T(4,128)(2,1)S(1)}, u32[]{:S(2)}, u32[]{:S(2)}) async-start(bf16[64,4,256]{2,1,0:T(4,128)(2,1)} %reshape.284), calls=%async_computation.4 | async-start | bytes 262144 | tf_op jit(solution)/shard_map/all_to_all | solution.py:19
  99.9 10.1 %all-to-all-done.4 = bf16[64,4,256]{2,1,0:T(4,128)(2,1)S(1)} async-done(((bf16[64,4,256]{2,1,0:T(4,128)(2,1)}), bf16[64,4,256]{2,1,0:T(4,128)(2,1)S(1)}, u32[]{:S(2)}, u32[]{:S(2)}) %all-to-all-start.4) | async-done | bytes 131104 | tf_op jit(solution)/shard_map/all_to_all | solution.py:19
  110.4 23.5 %all_to_all.32 = bf16[24,4,1024]{2,1,0:T(4,128)(2,1)S(1)} all-to-all(bf16[24,4,1024]{2,1,0:T(4,128)(2,1)S(1)} %broadcast_in_dim.80), channel_id=1, replica_groups=mesh['xl'=2,'ya'=4,'yb'=2,'c'=2,'xh'=2,'z2'=3,'z1'=4] {'xh','z2','z1'}, dimensions={0} | all-to-all | bytes 393216 | tf_op jit(solution)/shard_map/all_to_all | solution.py:19
  134.1 0.6 reshape.286
  (94 shorter events, 5.2 us)
Async XLA Ops:
  0.0 28.3 %copy-start = (f32[4096]{0:T(1024)S(1)}, f32[4096]{0:T(1024)}, u32[]{:S(2)}) copy-start(f32[4096]{0:T(1024)} %param.17) | copy-start | bytes 49156
  2.1 0.7 copy-start.7
  2.9 0.7 copy-start.6
  4.0 1.8 %copy-start.1 = (bf16[4,128,512]{2,1,0:T(8,128)(2,1)S(1)}, bf16[4,128,512]{2,1,0:T(8,128)(2,1)}, u32[]{:S(2)}) copy-start(bf16[4,128,512]{2,1,0:T(8,128)(2,1)} %param.12) | copy-start | bytes 1572868
  4.8 0.7 copy-start.5
  6.3 18.7 %copy-start.3 = (f32[128,600]{0,1:T(8,128)S(1)}, f32[128,600]{0,1:T(8,128)}, u32[]{:S(2)}) copy-start(f32[128,600]{0,1:T(8,128)} %param.18) | copy-start | bytes 921604
  7.1 18.0 %copy-start.2 = (f32[128,600]{0,1:T(8,128)S(1)}, f32[128,600]{0,1:T(8,128)}, u32[]{:S(2)}) copy-start(f32[128,600]{0,1:T(8,128)} %param.19) | copy-start | bytes 921604
  7.1 35.4 %all-to-all-start = ((bf16[24,33,128]{2,1,0:T(8,128)(2,1)}), bf16[24,33,128]{2,1,0:T(8,128)(2,1)S(1)}, u32[]{:S(2)}, u32[]{:S(2)}) async-start(bf16[24,33,128]{2,1,0:T(8,128)(2,1)} %bitcast.17), calls=%async_computation | async-start | bytes 491520 | tf_op jit(solution)/shard_map/all_to_all | solution.py:19
  25.1 3.1 %copy-start.4 = (bf16[4,2,4096]{2,1,0:T(2,128)(2,1)S(1)}, bf16[4,2,4096]{2,1,0:T(2,128)(2,1)}, u32[]{:S(2)}) copy-start(bf16[4,2,4096]{2,1,0:T(2,128)(2,1)} %param.16) | copy-start | bytes 196612
  25.2 39.2 %collective-permute-start.1 = (bf16[2,304,128]{2,1,0:T(8,128)(2,1)S(1)}, bf16[2,304,128]{2,1,0:T(8,128)(2,1)S(1)}, u32[]{:S(2)}, u32[]{:S(2)}) collective-permute-start(bf16[2,304,128]{2,1,0:T(8,128)(2,1)S(1)} %get-tuple-element.12), channel_id=1, source_target_pairs={{0,48},{1,144},{2,240},{3,336},{48,0},{49,96},{50,192},{51,288},{9... | collective-permute-start | bytes 466952 | tf_op jit(solution)/shard_map/ppermute | solution.py:46
  27.6 37.1 %collective-permute-start = (bf16[2,304,128]{2,1,0:T(8,128)(2,1)S(1)}, bf16[2,304,128]{2,1,0:T(8,128)(2,1)S(1)}, u32[]{:S(2)}, u32[]{:S(2)}) collective-permute-start(bf16[2,304,128]{2,1,0:T(8,128)(2,1)S(1)} %get-tuple-element.11), channel_id=1, source_target_pairs={{0,0},{1,96},{2,192},{3,288},{48,48},{49,144},{50,240},{51,336},{9... | collective-permute-start | bytes 466952 | tf_op jit(solution)/shard_map/ppermute | solution.py:46
  44.0 19.7 %all-to-all-start.1 = ((bf16[64,4,256]{2,1,0:T(4,128)(2,1)}), bf16[64,4,256]{2,1,0:T(4,128)(2,1)S(1)}, u32[]{:S(2)}, u32[]{:S(2)}) async-start(bf16[64,4,256]{2,1,0:T(4,128)(2,1)} %reshape.280), calls=%async_computation.1 | async-start | bytes 262144 | tf_op jit(solution)/shard_map/all_to_all | solution.py:19
  91.2 18.8 %all-to-all-start.4 = ((bf16[64,4,256]{2,1,0:T(4,128)(2,1)}), bf16[64,4,256]{2,1,0:T(4,128)(2,1)S(1)}, u32[]{:S(2)}, u32[]{:S(2)}) async-start(bf16[64,4,256]{2,1,0:T(4,128)(2,1)} %reshape.284), calls=%async_computation.4 | async-start | bytes 262144 | tf_op jit(solution)/shard_map/all_to_all | solution.py:19

commit v3 on v1

v3 whole, which is shorter than its diff:
```python
import jax
import jax.numpy as jnp
from jax import lax
from jax.experimental import pallas as pl
from jax.experimental.pallas import tpu as pltpu
from jax.sharding import Mesh
from jax.sharding import PartitionSpec as P


HD = 128
KVH = 4
HQ = 32
EACH = HQ // KVH
PER = 3
GRP = ("xl", "y", "c")
TP = ("xh", "z")
WIDE = ("xl", "y", "c", "xh")
HALF = 304
NEAR = 24
masked_score = -1e30
ANY = pl.BlockSpec(memory_space=pl.ANY)


def exchange(parts, axis):
    return lax.all_to_all(parts, axis, split_axis=0, concat_axis=0, tiled=True)


def copies(part, axis):
    return exchange(jnp.broadcast_to(part, (lax.axis_size(axis), *part.shape)), axis)


def two_words(value):
    high = value.astype(jnp.bfloat16)
    return high, (value - high.astype(jnp.float32)).astype(jnp.bfloat16)


def pad_to(array, axis, size, fill=0):
    widths = [(0, 0)] * array.ndim
    widths[axis] = (0, size - array.shape[axis])
    return jnp.pad(array, widths, constant_values=fill)


def by_slot(array, axis, fill=0):
    shape = array.shape
    array = array.reshape(*shape[:axis], KVH, EACH, *shape[axis + 1 :])
    array = pad_to(array, axis + 1, 3 * PER, fill)
    return array.reshape(*shape[:axis], 3 * KVH, PER, *shape[axis + 1 :])


def moved(halves, turn):
    slices = lax.axis_size("z")
    moves = []
    for head in range(HQ):
        half = (turn - head % EACH % PER) % PER
        if half > 1:
            continue
        deep = head // EACH * 3 + head % EACH // PER
        for at in range(slices):
            moves.append((head * slices + at, (at * 2 + half) * slices + deep))
    slot = lax.rem(lax.rem(lax.axis_index(GRP), EACH), PER)
    half = jnp.minimum(lax.rem(turn - slot + PER, PER), 1)
    sent = lax.dynamic_index_in_dim(halves, half, 1, False)
    return lax.ppermute(sent, (*GRP, "z"), moves)


def attend(lengths_ref, here_ref, q_hbm, k_hbm, v_hbm, nk_hbm, nv_hbm, out_ref, q, k, v, nk, nv, small, large):
    rows, positions = k.shape[0], k.shape[1]
    half_rows = rows // 2
    first = [pltpu.make_async_copy(s, d, small.at[i]) for i, (s, d) in enumerate(((q_hbm, q), (nk_hbm, nk), (nv_hbm, nv)))]
    keys = [pltpu.make_async_copy(k_hbm.at[r], k.at[r], large.at[0, r]) for r in range(rows)]
    values = [pltpu.make_async_copy(v_hbm.at[r], v.at[r], large.at[1, r]) for r in range(rows)]
    for copy in first:
        copy.start()
    for r in range(rows):
        keys[r].start()
        values[r].start()
    here = here_ref[0]
    lines = half_rows * 2 * EACH

    def of_line(line):
        each = lax.rem(line, EACH)
        return lax.div(each, PER), lax.div(line, EACH) * PER + lax.rem(each, PER)

    out_line = lax.broadcasted_iota(jnp.int32, (3 * 16, 4 * lines), 0)
    source = lax.broadcasted_iota(jnp.int32, (3 * 16, 4 * lines), 1)
    block, zone_of = lax.div(source, lines), None
    zone_of, slot_of = of_line(lax.rem(source, lines))
    place = lax.rem(out_line, 16)
    wanted = jnp.where(block == 0, slot_of, half_rows * 2 * PER + block - 1)
    select = jnp.where((lax.div(out_line, 16) == zone_of) & (place == wanted), 1.0, 0.0).astype(jnp.bfloat16)
    line = lax.broadcasted_iota(jnp.int32, (lines, HD), 0)
    lane = lax.broadcasted_iota(jnp.int32, (lines, HD), 1)
    spread = of_line(line)[1] == lane
    step = lax.div(lax.broadcasted_iota(jnp.int32, (2 * EACH, 1), 0), EACH)
    fresh_ok = [(here == 0) & (step >= t) for t in range(2)]
    position = lax.broadcasted_iota(jnp.int32, (2 * EACH, positions), 1) + here * positions
    for copy in first:
        copy.wait()
    turned = (((1,), (1,)), ((), ()))
    for half in range(2):
        for r in range(half * half_rows, (half + 1) * half_rows):
            keys[r].wait()
            values[r].wait()
        for j in range(KVH):
            at = pl.ds(j * HD, HD)
            parts = []
            for r in range(half * half_rows, (half + 1) * half_rows):
                query = q[r, j]
                visible = position < lengths_ref[r]
                scores = lax.dot_general(query, k[r, :, at], turned, preferred_element_type=jnp.float32) * HD**-0.5
                scores = jnp.where(visible, scores, masked_score)
                wide = query.astype(jnp.float32)
                fresh = [
                    jnp.where(
                        fresh_ok[t],
                        jnp.sum(wide * nk[r, t : t + 1, at].astype(jnp.float32), axis=1, keepdims=True) * HD**-0.5,
                        masked_score,
                    )
                    for t in range(2)
                ]
                top = jnp.maximum(jnp.max(scores, axis=1, keepdims=True), jnp.maximum(*fresh))
                shift = top.astype(jnp.bfloat16).astype(jnp.float32)
                weights = jnp.where(visible, jnp.exp(scores - shift), 0.0)
                added = [jnp.where(fresh_ok[t], jnp.exp(fresh[t] - shift), 0.0) for t in range(2)]
                total = jnp.sum(weights, axis=1, keepdims=True) + added[0] + added[1]
                accum = jnp.dot(weights.astype(jnp.bfloat16), v[r, :, at], preferred_element_type=jnp.float32)
                for t in range(2):
                    accum += added[t].astype(jnp.bfloat16).astype(jnp.float32) * nv[r, t : t + 1, at].astype(jnp.float32)
                parts.append((accum, shift, total))
            accum, shift, total = (jnp.concatenate(list(p), axis=0) for p in zip(*parts))
            high = total.astype(jnp.bfloat16).astype(jnp.float32)
            stacked = jnp.concatenate(
                [accum] + [jnp.where(spread, stat, 0.0) for stat in (shift, high, total - high)], axis=0
            ).astype(jnp.bfloat16)
            chosen = jnp.dot(select, stacked, preferred_element_type=jnp.float32).astype(jnp.bfloat16)
            out_ref[pl.ds((half * KVH + j) * 3, 3)] = chosen.reshape(3, 16, HD)


def attention(queries, cache_keys, cache_values, new_keys, new_values, lengths, here):
    rows, steps, _ = queries.shape
    queries = jnp.swapaxes(queries.reshape(rows, steps, KVH, EACH, HD), 1, 2).reshape(rows, KVH, steps * EACH, HD)
    kinds = (queries, cache_keys, cache_values, new_keys, new_values)
    smem = pl.BlockSpec(memory_space=pltpu.SMEM)
    return pl.pallas_call(
        attend,
        out_shape=jax.ShapeDtypeStruct((2 * 3 * KVH, 16, HD), jnp.bfloat16),
        in_specs=[smem, smem] + [ANY] * 5,
        out_specs=pl.BlockSpec(memory_space=pltpu.VMEM),
        scratch_shapes=[pltpu.VMEM(a.shape, a.dtype) for a in kinds]
        + [pltpu.SemaphoreType.DMA((3,)), pltpu.SemaphoreType.DMA((2, rows))],
        cost_estimate=pl.CostEstimate(flops=10**8, bytes_accessed=1 << 20, transcendentals=1 << 15),
        name="attend",
    )(lengths, here, *kinds)


def layer(
    queries,
    cache_keys,
    cache_values,
    new_keys,
    new_values,
    lengths,
    residual,
    norm_gain,
    w_gate,
    w_down,
):
    rows, steps, features = queries.shape
    groups, halves, slices = lax.axis_size(GRP), lax.axis_size("xh"), lax.axis_size("z")
    tokens = rows * steps
    share = tokens // halves
    total_tokens = groups * tokens
    wide = PER * HD

    stacked = jnp.stack([w_gate.T, w_down.T]).astype(jnp.bfloat16)
    stacked = pad_to(stacked, 1, 2 * HALF).reshape(2, 2, HALF, HD)
    weights = [moved(stacked, turn) for turn in range(PER)]

    here = lax.axis_index(TP).reshape(1)
    sent = attention(queries, cache_keys, cache_values, new_keys, new_values, lengths, here)
    pieces = exchange(sent, TP)

    lines = share * PER
    stats = pieces[:, lines : lines + 3, :lines].astype(jnp.float32)
    joint = jnp.max(stats[:, 0], axis=0)
    factor = jnp.exp(stats[:, 0] - joint)
    total = jnp.sum(factor * (stats[:, 1] + stats[:, 2]), axis=0)
    total = jnp.where(total > 0, total, 1.0)
    context = jnp.sum(factor[..., None] * pieces[:, :lines].astype(jnp.float32), axis=0) / total[:, None]

    half, deep = lax.axis_index("xh"), lax.axis_index("z")
    mine = by_slot(residual.reshape(halves, share, HQ, HD), 2)
    mine = lax.dynamic_index_in_dim(lax.dynamic_index_in_dim(mine, half, 0, False), deep, 1, False)
    gain = lax.dynamic_index_in_dim(by_slot(norm_gain.reshape(HQ, HD), 0, 1.0), deep, 0, False)
    summed = mine.astype(jnp.float32) + context.reshape(share, PER, HD)
    gained = (summed * gain).astype(jnp.bfloat16)
    ordered = jnp.stack([gained, jnp.roll(gained, 1, axis=1)])
    ordered = jnp.broadcast_to(ordered[None, :, None], (groups // 2, 2, halves, share, PER, HD))
    gain = jnp.where(lax.axis_index("c") == 0, gain, jnp.roll(gain, 1, axis=0)).reshape(wide)
    ordered, gain, summed = lax.optimization_barrier((ordered.reshape(groups * halves, share, wide), gain, summed))
    arrived = exchange(ordered, WIDE)
    arrived = arrived.reshape(total_tokens, wide)

    unscaled = arrived.astype(jnp.float32) / gain
    squares = jnp.stack(two_words(jnp.sum(unscaled * unscaled, axis=-1)), axis=-1)
    turned = (((1,), (1,)), ((), ()))
    gate = sum(
        lax.dot_general(arrived[:, k * HD : (k + 1) * HD], w[0], turned, preferred_element_type=jnp.float32)
        for k, w in enumerate(weights)
    )
    sent = jnp.concatenate([gate.astype(jnp.bfloat16), squares], axis=-1)
    sent = pad_to(sent, 0, slices * NEAR).reshape(slices, NEAR, -1)
    sums = exchange(sent, "z").astype(jnp.float32).sum(axis=0)
    mean_square = (sums[:, HALF] + sums[:, HALF + 1]) / features
    gate = sums[:, :HALF] * lax.rsqrt(mean_square + 1e-05)[:, None]
    hidden = copies(jax.nn.silu(gate).astype(jnp.bfloat16), "z").reshape(slices * NEAR, HALF)[:total_tokens]
    terms = jnp.concatenate(
        [jnp.dot(hidden, w[1], preferred_element_type=jnp.float32).astype(jnp.bfloat16) for w in weights], axis=-1
    )
    terms, summed = lax.optimization_barrier((terms.reshape(groups * halves, share, wide), summed))
    partial = exchange(terms, WIDE).reshape(groups // 2, 2, halves, share, PER, HD)
    partial = partial.astype(jnp.float32).sum(axis=(0, 2))
    mixed = summed + partial[0] + jnp.roll(partial[1], -1, axis=1)
    mixed = copies(mixed.astype(jnp.bfloat16).reshape(share, wide), TP)
    mixed = jnp.swapaxes(mixed.reshape(halves, KVH, 3, share, PER, HD), 2, 3)
    mixed = jnp.swapaxes(mixed, 1, 2).reshape(tokens, KVH, 3 * PER, HD)[:, :, :EACH]
    return mixed.reshape(rows, steps, features)


def solution(mesh):
    fine = Mesh(mesh.devices.reshape(2, 8, 2, 2, 12), ("xl", "y", "c", "xh", "z"))
    return jax.shard_map(
        layer,
        mesh=fine,
        in_specs=(
            P(GRP, None, None),
            P(GRP, TP, None),
            P(GRP, TP, None),
            P(GRP, None, None),
            P(GRP, None, None),
            P(GRP),
            P(GRP, None, None),
            P(),
            P(GRP, TP),
            P(GRP, TP),
        ),
        out_specs=P(GRP, None, None),
        check_vma=False,
    )
```

time: 168 us -> 192 us (1.14)
  blocking collectives: 47.1 us -> 111 us
  waiting for transfers between devices: 67.1 us -> 34.3 us
  starting transfers between devices: 37.9 us -> 31.2 us
  Pallas kernels: 0 us -> 6.59 us
  local copies, waits for them, and re-layouts: 11.3 us -> 5.36 us
    all_to_all x3 -> x4, blocking collectives: 47.1 us -> 111 us  [exchange(): return lax.all_to_all(parts, axis, split_axis=0, concat_axis=0, tiled=True)]
    all_to_all x5 -> x2, waiting for transfers between devices: 67.1 us -> 18.4 us  [exchange(): return lax.all_to_all(parts, axis, split_axis=0, concat_axis=0, tiled=True)]
    ppermute x0 -> x3, waiting for transfers between devices: none -> 15.9 us  [moved(): return lax.ppermute(sent, (*GRP, 'z'), moves)]
    all_to_all x5 -> x2, starting transfers between devices: 37.9 us -> 26 us  [exchange(): return lax.all_to_all(parts, axis, split_axis=0, concat_axis=0, tiled=True)]
    pallas_call x0 -> x1, Pallas kernels: none -> 6.59 us  [attention(): pl.pallas_call(attend, out_shape=jax.ShapeDtypeStruct((2 * 3 * KVH, 16, H...]
    ppermute x0 -> x3, starting transfers between devices: none -> 5.23 us  [moved(): return lax.ppermute(sent, (*GRP, 'z'), moves)]
    pad x5 -> x3, local copies, waits for them, and re-layouts: 2.01 us -> 0.06 us  [pad_to(): return jnp.pad(array, widths, constant_values=fill)]
  transfers between devices with their start and end apart: 5 -> 5, of which waited for: 5 -> 3; matrix products, arithmetic and copies ran while one was open for 2% -> 1% of each run, Pallas kernels for 0% -> 0%
where the time goes in v3:
time: 192 us; the launch traced here: 191 us
  blocking collectives  111 us (58%)
  waiting for transfers between devices  34.3 us (18%)
  starting transfers between devices  31.2 us (16%)
  Pallas kernels  6.59 us (3%)
  local copies, waits for them, and re-layouts  5.36 us (3%)
    all_to_all x4, blocking collectives, exchange(): return lax.all_to_all(parts, axis, split_axis=0, concat_axis=0, tiled=True)  111 us
    all_to_all x2, starting transfers between devices, exchange(): return lax.all_to_all(parts, axis, split_axis=0, concat_axis=0, tiled=True)  26 us
    all_to_all x2, waiting for transfers between devices, exchange(): return lax.all_to_all(parts, axis, split_axis=0, concat_axis=0, tiled=True)  18.4 us
    ppermute x3, waiting for transfers between devices, moved(): return lax.ppermute(sent, (*GRP, 'z'), moves)  15.9 us
    pallas_call x1, Pallas kernels, attention(): pl.pallas_call(attend, out_shape=jax.ShapeDtypeStruct((2 * 3 * KVH, 16, H...  6.59 us
    ppermute x3, starting transfers between devices, moved(): return lax.ppermute(sent, (*GRP, 'z'), moves)  5.23 us
  transfers between devices with their start and end apart: 5, of which 3 were waited for; matrix products, arithmetic and copies ran while one was open for 1% of the time, Pallas kernels for 0%

profile of v3, /device:TPU:8, one launch (start us, length us, event | category | flops | bytes accessed | tf_op | source)
XLA Modules:
  0.0 191.1 jit_solution(14320314744241621319)
XLA Ops:
  0.0 0.9 reshape.162
  0.9 0.6 copy.113
  1.5 6.6 %attend.1 = bf16[24,16,128]{2,1,0:T(8,128)(2,1)} custom-call(s32[4]{0:T(128)} %lengths_ref.1, s32[1]{0:T(128)} %bitcast.2.here_ref, bf16[4,4,16,128]{3,2,1,0:T(8,128)(2,1)} %bitcast.108, bf16[4,128,512]{2,1,0:T(8,128)(2,1)} %k_hbm.1, bf16[4,128,512]{2,1,0:T(8,128)(2,1)} %v_hbm.1, bf16[4,2,512]{2,1,0:T(2,128)(2,1)} %nk_hbm.1, bf16[4,2,512]{2,1,0:T(2,128)(2,1)} %nv_hbm.1), custom_call_target="tpu_custom_call" | custom-call | flops 100000000 | bytes 1048576 | tf_op jit(solution)/shard_map/attend/pallas_call | solution.py:144
  8.1 17.8 %all-to-all-start = ((bf16[24,16,128]{2,1,0:T(8,128)(2,1)}), bf16[24,16,128]{2,1,0:T(8,128)(2,1)S(1)}, u32[]{:S(2)}, u32[]{:S(2)}) async-start(bf16[24,16,128]{2,1,0:T(8,128)(2,1)} %attend.1), calls=%async_computation | async-start | bytes 196608 | tf_op jit(solution)/shard_map/all_to_all | solution.py:25
  26.1 0.7 copy-done.3
  27.1 12.2 %all-to-all-done = bf16[24,16,128]{2,1,0:T(8,128)(2,1)S(1)} async-done(((bf16[24,16,128]{2,1,0:T(8,128)(2,1)}), bf16[24,16,128]{2,1,0:T(8,128)(2,1)S(1)}, u32[]{:S(2)}, u32[]{:S(2)}) %all-to-all-start) | async-done | bytes 98336 | tf_op jit(solution)/shard_map/all_to_all | solution.py:25
  40.1 0.8 copy.91
  41.0 8.1 %all-to-all-start.1 = ((bf16[64,4,384]{2,1,0:T(4,128)(2,1)}), bf16[64,4,384]{2,1,0:T(4,128)(2,1)S(1)}, u32[]{:S(2)}, u32[]{:S(2)}) async-start(bf16[64,4,384]{2,1,0:T(4,128)(2,1)} %copy.91), calls=%async_computation.1 | async-start | bytes 393216 | tf_op jit(solution)/shard_map/all_to_all | solution.py:25
  49.3 2.0 %collective-permute-start = (bf16[2,304,128]{2,1,0:T(8,128)(2,1)S(1)}, bf16[2,304,128]{2,1,0:T(8,128)(2,1)S(1)}, u32[]{:S(2)}, u32[]{:S(2)}) collective-permute-start(bf16[2,304,128]{2,1,0:T(8,128)(2,1)S(1)} %get-tuple-element.19), channel_id=1, source_target_pairs={{0,0},{1,48},{2,96},{3,144},{4,192},{5,240},{6,288},{7,336},{8,384... | collective-permute-start | bytes 466952 | tf_op jit(solution)/shard_map/ppermute | solution.py:63
  51.3 1.9 %collective-permute-start.2 = (bf16[2,304,128]{2,1,0:T(8,128)(2,1)S(1)}, bf16[2,304,128]{2,1,0:T(8,128)(2,1)S(1)}, u32[]{:S(2)}, u32[]{:S(2)}) collective-permute-start(bf16[2,304,128]{2,1,0:T(8,128)(2,1)S(1)} %get-tuple-element.20), channel_id=1, source_target_pairs={{24,24},{25,72},{26,120},{27,168},{28,216},{29,264},{30,312},{31,3... | collective-permute-start | bytes 466952 | tf_op jit(solution)/shard_map/ppermute | solution.py:63
  53.2 1.3 collective-permute-start.1
  54.5 6.2 %all-to-all-done.1 = bf16[64,4,384]{2,1,0:T(4,128)(2,1)S(1)} async-done(((bf16[64,4,384]{2,1,0:T(4,128)(2,1)}), bf16[64,4,384]{2,1,0:T(4,128)(2,1)S(1)}, u32[]{:S(2)}, u32[]{:S(2)}) %all-to-all-start.1) | async-done | bytes 196640 | tf_op jit(solution)/shard_map/all_to_all | solution.py:25
  61.1 15.9 %collective-permute-done.1 = bf16[2,304,128]{2,1,0:T(8,128)(2,1)S(1)} collective-permute-done((bf16[2,304,128]{2,1,0:T(8,128)(2,1)S(1)}, bf16[2,304,128]{2,1,0:T(8,128)(2,1)S(1)}, u32[]{:S(2)}, u32[]{:S(2)}) %collective-permute-start.1) | collective-permute-done | bytes 155680 | tf_op jit(solution)/shard_map/ppermute | solution.py:63
  77.1 0.2 fusion.9
  77.3 0.2 fusion.8
  77.5 0.2 fusion.1
  77.9 48.4 %all_to_all.30 = bf16[12,24,306]{2,1,0:T(8,128)(2,1)S(1)} all-to-all(bf16[12,24,306]{2,1,0:T(8,128)(2,1)S(1)} %bitcast.105), channel_id=1, replica_groups=mesh['xl'=2,'y'=8,'c'=2,'xh'=2,'z'=12] {'z'}, dimensions={0} | all-to-all | bytes 352512 | tf_op jit(solution)/shard_map/all_to_all | solution.py:25
  126.7 15.9 %all_to_all.31 = bf16[12,24,304]{2,1,0:T(8,128)(2,1)S(1)} all-to-all(bf16[12,24,304]{2,1,0:T(8,128)(2,1)S(1)} %broadcast_in_dim.12), channel_id=1, replica_groups=mesh['xl'=2,'y'=8,'c'=2,'xh'=2,'z'=12] {'z'}, dimensions={0} | all-to-all | bytes 350208 | tf_op jit(solution)/shard_map/all_to_all | solution.py:25
  142.6 0.2 convolution_convert_fusion.1
  142.9 0.2 convolution_convert_fusion
  143.1 0.2 convolution_convert_fusion.2
  143.6 29.3 %all_to_all.32 = bf16[64,4,384]{2,1,0:T(4,128)(2,1)S(1)} all-to-all(bf16[64,4,384]{2,1,0:T(4,128)(2,1)S(1)} %reshape.170), channel_id=1, replica_groups=mesh['xl'=2,'y'=8,'c'=2,'xh'=2,'z'=12] {'xl','y','c','xh'}, dimensions={0} | all-to-all | bytes 393216 | tf_op jit(solution)/shard_map/all_to_all | solution.py:25
  173.3 17.0 %all_to_all.33 = bf16[24,4,384]{2,1,0:T(4,128)(2,1)S(1)} all-to-all(bf16[24,4,384]{2,1,0:T(4,128)(2,1)S(1)} %broadcast_in_dim.13), channel_id=1, replica_groups=mesh['xl'=2,'y'=8,'c'=2,'xh'=2,'z'=12] {'xh','z'}, dimensions={0} | all-to-all | bytes 147456 | tf_op jit(solution)/shard_map/all_to_all | solution.py:25
  190.5 0.6 reshape.174
  (70 shorter events, 2.8 us)
Async XLA Ops:
  8.1 31.1 %all-to-all-start = ((bf16[24,16,128]{2,1,0:T(8,128)(2,1)}), bf16[24,16,128]{2,1,0:T(8,128)(2,1)S(1)}, u32[]{:S(2)}, u32[]{:S(2)}) async-start(bf16[24,16,128]{2,1,0:T(8,128)(2,1)} %attend.1), calls=%async_computation | async-start | bytes 196608 | tf_op jit(solution)/shard_map/all_to_all | solution.py:25
  26.0 0.7 copy-start.3
  26.1 0.8 copy-start.2
  40.1 9.0 %copy-start = (f32[128,600]{0,1:T(8,128)S(1)}, f32[128,600]{0,1:T(8,128)}, u32[]{:S(2)}) copy-start(f32[128,600]{0,1:T(8,128)} %param.19) | copy-start | bytes 921604
  40.1 9.0 %copy-start.1 = (f32[128,600]{0,1:T(8,128)S(1)}, f32[128,600]{0,1:T(8,128)}, u32[]{:S(2)}) copy-start(f32[128,600]{0,1:T(8,128)} %param.18) | copy-start | bytes 921604
  41.0 19.8 %all-to-all-start.1 = ((bf16[64,4,384]{2,1,0:T(4,128)(2,1)}), bf16[64,4,384]{2,1,0:T(4,128)(2,1)S(1)}, u32[]{:S(2)}, u32[]{:S(2)}) async-start(bf16[64,4,384]{2,1,0:T(4,128)(2,1)} %copy.91), calls=%async_computation.1 | async-start | bytes 393216 | tf_op jit(solution)/shard_map/all_to_all | solution.py:25
  49.3 28.2 %collective-permute-start = (bf16[2,304,128]{2,1,0:T(8,128)(2,1)S(1)}, bf16[2,304,128]{2,1,0:T(8,128)(2,1)S(1)}, u32[]{:S(2)}, u32[]{:S(2)}) collective-permute-start(bf16[2,304,128]{2,1,0:T(8,128)(2,1)S(1)} %get-tuple-element.19), channel_id=1, source_target_pairs={{0,0},{1,48},{2,96},{3,144},{4,192},{5,240},{6,288},{7,336},{8,384... | collective-permute-start | bytes 466952 | tf_op jit(solution)/shard_map/ppermute | solution.py:63
  51.3 26.0 %collective-permute-start.2 = (bf16[2,304,128]{2,1,0:T(8,128)(2,1)S(1)}, bf16[2,304,128]{2,1,0:T(8,128)(2,1)S(1)}, u32[]{:S(2)}, u32[]{:S(2)}) collective-permute-start(bf16[2,304,128]{2,1,0:T(8,128)(2,1)S(1)} %get-tuple-element.20), channel_id=1, source_target_pairs={{24,24},{25,72},{26,120},{27,168},{28,216},{29,264},{30,312},{31,3... | collective-permute-start | bytes 466952 | tf_op jit(solution)/shard_map/ppermute | solution.py:63
  53.2 23.9 %collective-permute-start.1 = (bf16[2,304,128]{2,1,0:T(8,128)(2,1)S(1)}, bf16[2,304,128]{2,1,0:T(8,128)(2,1)S(1)}, u32[]{:S(2)}, u32[]{:S(2)}) collective-permute-start(bf16[2,304,128]{2,1,0:T(8,128)(2,1)S(1)} %get-tuple-element.21), channel_id=1, source_target_pairs={{0,24},{1,72},{2,120},{3,168},{4,216},{5,264},{6,312},{7,360},{8,4... | collective-permute-start | bytes 466952 | tf_op jit(solution)/shard_map/ppermute | solution.py:63

commit v4 on v2

v4 whole, which is shorter than its diff:
```python
import jax
import jax.numpy as jnp
from jax import lax
from jax.experimental import pallas as pl
from jax.experimental.pallas import tpu as pltpu
from jax.sharding import Mesh
from jax.sharding import PartitionSpec as P


HD = 128
KVH = 4
HQ = 32
EACH = HQ // KVH
NEAR = 4
FAR = 3
LINES = 32
GRP = ("xl", "ya", "yb", "c")
TP = ("xh", "z2", "z1")
WIDE = ("xl", "ya", "yb", "c", "xh")
DEEP = ("xl", "c", "z1")
HALF = 304
masked_score = -1e30


def exchange(parts, axis):
    return lax.all_to_all(parts, axis, split_axis=0, concat_axis=0, tiled=True)


def copies(part, axis):
    return exchange(jnp.broadcast_to(part, (lax.axis_size(axis), *part.shape)), axis)


def two_words(value):
    high = value.astype(jnp.bfloat16)
    return high, (value - high.astype(jnp.float32)).astype(jnp.bfloat16)


def pad_to(array, axis, size):
    widths = [(0, 0)] * array.ndim
    widths[axis] = (0, size - array.shape[axis])
    return jnp.pad(array, widths)


def traded(halves, other):
    near = lax.axis_size("ya")
    moves = []
    for row in range(near):
        for pair in range(2):
            for deep in range(near):
                target = (deep * 2 + (pair ^ other)) * near + row
                moves.append(((row * 2 + pair) * near + deep, target))
    at = lax.axis_index("yb") ^ other
    sent = lax.dynamic_index_in_dim(halves, at, 1, False)
    return lax.ppermute(sent, ("ya", "yb", "z1"), moves)


def attend(lengths_ref, here_ref, q_hbm, k_hbm, v_hbm, nk_hbm, nv_hbm, out_ref, q, k, v, nk, nv, small, large):
    rows, positions = k.shape[0], k.shape[1]
    pairs = ((q_hbm, q), (nk_hbm, nk), (nv_hbm, nv))
    first = [pltpu.make_async_copy(s, d, small.at[i]) for i, (s, d) in enumerate(pairs)]
    keys = [pltpu.make_async_copy(k_hbm.at[r], k.at[r], large.at[0, r]) for r in range(rows)]
    values = [pltpu.make_async_copy(v_hbm.at[r], v.at[r], large.at[1, r]) for r in range(rows)]
    for copy in first + keys + values:
        copy.start()
    here = here_ref[0]
    block = 2 * EACH
    lines = rows * KVH * block
    each_row = KVH * block
    step = lax.rem(lax.broadcasted_iota(jnp.int32, (lines, 1), 0), 2)
    fresh_ok = [(here == 0) & (step >= t) for t in range(2)]
    lane = lax.broadcasted_iota(jnp.int32, (each_row, positions), 1) + here * positions
    visible = jnp.concatenate([lane < lengths_ref[r] for r in range(rows)], axis=0)

    def all_lines(part):
        return jnp.concatenate([part(r, j) for r in range(rows) for j in range(KVH)], axis=0)

    def head_of(ref, r, j):
        return ref[r, :, j * HD : (j + 1) * HD]

    for copy in first:
        copy.wait()
    queries = []
    for r in range(rows):
        row = q[r].astype(jnp.float32)
        queries += [row[:, h * HD : (h + 1) * HD] for h in range(HQ)]
    queries = jnp.concatenate(queries, axis=0)
    narrow = queries.astype(jnp.bfloat16)

    def fresh_of(ref, t):
        return all_lines(
            lambda r, j: jnp.broadcast_to(ref[r, t : t + 1, j * HD : (j + 1) * HD].astype(jnp.float32), (block, HD))
        )

    fresh = [
        jnp.where(fresh_ok[t], jnp.sum(queries * fresh_of(nk, t), axis=1, keepdims=True) * HD**-0.5, masked_score)
        for t in range(2)
    ]
    for copy in keys:
        copy.wait()

    def lines_of(array, r, j):
        at = (r * KVH + j) * block
        return array[at : at + block]

    turned = (((1,), (1,)), ((), ()))
    scores = all_lines(
        lambda r, j: lax.dot_general(
            lines_of(narrow, r, j), head_of(k, r, j), turned, preferred_element_type=jnp.float32
        )
    )
    scores = jnp.where(visible, scores * HD**-0.5, masked_score)
    top = jnp.maximum(jnp.max(scores, axis=1, keepdims=True), jnp.maximum(*fresh))
    shift = top.astype(jnp.bfloat16).astype(jnp.float32)
    weights = jnp.where(visible, jnp.exp(scores - shift), 0.0)
    added = [jnp.where(fresh_ok[t], jnp.exp(fresh[t] - shift), 0.0) for t in range(2)]
    total = jnp.sum(weights, axis=1, keepdims=True) + added[0] + added[1]
    weights = weights.astype(jnp.bfloat16)
    for copy in values:
        copy.wait()
    accum = all_lines(
        lambda r, j: jnp.dot(lines_of(weights, r, j), head_of(v, r, j), preferred_element_type=jnp.float32)
    )
    for t in range(2):
        accum += added[t].astype(jnp.bfloat16).astype(jnp.float32) * fresh_of(nv, t)
    high = total.astype(jnp.bfloat16).astype(jnp.float32)
    line = lax.broadcasted_iota(jnp.int32, (LINES, HD), 0)
    offset = lax.broadcasted_iota(jnp.int32, (LINES, HD), 1) - line
    for half in range(2):
        for near in range(NEAR):

            def lines_to(array):
                parts = []
                for r in range(half * rows // 2, (half + 1) * rows // 2):
                    for side in range(2):
                        at = (r * KVH + side * 2 + near // 2) * block + near % 2 * 8
                        parts.append(array[at : at + 8])
                return jnp.concatenate(parts, axis=0)

            lead = lines_to(high)
            stats = jnp.where(offset == 0, lines_to(shift), 0.0)
            stats = jnp.where(offset == LINES, lead, stats)
            stats = jnp.where(offset == 2 * LINES, lines_to(total) - lead, stats)
            stats = jnp.broadcast_to(jnp.sum(stats, axis=0, keepdims=True), (8, HD))
            whole = jnp.concatenate([lines_to(accum), stats], axis=0).astype(jnp.bfloat16)
            for far in range(FAR):
                out_ref[(half * FAR + far) * NEAR + near] = whole


def attention(queries, cache_keys, cache_values, new_keys, new_values, lengths, here):
    kinds = (queries, cache_keys, cache_values, new_keys, new_values)
    smem = pl.BlockSpec(memory_space=pltpu.SMEM)
    return pl.pallas_call(
        attend,
        out_shape=jax.ShapeDtypeStruct((2 * FAR * NEAR, LINES + 8, HD), jnp.bfloat16),
        in_specs=[smem, smem] + [pl.BlockSpec(memory_space=pl.ANY)] * 5,
        out_specs=pl.BlockSpec(memory_space=pltpu.VMEM),
        scratch_shapes=[pltpu.VMEM(a.shape, a.dtype) for a in kinds]
        + [pltpu.SemaphoreType.DMA((3,)), pltpu.SemaphoreType.DMA((2, queries.shape[0]))],
        cost_estimate=pl.CostEstimate(flops=10**8, bytes_accessed=1 << 20, transcendentals=1 << 15),
        name="attend",
    )(lengths, here, *kinds)


def layer(
    queries,
    cache_keys,
    cache_values,
    new_keys,
    new_values,
    lengths,
    residual,
    norm_gain,
    w_gate,
    w_down,
):
    rows, steps, features = queries.shape
    groups, halves = lax.axis_size(GRP), lax.axis_size("xh")
    tokens = rows * steps
    share = tokens // halves
    total_tokens = groups * tokens
    near, far = NEAR, FAR

    stacked = jnp.stack([w_gate.T, w_down.T]).astype(jnp.bfloat16)
    stacked = pad_to(stacked, 1, 2 * HALF).reshape(2, 2, HALF, HD)
    own, other = traded(stacked, 0), traded(stacked, 1)

    here = lax.axis_index(TP).reshape(1)
    sent = attention(queries, cache_keys, cache_values, new_keys, new_values, lengths, here)

    half, deep = lax.axis_index("xh"), lax.axis_index("z1")
    mine = residual.reshape(halves, share, 2, near, 4, HD)
    mine = lax.dynamic_index_in_dim(lax.dynamic_index_in_dim(mine, half, 0, False), deep, 2, False).astype(jnp.float32)
    gain = lax.dynamic_index_in_dim(norm_gain.reshape(2, near, 4, HD), deep, 1, False)
    pair = lax.axis_index("yb")
    own_gain = gain.reshape(2, 2, 2, HD)[lax.axis_index("xl"), :, lax.axis_index("c")]
    own_gain = jnp.where(pair == 0, own_gain, own_gain[::-1]).reshape(2 * HD)
    first = (lax.axis_index("z2") == 0).astype(jnp.float32)
    sent, mine, gain, own_gain, first = lax.optimization_barrier((sent, mine, gain, own_gain, first))
    pieces = exchange(sent, TP)

    stats = pieces[:, LINES, : 3 * LINES].astype(jnp.float32).reshape(-1, 3, LINES)
    joint = jnp.max(stats[:, 0], axis=0)
    factor = jnp.exp(stats[:, 0] - joint)
    total = jnp.sum(factor * (stats[:, 1] + stats[:, 2]), axis=0)
    context = jnp.sum(factor[..., None] * pieces[:, :LINES].astype(jnp.float32), axis=0) / total[:, None]
    context = jnp.transpose(context.reshape(rows // halves, 2, 4, steps, HD), (0, 3, 1, 2, 4))

    summed = mine + context.reshape(share, 2, 4, HD)
    gained = (summed * gain).astype(jnp.bfloat16).reshape(share, 2, 2, 2, HD)
    gained = jnp.transpose(gained, (1, 3, 0, 2, 4))
    ordered = jnp.stack([gained, gained[:, :, :, ::-1]], axis=1)
    ordered = jnp.broadcast_to(ordered[:, None, :, :, None], (2, near, 2, 2, halves, share, 2, HD))
    ordered = ordered.reshape(groups * halves, share, 2 * HD)
    kept = summed * first
    ordered, kept = lax.optimization_barrier((ordered, kept))
    arrived = exchange(ordered, WIDE)
    arrived = arrived.reshape(total_tokens, 2 * HD)

    unscaled = arrived.astype(jnp.float32) / own_gain
    squares = jnp.stack(two_words(jnp.sum(unscaled * unscaled, axis=-1)), axis=-1)
    turned = (((1,), (1,)), ((), ()))
    gate = lax.dot_general(arrived[:, :HD], own[0], turned, preferred_element_type=jnp.float32)
    gate = gate + lax.dot_general(arrived[:, HD:], other[0], turned, preferred_element_type=jnp.float32)
    sent = jnp.concatenate([gate.astype(jnp.bfloat16), squares], axis=-1)
    depth = lax.axis_size(DEEP)
    sums = exchange(sent.reshape(depth, total_tokens // depth, -1), DEEP).astype(jnp.float32).sum(axis=0)
    mean_square = (sums[:, HALF] + sums[:, HALF + 1]) / features
    gate = sums[:, :HALF] * lax.rsqrt(mean_square + 1e-05)[:, None]
    hidden = copies(jax.nn.silu(gate).astype(jnp.bfloat16), DEEP).reshape(total_tokens, HALF)
    terms = jnp.concatenate(
        [jnp.dot(hidden, w[1], preferred_element_type=jnp.float32).astype(jnp.bfloat16) for w in (own, other)], axis=-1
    )
    partial = exchange(terms.reshape(groups * halves, share, 2 * HD), WIDE)
    partial = partial.reshape(2, near, 2, 2, halves, share, 2, HD).astype(jnp.float32).sum(axis=(1, 4))
    mlp = partial[:, 0] + partial[:, 1, :, :, ::-1]
    mlp = jnp.transpose(mlp, (2, 0, 3, 1, 4)).reshape(share, 2, 4, HD)
    mixed = mlp + kept
    mixed = copies(mixed.astype(jnp.bfloat16).reshape(share, 8 * HD), TP)
    mixed = mixed.reshape(halves, far, near, share, 2, 4, HD).astype(jnp.float32).sum(axis=1)
    mixed = jnp.transpose(mixed, (0, 2, 3, 1, 4, 5))
    return mixed.astype(jnp.bfloat16).reshape(rows, steps, features)


def solution(mesh):
    fine = Mesh(mesh.devices.reshape(2, 4, 2, 2, 2, 3, 4), ("xl", "ya", "yb", "c", "xh", "z2", "z1"))
    return jax.shard_map(
        layer,
        mesh=fine,
        in_specs=(
            P(GRP, None, None),
            P(GRP, TP, None),
            P(GRP, TP, None),
            P(GRP, None, None),
            P(GRP, None, None),
            P(GRP),
            P(GRP, None, None),
            P(),
            P(GRP, TP),
            P(GRP, TP),
        ),
        out_specs=P(GRP, None, None),
        check_vma=False,
    )
```

time: 135 us -> 145 us (1.074)
  blocking collectives: 47.9 us -> 115 us
  starting transfers between devices: 38.9 us -> 11.2 us
  waiting for transfers between devices: 34.4 us -> 8.48 us
  local copies, waits for them, and re-layouts: 8.77 us -> 3.87 us
  Pallas kernels: 0 us -> 3.57 us
  matrix products: 2.32 us -> 0.86 us
    all_to_all x3 -> x5, blocking collectives: 47.9 us -> 115 us  [exchange(): return lax.all_to_all(parts, axis, split_axis=0, concat_axis=0, tiled=True)]
    all_to_all x3 -> x1, starting transfers between devices: 35.8 us -> 8.14 us  [exchange(): return lax.all_to_all(parts, axis, split_axis=0, concat_axis=0, tiled=True)]
    all_to_all x3 -> x1, waiting for transfers between devices: 34.4 us -> 7.11 us  [exchange(): return lax.all_to_all(parts, axis, split_axis=0, concat_axis=0, tiled=True)]
    pallas_call x0 -> x1, Pallas kernels: none -> 3.57 us  [attention(): pl.pallas_call(attend, out_shape=jax.ShapeDtypeStruct((2 * FAR * NEAR, LI...]
    reshape x10 -> x6, local copies, waits for them, and re-layouts: 4.54 us -> 1.52 us  [the longest x1 0.73 us: layer(): ordered = ordered.reshape(groups * halves, share, 2 * HD)]
    dot_general x8 -> x4, matrix products: 2.32 us -> 0.86 us  [the longest x2 0.47 us: layer(): jnp.dot(hidden, w[1], preferred_element_type=jnp.float32)]
  transfers between devices with their start and end apart: 5 -> 3, of which waited for: 3 -> 2; matrix products, arithmetic and copies ran while one was open for 2% -> 1% of each run, Pallas kernels for 0% -> 0%
where the time goes in v4:
time: 145 us
  blocking collectives  115 us (79%)
  starting transfers between devices  11.2 us (8%)
  waiting for transfers between devices  8.48 us (6%)
  local copies, waits for them, and re-layouts  3.87 us (3%)
  Pallas kernels  3.57 us (2%)
    all_to_all x5, blocking collectives, exchange(): return lax.all_to_all(parts, axis, split_axis=0, concat_axis=0, tiled=True)  115 us
    all_to_all x1, starting transfers between devices, exchange(): return lax.all_to_all(parts, axis, split_axis=0, concat_axis=0, tiled=True)  8.14 us
    all_to_all x1, waiting for transfers between devices, exchange(): return lax.all_to_all(parts, axis, split_axis=0, concat_axis=0, tiled=True)  7.11 us
    pallas_call x1, Pallas kernels, attention(): pl.pallas_call(attend, out_shape=jax.ShapeDtypeStruct((2 * FAR * NEAR, LI...  3.57 us
    ppermute x2, starting transfers between devices, traded(): return lax.ppermute(sent, ('ya', 'yb', 'z1'), moves)  3.03 us
  transfers between devices with their start and end apart: 3, of which 2 were waited for; matrix products, arithmetic and copies ran while one was open for 1% of the time, Pallas kernels for 0%

profile of v4, /device:TPU:8, one launch (start us, length us, event | category | flops | bytes accessed | tf_op | source)
XLA Modules:
  0.0 144.9 jit_solution(9207497968201115215)
XLA Ops:
  0.0 0.7 copy-done
  1.0 3.6 %attend.1 = bf16[24,40,128]{2,1,0:T(8,128)(2,1)} custom-call(s32[4]{0:T(128)} %lengths_ref.1, s32[1]{0:T(128)} %bitcast.here_ref, bf16[4,2,4096]{2,1,0:T(2,128)(2,1)} %q_hbm.1, bf16[4,128,512]{2,1,0:T(8,128)(2,1)} %k_hbm.1, bf16[4,128,512]{2,1,0:T(8,128)(2,1)} %v_hbm.1, bf16[4,2,512]{2,1,0:T(2,128)(2,1)} %nk_hbm.1, bf16[4,2,512]{2,1,0:T(2,128)(2,1)} %nv_hbm.1), custom_call_target="tpu_custom_call" | custom-call | flops 100000000 | bytes 1048576 | tf_op jit(solution)/shard_map/attend/pallas_call | solution.py:152
  4.5 35.2 %all_to_all.30 = bf16[24,40,128]{2,1,0:T(8,128)(2,1)S(1)} all-to-all(bf16[24,40,128]{2,1,0:T(8,128)(2,1)} %attend.1), channel_id=1, replica_groups=mesh['xl'=2,'ya'=4,'yb'=2,'c'=2,'xh'=2,'z2'=3,'z1'=4] {'xh','z2','z1'}, dimensions={0} | all-to-all | bytes 491520 | tf_op jit(solution)/shard_map/all_to_all | solution.py:26
  40.1 0.2 multiply_reduce_fusion
  40.6 0.7 reshape.140
  41.3 8.1 %all-to-all-start.1 = ((bf16[64,4,256]{2,1,0:T(4,128)(2,1)}), bf16[64,4,256]{2,1,0:T(4,128)(2,1)S(1)}, u32[]{:S(2)}, u32[]{:S(2)}) async-start(bf16[64,4,256]{2,1,0:T(4,128)(2,1)} %reshape.140), calls=%async_computation.1 | async-start | bytes 262144 | tf_op jit(solution)/shard_map/all_to_all | solution.py:26
  49.6 0.7 collective-permute-start
  50.3 2.4 %collective-permute-start.1 = (bf16[2,304,128]{2,1,0:T(8,128)(2,1)S(1)}, bf16[2,304,128]{2,1,0:T(8,128)(2,1)S(1)}, u32[]{:S(2)}, u32[]{:S(2)}) collective-permute-start(bf16[2,304,128]{2,1,0:T(8,128)(2,1)S(1)} %get-tuple-element.24), channel_id=1, source_target_pairs={{0,48},{1,144},{2,240},{3,336},{48,0},{49,96},{50,192},{51,288},{9... | collective-permute-start | bytes 466952 | tf_op jit(solution)/shard_map/ppermute | solution.py:54
  52.6 7.1 %all-to-all-done.1 = bf16[64,4,256]{2,1,0:T(4,128)(2,1)S(1)} async-done(((bf16[64,4,256]{2,1,0:T(4,128)(2,1)}), bf16[64,4,256]{2,1,0:T(4,128)(2,1)S(1)}, u32[]{:S(2)}, u32[]{:S(2)}) %all-to-all-start.1) | async-done | bytes 131104 | tf_op jit(solution)/shard_map/all_to_all | solution.py:26
  60.1 0.2 copy.93
  60.2 0.2 copy.92
  60.5 1.4 collective-permute-done.1
  61.9 0.2 fusion.4
  62.1 0.2 fusion
  62.3 0.2 copy.89
  62.5 26.3 %all_to_all.31 = bf16[16,16,306]{2,1,0:T(8,128)(2,1)S(1)} all-to-all(bf16[16,16,306]{2,1,0:T(8,128)(2,1)S(1)} %pad_maximum_fusion), channel_id=1, replica_groups=mesh['xl'=2,'ya'=4,'yb'=2,'c'=2,'xh'=2,'z2'=3,'z1'=4] {'xl','c','z1'}, dimensions={0} | all-to-all | bytes 313344 | tf_op jit(solution)/shard_map/all_to_all | solution.py:26
  88.9 0.2 fusion.12
  89.2 11.8 %all_to_all.32 = bf16[16,16,304]{2,1,0:T(8,128)(2,1)S(1)} all-to-all(bf16[16,16,304]{2,1,0:T(8,128)(2,1)S(1)} %broadcast_in_dim.7), channel_id=1, replica_groups=mesh['xl'=2,'ya'=4,'yb'=2,'c'=2,'xh'=2,'z2'=3,'z1'=4] {'xl','c','z1'}, dimensions={0} | all-to-all | bytes 311296 | tf_op jit(solution)/shard_map/all_to_all | solution.py:26
  101.0 0.2 convolution_convert_fusion
  101.2 0.2 convolution_convert_fusion.1
  101.6 21.1 %all_to_all.33 = bf16[64,4,256]{2,1,0:T(4,128)(2,1)S(1)} all-to-all(bf16[64,4,256]{2,1,0:T(4,128)(2,1)S(1)} %reshape.144), channel_id=1, replica_groups=mesh['xl'=2,'ya'=4,'yb'=2,'c'=2,'xh'=2,'z2'=3,'z1'=4] {'xl','ya','yb','c..., dimensions={0} | all-to-all | bytes 262144 | tf_op jit(solution)/shard_map/all_to_all | solution.py:26
  122.7 0.1 reshape.150
  123.2 20.8 %all_to_all.34 = bf16[24,4,1024]{2,1,0:T(4,128)(2,1)S(1)} all-to-all(bf16[24,4,1024]{2,1,0:T(4,128)(2,1)S(1)} %broadcast_in_dim.8), channel_id=1, replica_groups=mesh['xl'=2,'ya'=4,'yb'=2,'c'=2,'xh'=2,'z2'=3,'z1'=4] {'xh','z2','z1'}, dimensions={0} | all-to-all | bytes 393216 | tf_op jit(solution)/shard_map/all_to_all | solution.py:26
  144.2 0.6 reshape.147
  (54 shorter events, 2.0 us)
Async XLA Ops:
  0.0 0.7 copy-start
  0.0 0.9 copy-start.3
  40.5 9.0 %copy-start.1 = (f32[128,600]{0,1:T(8,128)S(1)}, f32[128,600]{0,1:T(8,128)}, u32[]{:S(2)}) copy-start(f32[128,600]{0,1:T(8,128)} %param.19) | copy-start | bytes 921604
  40.5 9.0 %copy-start.2 = (f32[128,600]{0,1:T(8,128)S(1)}, f32[128,600]{0,1:T(8,128)}, u32[]{:S(2)}) copy-start(f32[128,600]{0,1:T(8,128)} %param.18) | copy-start | bytes 921604
  41.3 18.5 %all-to-all-start.1 = ((bf16[64,4,256]{2,1,0:T(4,128)(2,1)}), bf16[64,4,256]{2,1,0:T(4,128)(2,1)S(1)}, u32[]{:S(2)}, u32[]{:S(2)}) async-start(bf16[64,4,256]{2,1,0:T(4,128)(2,1)} %reshape.140), calls=%async_computation.1 | async-start | bytes 262144 | tf_op jit(solution)/shard_map/all_to_all | solution.py:26
  49.6 12.5 %collective-permute-start = (bf16[2,304,128]{2,1,0:T(8,128)(2,1)S(1)}, bf16[2,304,128]{2,1,0:T(8,128)(2,1)S(1)}, u32[]{:S(2)}, u32[]{:S(2)}) collective-permute-start(bf16[2,304,128]{2,1,0:T(8,128)(2,1)S(1)} %get-tuple-element.23), channel_id=1, source_target_pairs={{0,0},{1,96},{2,192},{3,288},{48,48},{49,144},{50,240},{51,336},{9... | collective-permute-start | bytes 466952 | tf_op jit(solution)/shard_map/ppermute | solution.py:54
  50.3 11.6 %collective-permute-start.1 = (bf16[2,304,128]{2,1,0:T(8,128)(2,1)S(1)}, bf16[2,304,128]{2,1,0:T(8,128)(2,1)S(1)}, u32[]{:S(2)}, u32[]{:S(2)}) collective-permute-start(bf16[2,304,128]{2,1,0:T(8,128)(2,1)S(1)} %get-tuple-element.24), channel_id=1, source_target_pairs={{0,48},{1,144},{2,240},{3,336},{48,0},{49,96},{50,192},{51,288},{9... | collective-permute-start | bytes 466952 | tf_op jit(solution)/shard_map/ppermute | solution.py:54

commit v5 on v4

--- a/solution.py
+++ b/solution.py
@@ -18,7 +18,8 @@
 TP = ("xh", "z2", "z1")
 WIDE = ("xl", "ya", "yb", "c", "xh")
 DEEP = ("xl", "c", "z1")
-HALF = 304
+PIECE = 152
+HALF = 2 * PIECE
 masked_score = -1e30
 
 
@@ -41,16 +42,16 @@
     return jnp.pad(array, widths)
 
 
-def traded(halves, other):
-    near = lax.axis_size("ya")
+def traded(pieces, turn):
+    over, under = turn // 2, turn % 2
     moves = []
-    for row in range(near):
+    for row in range(NEAR):
         for pair in range(2):
-            for deep in range(near):
-                target = (deep * 2 + (pair ^ other)) * near + row
-                moves.append(((row * 2 + pair) * near + deep, target))
-    at = lax.axis_index("yb") ^ other
-    sent = lax.dynamic_index_in_dim(halves, at, 1, False)
+            for deep in range(NEAR):
+                target = (pair ^ over) * 2 + (deep // 2 ^ under)
+                moves.append(((row * 2 + pair) * NEAR + deep, (target * 2 + deep % 2) * NEAR + row))
+    at = (lax.axis_index("yb") ^ over) * 2 + (lax.axis_index("z1") // 2 ^ under)
+    sent = lax.dynamic_index_in_dim(pieces, at, 1, False)
     return lax.ppermute(sent, ("ya", "yb", "z1"), moves)
 
 
@@ -181,8 +182,8 @@
     near, far = NEAR, FAR
 
     stacked = jnp.stack([w_gate.T, w_down.T]).astype(jnp.bfloat16)
-    stacked = pad_to(stacked, 1, 2 * HALF).reshape(2, 2, HALF, HD)
-    own, other = traded(stacked, 0), traded(stacked, 1)
+    stacked = pad_to(stacked, 1, 4 * PIECE).reshape(2, 4, PIECE, HD)
+    moved = [traded(stacked, turn) for turn in range(4)]
 
     here = lax.axis_index(TP).reshape(1)
     sent = attention(queries, cache_keys, cache_values, new_keys, new_values, lengths, here)
@@ -191,11 +192,9 @@
     mine = residual.reshape(halves, share, 2, near, 4, HD)
     mine = lax.dynamic_index_in_dim(lax.dynamic_index_in_dim(mine, half, 0, False), deep, 2, False).astype(jnp.float32)
     gain = lax.dynamic_index_in_dim(norm_gain.reshape(2, near, 4, HD), deep, 1, False)
-    pair = lax.axis_index("yb")
     own_gain = gain.reshape(2, 2, 2, HD)[lax.axis_index("xl"), :, lax.axis_index("c")]
-    own_gain = jnp.where(pair == 0, own_gain, own_gain[::-1]).reshape(2 * HD)
+    own_gain = jnp.where(lax.axis_index("ya") < NEAR // 2, own_gain, own_gain[::-1]).reshape(2 * HD)
     first = (lax.axis_index("z2") == 0).astype(jnp.float32)
-    sent, mine, gain, own_gain, first = lax.optimization_barrier((sent, mine, gain, own_gain, first))
     pieces = exchange(sent, TP)
 
     stats = pieces[:, LINES, : 3 * LINES].astype(jnp.float32).reshape(-1, 3, LINES)
@@ -209,18 +208,25 @@
     gained = (summed * gain).astype(jnp.bfloat16).reshape(share, 2, 2, 2, HD)
     gained = jnp.transpose(gained, (1, 3, 0, 2, 4))
     ordered = jnp.stack([gained, gained[:, :, :, ::-1]], axis=1)
-    ordered = jnp.broadcast_to(ordered[:, None, :, :, None], (2, near, 2, 2, halves, share, 2, HD))
+    ordered = jnp.broadcast_to(ordered[:, :, None, :, None], (2, 2, near, 2, halves, share, 2, HD))
     ordered = ordered.reshape(groups * halves, share, 2 * HD)
     kept = summed * first
-    ordered, kept = lax.optimization_barrier((ordered, kept))
+    ordered, kept, own_gain = lax.optimization_barrier((ordered, kept, own_gain))
     arrived = exchange(ordered, WIDE)
     arrived = arrived.reshape(total_tokens, 2 * HD)
 
     unscaled = arrived.astype(jnp.float32) / own_gain
     squares = jnp.stack(two_words(jnp.sum(unscaled * unscaled, axis=-1)), axis=-1)
+    squares, moved = lax.optimization_barrier((squares, moved))
     turned = (((1,), (1,)), ((), ()))
-    gate = lax.dot_general(arrived[:, :HD], own[0], turned, preferred_element_type=jnp.float32)
-    gate = gate + lax.dot_general(arrived[:, HD:], other[0], turned, preferred_element_type=jnp.float32)
+    gate_weights, down_weights = (
+        [jnp.concatenate([moved[2 * block][kind], moved[2 * block + 1][kind]], axis=0) for block in range(2)]
+        for kind in range(2)
+    )
+    gate = sum(
+        lax.dot_general(arrived[:, at * HD : (at + 1) * HD], w, turned, preferred_element_type=jnp.float32)
+        for at, w in enumerate(gate_weights)
+    )
     sent = jnp.concatenate([gate.astype(jnp.bfloat16), squares], axis=-1)
     depth = lax.axis_size(DEEP)
     sums = exchange(sent.reshape(depth, total_tokens // depth, -1), DEEP).astype(jnp.float32).sum(axis=0)
@@ -228,10 +234,10 @@
     gate = sums[:, :HALF] * lax.rsqrt(mean_square + 1e-05)[:, None]
     hidden = copies(jax.nn.silu(gate).astype(jnp.bfloat16), DEEP).reshape(total_tokens, HALF)
     terms = jnp.concatenate(
-        [jnp.dot(hidden, w[1], preferred_element_type=jnp.float32).astype(jnp.bfloat16) for w in (own, other)], axis=-1
+        [jnp.dot(hidden, w, preferred_element_type=jnp.float32).astype(jnp.bfloat16) for w in down_weights], axis=-1
     )
     partial = exchange(terms.reshape(groups * halves, share, 2 * HD), WIDE)
-    partial = partial.reshape(2, near, 2, 2, halves, share, 2, HD).astype(jnp.float32).sum(axis=(1, 4))
+    partial = partial.reshape(2, 2, near, 2, halves, share, 2, HD).astype(jnp.float32).sum(axis=(2, 4))
     mlp = partial[:, 0] + partial[:, 1, :, :, ::-1]
     mlp = jnp.transpose(mlp, (2, 0, 3, 1, 4)).reshape(share, 2, 4, HD)
     mixed = mlp + kept

time: 145 us -> 146 us (level)
  blocking collectives: 115 us -> 65 us
  starting transfers between devices: 11.2 us -> 44.8 us
  waiting for transfers between devices: 8.48 us -> 26.1 us
    all_to_all x5 -> x4, blocking collectives: 115 us -> 65 us  [exchange(): return lax.all_to_all(parts, axis, split_axis=0, concat_axis=0, tiled=True)]
    all_to_all x1 -> x2, starting transfers between devices: 8.14 us -> 26 us  [exchange(): return lax.all_to_all(parts, axis, split_axis=0, concat_axis=0, tiled=True)]
    ppermute x2 -> x4, starting transfers between devices: 3.03 us -> 18.9 us  [traded(): return lax.ppermute(sent, ('ya', 'yb', 'z1'), moves)]
    all_to_all x1 -> x2, waiting for transfers between devices: 7.11 us -> 16.5 us  [exchange(): return lax.all_to_all(parts, axis, split_axis=0, concat_axis=0, tiled=True)]
    ppermute x2 -> x4, waiting for transfers between devices: 1.37 us -> 9.61 us  [traded(): return lax.ppermute(sent, ('ya', 'yb', 'z1'), moves)]
  transfers between devices with their start and end apart: 3 -> 6, of which waited for: 2 -> 3; matrix products, arithmetic and copies ran while one was open for 1% -> 0% of each run, Pallas kernels for 0% -> 0%
where the time goes in v5:
time: 146 us
  blocking collectives  65 us (45%)
  starting transfers between devices  44.8 us (31%)
  waiting for transfers between devices  26.1 us (18%)
  Pallas kernels  3.7 us (3%)
  local copies, waits for them, and re-layouts  3.5 us (2%)
    all_to_all x4, blocking collectives, exchange(): return lax.all_to_all(parts, axis, split_axis=0, concat_axis=0, tiled=True)  65 us
    all_to_all x2, starting transfers between devices, exchange(): return lax.all_to_all(parts, axis, split_axis=0, concat_axis=0, tiled=True)  26 us
    ppermute x4, starting transfers between devices, traded(): return lax.ppermute(sent, ('ya', 'yb', 'z1'), moves)  18.9 us
    all_to_all x2, waiting for transfers between devices, exchange(): return lax.all_to_all(parts, axis, split_axis=0, concat_axis=0, tiled=True)  16.5 us
    ppermute x4, waiting for transfers between devices, traded(): return lax.ppermute(sent, ('ya', 'yb', 'z1'), moves)  9.61 us
    pallas_call x1, Pallas kernels, attention(): pl.pallas_call(attend, out_shape=jax.ShapeDtypeStruct((2 * FAR * NEAR, LI...  3.7 us
  transfers between devices with their start and end apart: 6, of which 3 were waited for; matrix products, arithmetic and copies ran while one was open for 0% of the time, Pallas kernels for 0%

profile of v5, /device:TPU:8, one launch (start us, length us, event | category | flops | bytes accessed | tf_op | source)
XLA Modules:
  0.0 145.8 jit_solution(12504914298462784447)
XLA Ops:
  0.0 3.7 %attend.1 = bf16[24,40,128]{2,1,0:T(8,128)(2,1)} custom-call(s32[4]{0:T(128)} %lengths_ref.1, s32[1]{0:T(128)} %bitcast.1.here_ref, bf16[4,2,4096]{2,1,0:T(2,128)(2,1)} %q_hbm.1, bf16[4,128,512]{2,1,0:T(8,128)(2,1)} %k_hbm.1, bf16[4,128,512]{2,1,0:T(8,128)(2,1)} %v_hbm.1, bf16[4,2,512]{2,1,0:T(2,128)(2,1)} %nk_hbm.1, bf16[4,2,512]{2,1,0:T(2,128)(2,1)} %nv_hbm.1), custom_call_target="tpu_custom_call" | custom-call | flops 100000000 | bytes 1048576 | tf_op jit(solution)/shard_map/attend/pallas_call | solution.py:153
  3.7 17.8 %all-to-all-start = ((bf16[24,40,128]{2,1,0:T(8,128)(2,1)}), bf16[24,40,128]{2,1,0:T(8,128)(2,1)S(1)}, u32[]{:S(2)}, u32[]{:S(2)}) async-start(bf16[24,40,128]{2,1,0:T(8,128)(2,1)} %attend.1), calls=%async_computation | async-start | bytes 491520 | tf_op jit(solution)/shard_map/all_to_all | solution.py:27
  21.7 0.7 copy-done.3
  22.5 16.5 %all-to-all-done = bf16[24,40,128]{2,1,0:T(8,128)(2,1)S(1)} async-done(((bf16[24,40,128]{2,1,0:T(8,128)(2,1)}), bf16[24,40,128]{2,1,0:T(8,128)(2,1)S(1)}, u32[]{:S(2)}, u32[]{:S(2)}) %all-to-all-start) | async-done | bytes 245792 | tf_op jit(solution)/shard_map/all_to_all | solution.py:27
  39.3 0.2 multiply_reduce_fusion
  39.8 0.7 reshape.139
  40.5 8.1 %all-to-all-start.1 = ((bf16[64,4,256]{2,1,0:T(4,128)(2,1)}), bf16[64,4,256]{2,1,0:T(4,128)(2,1)S(1)}, u32[]{:S(2)}, u32[]{:S(2)}) async-start(bf16[64,4,256]{2,1,0:T(4,128)(2,1)} %reshape.139), calls=%async_computation.1 | async-start | bytes 262144 | tf_op jit(solution)/shard_map/all_to_all | solution.py:27
  48.9 3.4 %collective-permute-start.3 = (bf16[2,152,128]{2,1,0:T(8,128)(2,1)S(1)}, bf16[2,152,128]{2,1,0:T(8,128)(2,1)S(1)}, u32[]{:S(2)}, u32[]{:S(2)}) collective-permute-start(bf16[2,152,128]{2,1,0:T(8,128)(2,1)S(1)} %get-tuple-element.23), channel_id=1, source_target_pairs={{0,288},{1,336},{2,192},{3,240},{48,96},{49,144},{50,0},{51,48},{9... | collective-permute-start | bytes 233480 | tf_op jit(solution)/shard_map/ppermute | solution.py:55
  52.2 4.6 %collective-permute-start.2 = (bf16[2,152,128]{2,1,0:T(8,128)(2,1)S(1)}, bf16[2,152,128]{2,1,0:T(8,128)(2,1)S(1)}, u32[]{:S(2)}, u32[]{:S(2)}) collective-permute-start(bf16[2,152,128]{2,1,0:T(8,128)(2,1)S(1)} %get-tuple-element.24), channel_id=1, source_target_pairs={{0,192},{1,240},{2,288},{3,336},{48,0},{49,48},{50,96},{51,144},{9... | collective-permute-start | bytes 233480 | tf_op jit(solution)/shard_map/ppermute | solution.py:55
  56.9 5.8 %collective-permute-start.1 = (bf16[2,152,128]{2,1,0:T(8,128)(2,1)S(1)}, bf16[2,152,128]{2,1,0:T(8,128)(2,1)S(1)}, u32[]{:S(2)}, u32[]{:S(2)}) collective-permute-start(bf16[2,152,128]{2,1,0:T(8,128)(2,1)S(1)} %get-tuple-element.25), channel_id=1, source_target_pairs={{0,96},{1,144},{2,0},{3,48},{48,288},{49,336},{50,192},{51,240},{9... | collective-permute-start | bytes 233480 | tf_op jit(solution)/shard_map/ppermute | solution.py:55
  62.7 5.1 %collective-permute-start = (bf16[2,152,128]{2,1,0:T(8,128)(2,1)S(1)}, bf16[2,152,128]{2,1,0:T(8,128)(2,1)S(1)}, u32[]{:S(2)}, u32[]{:S(2)}) collective-permute-start(bf16[2,152,128]{2,1,0:T(8,128)(2,1)S(1)} %get-tuple-element.26), channel_id=1, source_target_pairs={{0,0},{1,48},{2,96},{3,144},{48,192},{49,240},{50,288},{51,336},{9... | collective-permute-start | bytes 233480 | tf_op jit(solution)/shard_map/ppermute | solution.py:55
  68.1 0.7 collective-permute-done.2
  68.8 8.9 %collective-permute-done = bf16[2,152,128]{2,1,0:T(8,128)(2,1)S(1)} collective-permute-done((bf16[2,152,128]{2,1,0:T(8,128)(2,1)S(1)}, bf16[2,152,128]{2,1,0:T(8,128)(2,1)S(1)}, u32[]{:S(2)}, u32[]{:S(2)}) %collective-permute-start) | collective-permute-done | bytes 77856 | tf_op jit(solution)/shard_map/ppermute | solution.py:55
  77.8 0.2 fusion.4
  78.0 0.2 fusion
  78.3 0.2 copy.83
  78.4 13.8 %all_to_all.30 = bf16[16,16,306]{2,1,0:T(8,128)(2,1)S(1)} all-to-all(bf16[16,16,306]{2,1,0:T(8,128)(2,1)S(1)} %bitcast.75), channel_id=1, replica_groups=mesh['xl'=2,'ya'=4,'yb'=2,'c'=2,'xh'=2,'z2'=3,'z1'=4] {'xl','c','z1'}, dimensions={0} | all-to-all | bytes 313344 | tf_op jit(solution)/shard_map/all_to_all | solution.py:27
  92.3 0.2 fusion.25
  92.6 11.8 %all_to_all.31 = bf16[16,16,304]{2,1,0:T(8,128)(2,1)S(1)} all-to-all(bf16[16,16,304]{2,1,0:T(8,128)(2,1)S(1)} %broadcast_in_dim.7), channel_id=1, replica_groups=mesh['xl'=2,'ya'=4,'yb'=2,'c'=2,'xh'=2,'z2'=3,'z1'=4] {'xl','c','z1'}, dimensions={0} | all-to-all | bytes 311296 | tf_op jit(solution)/shard_map/all_to_all | solution.py:27
  104.4 0.3 convolution_convert_fusion
  104.6 0.3 convolution_convert_fusion.1
  105.1 18.9 %all_to_all.32 = bf16[64,4,256]{2,1,0:T(4,128)(2,1)S(1)} all-to-all(bf16[64,4,256]{2,1,0:T(4,128)(2,1)S(1)} %reshape.146), channel_id=1, replica_groups=mesh['xl'=2,'ya'=4,'yb'=2,'c'=2,'xh'=2,'z2'=3,'z1'=4] {'xl','ya','yb','c..., dimensions={0} | all-to-all | bytes 262144 | tf_op jit(solution)/shard_map/all_to_all | solution.py:27
  124.3 20.5 %all_to_all.33 = bf16[24,4,1024]{2,1,0:T(4,128)(2,1)S(1)} all-to-all(bf16[24,4,1024]{2,1,0:T(4,128)(2,1)S(1)} %broadcast_in_dim.8), channel_id=1, replica_groups=mesh['xl'=2,'ya'=4,'yb'=2,'c'=2,'xh'=2,'z2'=3,'z1'=4] {'xh','z2','z1'}, dimensions={0} | all-to-all | bytes 393216 | tf_op jit(solution)/shard_map/all_to_all | solution.py:27
  145.1 0.6 reshape.149
  (63 shorter events, 2.1 us)
Async XLA Ops:
  0.0 21.6 %copy-start = (f32[4096]{0:T(1024)S(1)}, f32[4096]{0:T(1024)}, u32[]{:S(2)}) copy-start(f32[4096]{0:T(1024)} %param.17) | copy-start | bytes 49156
  3.7 35.3 %all-to-all-start = ((bf16[24,40,128]{2,1,0:T(8,128)(2,1)}), bf16[24,40,128]{2,1,0:T(8,128)(2,1)S(1)}, u32[]{:S(2)}, u32[]{:S(2)}) async-start(bf16[24,40,128]{2,1,0:T(8,128)(2,1)} %attend.1), calls=%async_computation | async-start | bytes 491520 | tf_op jit(solution)/shard_map/all_to_all | solution.py:27
  21.6 0.8 copy-start.3
  39.7 9.0 %copy-start.1 = (f32[128,600]{0,1:T(8,128)S(1)}, f32[128,600]{0,1:T(8,128)}, u32[]{:S(2)}) copy-start(f32[128,600]{0,1:T(8,128)} %param.19) | copy-start | bytes 921604
  39.7 9.0 %copy-start.2 = (f32[128,600]{0,1:T(8,128)S(1)}, f32[128,600]{0,1:T(8,128)}, u32[]{:S(2)}) copy-start(f32[128,600]{0,1:T(8,128)} %param.18) | copy-start | bytes 921604
  40.5 27.2 %all-to-all-start.1 = ((bf16[64,4,256]{2,1,0:T(4,128)(2,1)}), bf16[64,4,256]{2,1,0:T(4,128)(2,1)S(1)}, u32[]{:S(2)}, u32[]{:S(2)}) async-start(bf16[64,4,256]{2,1,0:T(4,128)(2,1)} %reshape.139), calls=%async_computation.1 | async-start | bytes 262144 | tf_op jit(solution)/shard_map/all_to_all | solution.py:27
  48.9 19.3 %collective-permute-start.3 = (bf16[2,152,128]{2,1,0:T(8,128)(2,1)S(1)}, bf16[2,152,128]{2,1,0:T(8,128)(2,1)S(1)}, u32[]{:S(2)}, u32[]{:S(2)}) collective-permute-start(bf16[2,152,128]{2,1,0:T(8,128)(2,1)S(1)} %get-tuple-element.23), channel_id=1, source_target_pairs={{0,288},{1,336},{2,192},{3,240},{48,96},{49,144},{50,0},{51,48},{9... | collective-permute-start | bytes 233480 | tf_op jit(solution)/shard_map/ppermute | solution.py:55
  52.2 16.5 %collective-permute-start.2 = (bf16[2,152,128]{2,1,0:T(8,128)(2,1)S(1)}, bf16[2,152,128]{2,1,0:T(8,128)(2,1)S(1)}, u32[]{:S(2)}, u32[]{:S(2)}) collective-permute-start(bf16[2,152,128]{2,1,0:T(8,128)(2,1)S(1)} %get-tuple-element.24), channel_id=1, source_target_pairs={{0,192},{1,240},{2,288},{3,336},{48,0},{49,48},{50,96},{51,144},{9... | collective-permute-start | bytes 233480 | tf_op jit(solution)/shard_map/ppermute | solution.py:55
  56.9 11.9 %collective-permute-start.1 = (bf16[2,152,128]{2,1,0:T(8,128)(2,1)S(1)}, bf16[2,152,128]{2,1,0:T(8,128)(2,1)S(1)}, u32[]{:S(2)}, u32[]{:S(2)}) collective-permute-start(bf16[2,152,128]{2,1,0:T(8,128)(2,1)S(1)} %get-tuple-element.25), channel_id=1, source_target_pairs={{0,96},{1,144},{2,0},{3,48},{48,288},{49,336},{50,192},{51,240},{9... | collective-permute-start | bytes 233480 | tf_op jit(solution)/shard_map/ppermute | solution.py:55
  62.7 15.1 %collective-permute-start = (bf16[2,152,128]{2,1,0:T(8,128)(2,1)S(1)}, bf16[2,152,128]{2,1,0:T(8,128)(2,1)S(1)}, u32[]{:S(2)}, u32[]{:S(2)}) collective-permute-start(bf16[2,152,128]{2,1,0:T(8,128)(2,1)S(1)} %get-tuple-element.26), channel_id=1, source_target_pairs={{0,0},{1,48},{2,96},{3,144},{48,192},{49,240},{50,288},{51,336},{9... | collective-permute-start | bytes 233480 | tf_op jit(solution)/shard_map/ppermute | solution.py:55

commit v6 on v5

--- a/solution.py
+++ b/solution.py
@@ -18,8 +18,7 @@
 TP = ("xh", "z2", "z1")
 WIDE = ("xl", "ya", "yb", "c", "xh")
 DEEP = ("xl", "c", "z1")
-PIECE = 152
-HALF = 2 * PIECE
+HALF = 304
 masked_score = -1e30
 
 
@@ -42,16 +41,14 @@
     return jnp.pad(array, widths)
 
 
-def traded(pieces, turn):
-    over, under = turn // 2, turn % 2
+def traded(halves, turn):
     moves = []
     for row in range(NEAR):
         for pair in range(2):
             for deep in range(NEAR):
-                target = (pair ^ over) * 2 + (deep // 2 ^ under)
-                moves.append(((row * 2 + pair) * NEAR + deep, (target * 2 + deep % 2) * NEAR + row))
-    at = (lax.axis_index("yb") ^ over) * 2 + (lax.axis_index("z1") // 2 ^ under)
-    sent = lax.dynamic_index_in_dim(pieces, at, 1, False)
+                target = (pair ^ turn) * NEAR + deep
+                moves.append(((row * 2 + pair) * NEAR + deep, target * NEAR + row))
+    sent = lax.dynamic_index_in_dim(halves, lax.axis_index("yb") ^ turn, 0, False)
     return lax.ppermute(sent, ("ya", "yb", "z1"), moves)
 
 
@@ -181,9 +178,11 @@
     total_tokens = groups * tokens
     near, far = NEAR, FAR
 
-    stacked = jnp.stack([w_gate.T, w_down.T]).astype(jnp.bfloat16)
-    stacked = pad_to(stacked, 1, 4 * PIECE).reshape(2, 4, PIECE, HD)
-    moved = [traded(stacked, turn) for turn in range(4)]
+    def moved(weights):
+        halves = pad_to(weights.T.astype(jnp.bfloat16), 0, 2 * HALF).reshape(2, HALF, HD)
+        return [traded(halves, turn) for turn in range(2)]
+
+    gate_weights, down_weights = moved(w_gate), moved(w_down)
 
     here = lax.axis_index(TP).reshape(1)
     sent = attention(queries, cache_keys, cache_values, new_keys, new_values, lengths, here)
@@ -217,12 +216,7 @@
 
     unscaled = arrived.astype(jnp.float32) / own_gain
     squares = jnp.stack(two_words(jnp.sum(unscaled * unscaled, axis=-1)), axis=-1)
-    squares, moved = lax.optimization_barrier((squares, moved))
     turned = (((1,), (1,)), ((), ()))
-    gate_weights, down_weights = (
-        [jnp.concatenate([moved[2 * block][kind], moved[2 * block + 1][kind]], axis=0) for block in range(2)]
-        for kind in range(2)
-    )
     gate = sum(
         lax.dot_general(arrived[:, at * HD : (at + 1) * HD], w, turned, preferred_element_type=jnp.float32)
         for at, w in enumerate(gate_weights)
@@ -232,7 +226,9 @@
     sums = exchange(sent.reshape(depth, total_tokens // depth, -1), DEEP).astype(jnp.float32).sum(axis=0)
     mean_square = (sums[:, HALF] + sums[:, HALF + 1]) / features
     gate = sums[:, :HALF] * lax.rsqrt(mean_square + 1e-05)[:, None]
-    hidden = copies(jax.nn.silu(gate).astype(jnp.bfloat16), DEEP).reshape(total_tokens, HALF)
+    hidden = jax.nn.silu(gate).astype(jnp.bfloat16)
+    hidden, down_weights = lax.optimization_barrier((hidden, down_weights))
+    hidden = copies(hidden, DEEP).reshape(total_tokens, HALF)
     terms = jnp.concatenate(
         [jnp.dot(hidden, w, preferred_element_type=jnp.float32).astype(jnp.bfloat16) for w in down_weights], axis=-1
     )

time: 146 us -> 147 us (level)
  blocking collectives: 65 us -> 52.9 us
  waiting for transfers between devices: 26.1 us -> 38.1 us
    all_to_all x4 -> x3, blocking collectives: 65 us -> 52.9 us  [exchange(): return lax.all_to_all(parts, axis, split_axis=0, concat_axis=0, tiled=True)]
    ppermute x4, waiting for transfers between devices: 9.61 us -> 17.7 us  [traded(): return lax.ppermute(sent, ('ya', 'yb', 'z1'), moves)]
    all_to_all x2 -> x3, waiting for transfers between devices: 16.5 us -> 20.4 us  [exchange(): return lax.all_to_all(parts, axis, split_axis=0, concat_axis=0, tiled=True)]
    all_to_all x2 -> x3, starting transfers between devices: 26 us -> 29.9 us  [exchange(): return lax.all_to_all(parts, axis, split_axis=0, concat_axis=0, tiled=True)]
    ppermute x4, starting transfers between devices: 18.9 us -> 15 us  [traded(): return lax.ppermute(sent, ('ya', 'yb', 'z1'), moves)]
  transfers between devices with their start and end apart: 6 -> 7, of which waited for: 3 -> 6; matrix products, arithmetic and copies ran while one was open for 0% -> 1% of each run, Pallas kernels for 0% -> 0%
where the time goes in v6:
time: 147 us; the launch traced here: 146 us
  blocking collectives  52.9 us (36%)
  starting transfers between devices  44.9 us (31%)
  waiting for transfers between devices  38.1 us (26%)
  Pallas kernels  3.7 us (3%)
  local copies, waits for them, and re-layouts  3.12 us (2%)
  other arithmetic  1.97 us (1%)
    all_to_all x3, blocking collectives, exchange(): return lax.all_to_all(parts, axis, split_axis=0, concat_axis=0, tiled=True)  52.9 us
    all_to_all x3, starting transfers between devices, exchange(): return lax.all_to_all(parts, axis, split_axis=0, concat_axis=0, tiled=True)  29.9 us
    all_to_all x3, waiting for transfers between devices, exchange(): return lax.all_to_all(parts, axis, split_axis=0, concat_axis=0, tiled=True)  20.4 us
    ppermute x4, waiting for transfers between devices, traded(): return lax.ppermute(sent, ('ya', 'yb', 'z1'), moves)  17.7 us
    ppermute x4, starting transfers between devices, traded(): return lax.ppermute(sent, ('ya', 'yb', 'z1'), moves)  15 us
    pallas_call x1, Pallas kernels, attention(): pl.pallas_call(attend, out_shape=jax.ShapeDtypeStruct((2 * FAR * NEAR, LI...  3.7 us
  transfers between devices with their start and end apart: 7, of which 6 were waited for; matrix products, arithmetic and copies ran while one was open for 1% of the time, Pallas kernels for 0%

profile of v6, /device:TPU:8, one launch (start us, length us, event | category | flops | bytes accessed | tf_op | source)
XLA Modules:
  0.0 146.0 jit_solution(8849019146304912551)
XLA Ops:
  0.0 3.7 %attend.1 = bf16[24,40,128]{2,1,0:T(8,128)(2,1)} custom-call(s32[4]{0:T(128)} %lengths_ref.1, s32[1]{0:T(128)} %bitcast.1.here_ref, bf16[4,2,4096]{2,1,0:T(2,128)(2,1)} %q_hbm.1, bf16[4,128,512]{2,1,0:T(8,128)(2,1)} %k_hbm.1, bf16[4,128,512]{2,1,0:T(8,128)(2,1)} %v_hbm.1, bf16[4,2,512]{2,1,0:T(2,128)(2,1)} %nk_hbm.1, bf16[4,2,512]{2,1,0:T(2,128)(2,1)} %nv_hbm.1), custom_call_target="tpu_custom_call" | custom-call | flops 100000000 | bytes 1048576 | tf_op jit(solution)/shard_map/attend/pallas_call | solution.py:150
  3.7 18.0 %all-to-all-start = ((bf16[24,40,128]{2,1,0:T(8,128)(2,1)}), bf16[24,40,128]{2,1,0:T(8,128)(2,1)S(1)}, u32[]{:S(2)}, u32[]{:S(2)}) async-start(bf16[24,40,128]{2,1,0:T(8,128)(2,1)} %attend.1), calls=%async_computation | async-start | bytes 491520 | tf_op jit(solution)/shard_map/all_to_all | solution.py:26
  21.9 17.2 %all-to-all-done = bf16[24,40,128]{2,1,0:T(8,128)(2,1)S(1)} async-done(((bf16[24,40,128]{2,1,0:T(8,128)(2,1)}), bf16[24,40,128]{2,1,0:T(8,128)(2,1)S(1)}, u32[]{:S(2)}, u32[]{:S(2)}) %all-to-all-start) | async-done | bytes 245792 | tf_op jit(solution)/shard_map/all_to_all | solution.py:26
  39.9 0.7 reshape.145
  40.7 8.1 %all-to-all-start.1 = ((bf16[64,4,256]{2,1,0:T(4,128)(2,1)}), bf16[64,4,256]{2,1,0:T(4,128)(2,1)S(1)}, u32[]{:S(2)}, u32[]{:S(2)}) async-start(bf16[64,4,256]{2,1,0:T(4,128)(2,1)} %reshape.145), calls=%async_computation.1 | async-start | bytes 262144 | tf_op jit(solution)/shard_map/all_to_all | solution.py:26
  48.9 2.4 %collective-permute-start.1 = (bf16[304,128]{1,0:T(8,128)(2,1)S(1)}, bf16[304,128]{1,0:T(8,128)(2,1)S(1)}, u32[]{:S(2)}, u32[]{:S(2)}) collective-permute-start(bf16[304,128]{1,0:T(8,128)(2,1)S(1)} %get-tuple-element.24), channel_id=1, source_target_pairs={{0,192},{1,240},{2,288},{3,336},{48,0},{49,48},{50,96},{51,144},{9... | collective-permute-start | bytes 233480 | tf_op jit(solution)/shard_map/ppermute | solution.py:52
  51.3 7.2 %collective-permute-start = (bf16[304,128]{1,0:T(8,128)(2,1)S(1)}, bf16[304,128]{1,0:T(8,128)(2,1)S(1)}, u32[]{:S(2)}, u32[]{:S(2)}) collective-permute-start(bf16[304,128]{1,0:T(8,128)(2,1)S(1)} %get-tuple-element.23), channel_id=1, source_target_pairs={{0,0},{1,48},{2,96},{3,144},{48,192},{49,240},{50,288},{51,336},{9... | collective-permute-start | bytes 233480 | tf_op jit(solution)/shard_map/ppermute | solution.py:52
  58.4 0.7 all-to-all-done.1
  59.5 0.2 fusion.1
  59.7 0.2 copy.101
  60.1 8.1 %collective-permute-done = bf16[304,128]{1,0:T(8,128)(2,1)S(1)} collective-permute-done((bf16[304,128]{1,0:T(8,128)(2,1)S(1)}, bf16[304,128]{1,0:T(8,128)(2,1)S(1)}, u32[]{:S(2)}, u32[]{:S(2)}) %collective-permute-start) | collective-permute-done | bytes 77856 | tf_op jit(solution)/shard_map/ppermute | solution.py:52
  68.1 0.2 fusion
  68.5 0.8 pad_maximum_fusion
  69.3 3.8 %all-to-all-start.2 = ((bf16[16,16,306]{2,1,0:T(8,128)(2,1)}), bf16[16,16,306]{2,1,0:T(8,128)(2,1)S(1)}, u32[]{:S(2)}, u32[]{:S(2)}) async-start(bf16[16,16,306]{2,1,0:T(8,128)(2,1)} %pad_maximum_fusion), calls=%async_computation.2 | async-start | bytes 393216 | tf_op jit(solution)/shard_map/all_to_all | solution.py:26
  73.1 3.6 %collective-permute-start.2 = (bf16[304,128]{1,0:T(8,128)(2,1)S(1)}, bf16[304,128]{1,0:T(8,128)(2,1)S(1)}, u32[]{:S(2)}, u32[]{:S(2)}) collective-permute-start(bf16[304,128]{1,0:T(8,128)(2,1)S(1)} %get-tuple-element.22), channel_id=1, source_target_pairs={{0,0},{1,48},{2,96},{3,144},{48,192},{49,240},{50,288},{51,336},{9... | collective-permute-start | bytes 233480 | tf_op jit(solution)/shard_map/ppermute | solution.py:52
  76.7 1.9 %collective-permute-start.3 = (bf16[304,128]{1,0:T(8,128)(2,1)S(1)}, bf16[304,128]{1,0:T(8,128)(2,1)S(1)}, u32[]{:S(2)}, u32[]{:S(2)}) collective-permute-start(bf16[304,128]{1,0:T(8,128)(2,1)S(1)} %get-tuple-element.21), channel_id=1, source_target_pairs={{0,192},{1,240},{2,288},{3,336},{48,0},{49,48},{50,96},{51,144},{9... | collective-permute-start | bytes 233480 | tf_op jit(solution)/shard_map/ppermute | solution.py:52
  78.7 2.5 %all-to-all-done.2 = bf16[16,16,306]{2,1,0:T(8,128)(2,1)S(1)} async-done(((bf16[16,16,306]{2,1,0:T(8,128)(2,1)}), bf16[16,16,306]{2,1,0:T(8,128)(2,1)S(1)}, u32[]{:S(2)}, u32[]{:S(2)}) %all-to-all-start.2) | async-done | bytes 156704 | tf_op jit(solution)/shard_map/all_to_all | solution.py:26
  81.6 9.5 %collective-permute-done.3 = bf16[304,128]{1,0:T(8,128)(2,1)S(1)} collective-permute-done((bf16[304,128]{1,0:T(8,128)(2,1)S(1)}, bf16[304,128]{1,0:T(8,128)(2,1)S(1)}, u32[]{:S(2)}, u32[]{:S(2)}) %collective-permute-start.3) | collective-permute-done | bytes 77856 | tf_op jit(solution)/shard_map/ppermute | solution.py:52
  91.2 13.0 %all_to_all.30 = bf16[16,16,304]{2,1,0:T(8,128)(2,1)S(1)} all-to-all(bf16[16,16,304]{2,1,0:T(8,128)(2,1)S(1)} %broadcast_in_dim.7), channel_id=1, replica_groups=mesh['xl'=2,'ya'=4,'yb'=2,'c'=2,'xh'=2,'z2'=3,'z1'=4] {'xl','c','z1'}, dimensions={0} | all-to-all | bytes 311296 | tf_op jit(solution)/shard_map/all_to_all | solution.py:26
  104.2 0.2 convolution_convert_fusion
  104.4 0.2 convolution_convert_fusion.1
  104.8 18.8 %all_to_all.31 = bf16[64,4,256]{2,1,0:T(4,128)(2,1)S(1)} all-to-all(bf16[64,4,256]{2,1,0:T(4,128)(2,1)S(1)} %reshape.152), channel_id=1, replica_groups=mesh['xl'=2,'ya'=4,'yb'=2,'c'=2,'xh'=2,'z2'=3,'z1'=4] {'xl','ya','yb','c..., dimensions={0} | all-to-all | bytes 262144 | tf_op jit(solution)/shard_map/all_to_all | solution.py:26
  124.1 21.0 %all_to_all.32 = bf16[24,4,1024]{2,1,0:T(4,128)(2,1)S(1)} all-to-all(bf16[24,4,1024]{2,1,0:T(4,128)(2,1)S(1)} %broadcast_in_dim.8), channel_id=1, replica_groups=mesh['xl'=2,'ya'=4,'yb'=2,'c'=2,'xh'=2,'z2'=3,'z1'=4] {'xh','z2','z1'}, dimensions={0} | all-to-all | bytes 393216 | tf_op jit(solution)/shard_map/all_to_all | solution.py:26
  145.3 0.6 reshape.155
  (64 shorter events, 2.9 us)
Async XLA Ops:
  0.0 21.8 %copy-start = (f32[4096]{0:T(1024)S(1)}, f32[4096]{0:T(1024)}, u32[]{:S(2)}) copy-start(f32[4096]{0:T(1024)} %param.17) | copy-start | bytes 49156
  3.7 18.0 %copy-start.3 = (bf16[4,2,4096]{2,1,0:T(2,128)(2,1)S(1)}, bf16[4,2,4096]{2,1,0:T(2,128)(2,1)}, u32[]{:S(2)}) copy-start(bf16[4,2,4096]{2,1,0:T(2,128)(2,1)} %param.16) | copy-start | bytes 196612
  3.7 35.4 %all-to-all-start = ((bf16[24,40,128]{2,1,0:T(8,128)(2,1)}), bf16[24,40,128]{2,1,0:T(8,128)(2,1)S(1)}, u32[]{:S(2)}, u32[]{:S(2)}) async-start(bf16[24,40,128]{2,1,0:T(8,128)(2,1)} %attend.1), calls=%async_computation | async-start | bytes 491520 | tf_op jit(solution)/shard_map/all_to_all | solution.py:26
  39.9 8.9 %copy-start.1 = (f32[128,600]{0,1:T(8,128)S(1)}, f32[128,600]{0,1:T(8,128)}, u32[]{:S(2)}) copy-start(f32[128,600]{0,1:T(8,128)} %param.18) | copy-start | bytes 921604
  40.7 18.5 %all-to-all-start.1 = ((bf16[64,4,256]{2,1,0:T(4,128)(2,1)}), bf16[64,4,256]{2,1,0:T(4,128)(2,1)S(1)}, u32[]{:S(2)}, u32[]{:S(2)}) async-start(bf16[64,4,256]{2,1,0:T(4,128)(2,1)} %reshape.145), calls=%async_computation.1 | async-start | bytes 262144 | tf_op jit(solution)/shard_map/all_to_all | solution.py:26
  48.9 10.6 %collective-permute-start.1 = (bf16[304,128]{1,0:T(8,128)(2,1)S(1)}, bf16[304,128]{1,0:T(8,128)(2,1)S(1)}, u32[]{:S(2)}, u32[]{:S(2)}) collective-permute-start(bf16[304,128]{1,0:T(8,128)(2,1)S(1)} %get-tuple-element.24), channel_id=1, source_target_pairs={{0,192},{1,240},{2,288},{3,336},{48,0},{49,48},{50,96},{51,144},{9... | collective-permute-start | bytes 233480 | tf_op jit(solution)/shard_map/ppermute | solution.py:52
  51.3 16.9 %collective-permute-start = (bf16[304,128]{1,0:T(8,128)(2,1)S(1)}, bf16[304,128]{1,0:T(8,128)(2,1)S(1)}, u32[]{:S(2)}, u32[]{:S(2)}) collective-permute-start(bf16[304,128]{1,0:T(8,128)(2,1)S(1)} %get-tuple-element.23), channel_id=1, source_target_pairs={{0,0},{1,48},{2,96},{3,144},{48,192},{49,240},{50,288},{51,336},{9... | collective-permute-start | bytes 233480 | tf_op jit(solution)/shard_map/ppermute | solution.py:52
  69.3 3.8 %copy-start.2 = (f32[128,600]{0,1:T(8,128)S(1)}, f32[128,600]{0,1:T(8,128)}, u32[]{:S(2)}) copy-start(f32[128,600]{0,1:T(8,128)} %param.19) | copy-start | bytes 921604
  69.3 11.9 %all-to-all-start.2 = ((bf16[16,16,306]{2,1,0:T(8,128)(2,1)}), bf16[16,16,306]{2,1,0:T(8,128)(2,1)S(1)}, u32[]{:S(2)}, u32[]{:S(2)}) async-start(bf16[16,16,306]{2,1,0:T(8,128)(2,1)} %pad_maximum_fusion), calls=%async_computation.2 | async-start | bytes 393216 | tf_op jit(solution)/shard_map/all_to_all | solution.py:26
  73.1 8.5 %collective-permute-start.2 = (bf16[304,128]{1,0:T(8,128)(2,1)S(1)}, bf16[304,128]{1,0:T(8,128)(2,1)S(1)}, u32[]{:S(2)}, u32[]{:S(2)}) collective-permute-start(bf16[304,128]{1,0:T(8,128)(2,1)S(1)} %get-tuple-element.22), channel_id=1, source_target_pairs={{0,0},{1,48},{2,96},{3,144},{48,192},{49,240},{50,288},{51,336},{9... | collective-permute-start | bytes 233480 | tf_op jit(solution)/shard_map/ppermute | solution.py:52
  76.7 14.4 %collective-permute-start.3 = (bf16[304,128]{1,0:T(8,128)(2,1)S(1)}, bf16[304,128]{1,0:T(8,128)(2,1)S(1)}, u32[]{:S(2)}, u32[]{:S(2)}) collective-permute-start(bf16[304,128]{1,0:T(8,128)(2,1)S(1)} %get-tuple-element.21), channel_id=1, source_target_pairs={{0,192},{1,240},{2,288},{3,336},{48,0},{49,48},{50,96},{51,144},{9... | collective-permute-start | bytes 233480 | tf_op jit(solution)/shard_map/ppermute | solution.py:52

commit v7 on v6

--- a/solution.py
+++ b/solution.py
@@ -48,7 +48,7 @@
             for deep in range(NEAR):
                 target = (pair ^ turn) * NEAR + deep
                 moves.append(((row * 2 + pair) * NEAR + deep, target * NEAR + row))
-    sent = lax.dynamic_index_in_dim(halves, lax.axis_index("yb") ^ turn, 0, False)
+    sent = lax.dynamic_index_in_dim(halves, lax.axis_index("yb") ^ turn, 1, False)
     return lax.ppermute(sent, ("ya", "yb", "z1"), moves)
 
 
@@ -178,11 +178,10 @@
     total_tokens = groups * tokens
     near, far = NEAR, FAR
 
-    def moved(weights):
-        halves = pad_to(weights.T.astype(jnp.bfloat16), 0, 2 * HALF).reshape(2, HALF, HD)
-        return [traded(halves, turn) for turn in range(2)]
-
-    gate_weights, down_weights = moved(w_gate), moved(w_down)
+    stacked = jnp.stack([w_gate.T, w_down.T]).astype(jnp.bfloat16)
+    halves_of = pad_to(stacked, 1, 2 * HALF).reshape(2, 2, HALF, HD)
+    moved = [traded(halves_of, turn) for turn in range(2)]
+    gate_weights, down_weights = ([pieces[kind] for pieces in moved] for kind in range(2))
 
     here = lax.axis_index(TP).reshape(1)
     sent = attention(queries, cache_keys, cache_values, new_keys, new_values, lengths, here)
@@ -227,7 +226,6 @@
     mean_square = (sums[:, HALF] + sums[:, HALF + 1]) / features
     gate = sums[:, :HALF] * lax.rsqrt(mean_square + 1e-05)[:, None]
     hidden = jax.nn.silu(gate).astype(jnp.bfloat16)
-    hidden, down_weights = lax.optimization_barrier((hidden, down_weights))
     hidden = copies(hidden, DEEP).reshape(total_tokens, HALF)
     terms = jnp.concatenate(
         [jnp.dot(hidden, w, preferred_element_type=jnp.float32).astype(jnp.bfloat16) for w in down_weights], axis=-1

time: 147 us -> 145 us (0.986)
  starting transfers between devices: 44.9 us -> 34.3 us
  blocking collectives: 52.9 us -> 61.9 us
    all_to_all x3 -> x4, blocking collectives: 52.9 us -> 61.9 us  [exchange(): return lax.all_to_all(parts, axis, split_axis=0, concat_axis=0, tiled=True)]
    ppermute x4 -> x2, starting transfers between devices: 15 us -> 8.31 us  [traded(): return lax.ppermute(sent, ('ya', 'yb', 'z1'), moves)]
    all_to_all x3 -> x2, starting transfers between devices: 29.9 us -> 26 us  [exchange(): return lax.all_to_all(parts, axis, split_axis=0, concat_axis=0, tiled=True)]
    all_to_all x3 -> x2, waiting for transfers between devices: 20.4 us -> 18.3 us  [exchange(): return lax.all_to_all(parts, axis, split_axis=0, concat_axis=0, tiled=True)]
    ppermute x4 -> x2, waiting for transfers between devices: 17.7 us -> 19.5 us  [traded(): return lax.ppermute(sent, ('ya', 'yb', 'z1'), moves)]
  transfers between devices with their start and end apart: 7 -> 4, of which waited for: 6 -> 3; matrix products, arithmetic and copies ran while one was open for 1% -> 1% of each run, Pallas kernels for 0% -> 0%
where the time goes in v7:
time: 145 us; the launch traced here: 144 us
  blocking collectives  61.9 us (43%)
  waiting for transfers between devices  37.8 us (26%)
  starting transfers between devices  34.3 us (24%)
  local copies, waits for them, and re-layouts  3.82 us (3%)
  Pallas kernels  3.7 us (3%)
    all_to_all x4, blocking collectives, exchange(): return lax.all_to_all(parts, axis, split_axis=0, concat_axis=0, tiled=True)  61.9 us
    all_to_all x2, starting transfers between devices, exchange(): return lax.all_to_all(parts, axis, split_axis=0, concat_axis=0, tiled=True)  26 us
    ppermute x2, waiting for transfers between devices, traded(): return lax.ppermute(sent, ('ya', 'yb', 'z1'), moves)  19.5 us
    all_to_all x2, waiting for transfers between devices, exchange(): return lax.all_to_all(parts, axis, split_axis=0, concat_axis=0, tiled=True)  18.3 us
    ppermute x2, starting transfers between devices, traded(): return lax.ppermute(sent, ('ya', 'yb', 'z1'), moves)  8.31 us
    pallas_call x1, Pallas kernels, attention(): pl.pallas_call(attend, out_shape=jax.ShapeDtypeStruct((2 * FAR * NEAR, LI...  3.7 us
  transfers between devices with their start and end apart: 4, of which 3 were waited for; matrix products, arithmetic and copies ran while one was open for 1% of the time, Pallas kernels for 0%

profile of v7, /device:TPU:8, one launch (start us, length us, event | category | flops | bytes accessed | tf_op | source)
XLA Modules:
  0.0 144.2 jit_solution(6756410497078391227)
XLA Ops:
  0.0 3.7 %attend.1 = bf16[24,40,128]{2,1,0:T(8,128)(2,1)} custom-call(s32[4]{0:T(128)} %lengths_ref.1, s32[1]{0:T(128)} %bitcast.1.here_ref, bf16[4,2,4096]{2,1,0:T(2,128)(2,1)} %q_hbm.1, bf16[4,128,512]{2,1,0:T(8,128)(2,1)} %k_hbm.1, bf16[4,128,512]{2,1,0:T(8,128)(2,1)} %v_hbm.1, bf16[4,2,512]{2,1,0:T(2,128)(2,1)} %nk_hbm.1, bf16[4,2,512]{2,1,0:T(2,128)(2,1)} %nv_hbm.1), custom_call_target="tpu_custom_call" | custom-call | flops 100000000 | bytes 1048576 | tf_op jit(solution)/shard_map/attend/pallas_call | solution.py:150
  3.7 17.8 %all-to-all-start = ((bf16[24,40,128]{2,1,0:T(8,128)(2,1)}), bf16[24,40,128]{2,1,0:T(8,128)(2,1)S(1)}, u32[]{:S(2)}, u32[]{:S(2)}) async-start(bf16[24,40,128]{2,1,0:T(8,128)(2,1)} %attend.1), calls=%async_computation | async-start | bytes 491520 | tf_op jit(solution)/shard_map/all_to_all | solution.py:26
  21.7 0.7 copy-done.3
  22.5 16.5 %all-to-all-done = bf16[24,40,128]{2,1,0:T(8,128)(2,1)S(1)} async-done(((bf16[24,40,128]{2,1,0:T(8,128)(2,1)}), bf16[24,40,128]{2,1,0:T(8,128)(2,1)S(1)}, u32[]{:S(2)}, u32[]{:S(2)}) %all-to-all-start) | async-done | bytes 245792 | tf_op jit(solution)/shard_map/all_to_all | solution.py:26
  39.3 0.2 multiply_reduce_fusion
  39.8 0.7 reshape.142
  40.5 8.1 %all-to-all-start.1 = ((bf16[64,4,256]{2,1,0:T(4,128)(2,1)}), bf16[64,4,256]{2,1,0:T(4,128)(2,1)S(1)}, u32[]{:S(2)}, u32[]{:S(2)}) async-start(bf16[64,4,256]{2,1,0:T(4,128)(2,1)} %reshape.142), calls=%async_computation.1 | async-start | bytes 262144 | tf_op jit(solution)/shard_map/all_to_all | solution.py:26
  48.8 6.4 %collective-permute-start = (bf16[2,304,128]{2,1,0:T(8,128)(2,1)S(1)}, bf16[2,304,128]{2,1,0:T(8,128)(2,1)S(1)}, u32[]{:S(2)}, u32[]{:S(2)}) collective-permute-start(bf16[2,304,128]{2,1,0:T(8,128)(2,1)S(1)} %get-tuple-element.15), channel_id=1, source_target_pairs={{0,0},{1,48},{2,96},{3,144},{48,192},{49,240},{50,288},{51,336},{9... | collective-permute-start | bytes 466952 | tf_op jit(solution)/shard_map/ppermute | solution.py:52
  55.2 1.9 %collective-permute-start.1 = (bf16[2,304,128]{2,1,0:T(8,128)(2,1)S(1)}, bf16[2,304,128]{2,1,0:T(8,128)(2,1)S(1)}, u32[]{:S(2)}, u32[]{:S(2)}) collective-permute-start(bf16[2,304,128]{2,1,0:T(8,128)(2,1)S(1)} %get-tuple-element.16), channel_id=1, source_target_pairs={{0,192},{1,240},{2,288},{3,336},{48,0},{49,48},{50,96},{51,144},{9... | collective-permute-start | bytes 466952 | tf_op jit(solution)/shard_map/ppermute | solution.py:52
  57.2 1.8 %all-to-all-done.1 = bf16[64,4,256]{2,1,0:T(4,128)(2,1)S(1)} async-done(((bf16[64,4,256]{2,1,0:T(4,128)(2,1)}), bf16[64,4,256]{2,1,0:T(4,128)(2,1)S(1)}, u32[]{:S(2)}, u32[]{:S(2)}) %all-to-all-start.1) | async-done | bytes 131104 | tf_op jit(solution)/shard_map/all_to_all | solution.py:26
  59.3 0.2 copy.101
  59.5 0.2 copy.100
  59.7 19.5 %collective-permute-done.1 = bf16[2,304,128]{2,1,0:T(8,128)(2,1)S(1)} collective-permute-done((bf16[2,304,128]{2,1,0:T(8,128)(2,1)S(1)}, bf16[2,304,128]{2,1,0:T(8,128)(2,1)S(1)}, u32[]{:S(2)}, u32[]{:S(2)}) %collective-permute-start.1) | collective-permute-done | bytes 155680 | tf_op jit(solution)/shard_map/ppermute | solution.py:52
  79.2 0.2 fusion.4
  79.4 0.2 fusion
  79.6 0.2 copy.97
  79.9 10.9 %all_to_all.30 = bf16[16,16,306]{2,1,0:T(8,128)(2,1)S(1)} all-to-all(bf16[16,16,306]{2,1,0:T(8,128)(2,1)S(1)} %pad_maximum_fusion), channel_id=1, replica_groups=mesh['xl'=2,'ya'=4,'yb'=2,'c'=2,'xh'=2,'z2'=3,'z1'=4] {'xl','c','z1'}, dimensions={0} | all-to-all | bytes 313344 | tf_op jit(solution)/shard_map/all_to_all | solution.py:26
  90.9 0.2 fusion.13
  91.2 11.8 %all_to_all.31 = bf16[16,16,304]{2,1,0:T(8,128)(2,1)S(1)} all-to-all(bf16[16,16,304]{2,1,0:T(8,128)(2,1)S(1)} %broadcast_in_dim.7), channel_id=1, replica_groups=mesh['xl'=2,'ya'=4,'yb'=2,'c'=2,'xh'=2,'z2'=3,'z1'=4] {'xl','c','z1'}, dimensions={0} | all-to-all | bytes 311296 | tf_op jit(solution)/shard_map/all_to_all | solution.py:26
  102.9 0.2 convolution_convert_fusion
  103.2 0.2 convolution_convert_fusion.1
  103.6 19.0 %all_to_all.32 = bf16[64,4,256]{2,1,0:T(4,128)(2,1)S(1)} all-to-all(bf16[64,4,256]{2,1,0:T(4,128)(2,1)S(1)} %reshape.148), channel_id=1, replica_groups=mesh['xl'=2,'ya'=4,'yb'=2,'c'=2,'xh'=2,'z2'=3,'z1'=4] {'xl','ya','yb','c..., dimensions={0} | all-to-all | bytes 262144 | tf_op jit(solution)/shard_map/all_to_all | solution.py:26
  123.0 20.3 %all_to_all.33 = bf16[24,4,1024]{2,1,0:T(4,128)(2,1)S(1)} all-to-all(bf16[24,4,1024]{2,1,0:T(4,128)(2,1)S(1)} %broadcast_in_dim.8), channel_id=1, replica_groups=mesh['xl'=2,'ya'=4,'yb'=2,'c'=2,'xh'=2,'z2'=3,'z1'=4] {'xh','z2','z1'}, dimensions={0} | all-to-all | bytes 393216 | tf_op jit(solution)/shard_map/all_to_all | solution.py:26
  143.5 0.6 reshape.151
  (56 shorter events, 2.1 us)
Async XLA Ops:
  0.0 21.6 %copy-start = (f32[4096]{0:T(1024)S(1)}, f32[4096]{0:T(1024)}, u32[]{:S(2)}) copy-start(f32[4096]{0:T(1024)} %param.17) | copy-start | bytes 49156
  3.7 35.3 %all-to-all-start = ((bf16[24,40,128]{2,1,0:T(8,128)(2,1)}), bf16[24,40,128]{2,1,0:T(8,128)(2,1)S(1)}, u32[]{:S(2)}, u32[]{:S(2)}) async-start(bf16[24,40,128]{2,1,0:T(8,128)(2,1)} %attend.1), calls=%async_computation | async-start | bytes 491520 | tf_op jit(solution)/shard_map/all_to_all | solution.py:26
  21.6 0.8 copy-start.3
  39.7 9.0 %copy-start.1 = (f32[128,600]{0,1:T(8,128)S(1)}, f32[128,600]{0,1:T(8,128)}, u32[]{:S(2)}) copy-start(f32[128,600]{0,1:T(8,128)} %param.19) | copy-start | bytes 921604
  39.7 9.0 %copy-start.2 = (f32[128,600]{0,1:T(8,128)S(1)}, f32[128,600]{0,1:T(8,128)}, u32[]{:S(2)}) copy-start(f32[128,600]{0,1:T(8,128)} %param.18) | copy-start | bytes 921604
  40.5 18.5 %all-to-all-start.1 = ((bf16[64,4,256]{2,1,0:T(4,128)(2,1)}), bf16[64,4,256]{2,1,0:T(4,128)(2,1)S(1)}, u32[]{:S(2)}, u32[]{:S(2)}) async-start(bf16[64,4,256]{2,1,0:T(4,128)(2,1)} %reshape.142), calls=%async_computation.1 | async-start | bytes 262144 | tf_op jit(solution)/shard_map/all_to_all | solution.py:26
  48.8 30.6 %collective-permute-start = (bf16[2,304,128]{2,1,0:T(8,128)(2,1)S(1)}, bf16[2,304,128]{2,1,0:T(8,128)(2,1)S(1)}, u32[]{:S(2)}, u32[]{:S(2)}) collective-permute-start(bf16[2,304,128]{2,1,0:T(8,128)(2,1)S(1)} %get-tuple-element.15), channel_id=1, source_target_pairs={{0,0},{1,48},{2,96},{3,144},{48,192},{49,240},{50,288},{51,336},{9... | collective-permute-start | bytes 466952 | tf_op jit(solution)/shard_map/ppermute | solution.py:52
  55.2 24.0 %collective-permute-start.1 = (bf16[2,304,128]{2,1,0:T(8,128)(2,1)S(1)}, bf16[2,304,128]{2,1,0:T(8,128)(2,1)S(1)}, u32[]{:S(2)}, u32[]{:S(2)}) collective-permute-start(bf16[2,304,128]{2,1,0:T(8,128)(2,1)S(1)} %get-tuple-element.16), channel_id=1, source_target_pairs={{0,192},{1,240},{2,288},{3,336},{48,0},{49,48},{50,96},{51,144},{9... | collective-permute-start | bytes 466952 | tf_op jit(solution)/shard_map/ppermute | solution.py:52

commit v8 on v6

--- a/solution.py
+++ b/solution.py
@@ -223,12 +223,13 @@
     )
     sent = jnp.concatenate([gate.astype(jnp.bfloat16), squares], axis=-1)
     depth = lax.axis_size(DEEP)
-    sums = exchange(sent.reshape(depth, total_tokens // depth, -1), DEEP).astype(jnp.float32).sum(axis=0)
+    sums = exchange(sent.reshape(depth, total_tokens // depth, -1), DEEP)
+    sums = sums.astype(jnp.float32).sum(axis=0)
     mean_square = (sums[:, HALF] + sums[:, HALF + 1]) / features
     gate = sums[:, :HALF] * lax.rsqrt(mean_square + 1e-05)[:, None]
     hidden = jax.nn.silu(gate).astype(jnp.bfloat16)
-    hidden, down_weights = lax.optimization_barrier((hidden, down_weights))
-    hidden = copies(hidden, DEEP).reshape(total_tokens, HALF)
+    hidden = copies(hidden, DEEP)
+    hidden = hidden.reshape(total_tokens, HALF)
     terms = jnp.concatenate(
         [jnp.dot(hidden, w, preferred_element_type=jnp.float32).astype(jnp.bfloat16) for w in down_weights], axis=-1
     )

time: 147 us -> 146 us (level)
  starting transfers between devices: 44.9 us -> 47.4 us
  waiting for transfers between devices: 38.1 us -> 35.8 us
    all_to_all x3, waiting for transfers between devices: 20.4 us -> 17.9 us  [exchange(): return lax.all_to_all(parts, axis, split_axis=0, concat_axis=0, tiled=True)]
    ppermute x4, starting transfers between devices: 15 us -> 17.3 us  [traded(): return lax.ppermute(sent, ('ya', 'yb', 'z1'), moves)]
  transfers between devices with their start and end apart: 7 -> 7, of which waited for: 6 -> 5; matrix products, arithmetic and copies ran while one was open for 1% -> 1% of each run, Pallas kernels for 0% -> 0%
where the time goes in v8:
time: 146 us; the launch traced here: 145 us
  blocking collectives  52.1 us (36%)
  starting transfers between devices  47.4 us (32%)
  waiting for transfers between devices  35.8 us (25%)
  local copies, waits for them, and re-layouts  3.8 us (3%)
  Pallas kernels  3.7 us (3%)
    all_to_all x3, blocking collectives, exchange(): return lax.all_to_all(parts, axis, split_axis=0, concat_axis=0, tiled=True)  52.1 us
    all_to_all x3, starting transfers between devices, exchange(): return lax.all_to_all(parts, axis, split_axis=0, concat_axis=0, tiled=True)  30.1 us
    ppermute x4, waiting for transfers between devices, traded(): return lax.ppermute(sent, ('ya', 'yb', 'z1'), moves)  17.9 us
    all_to_all x3, waiting for transfers between devices, exchange(): return lax.all_to_all(parts, axis, split_axis=0, concat_axis=0, tiled=True)  17.9 us
    ppermute x4, starting transfers between devices, traded(): return lax.ppermute(sent, ('ya', 'yb', 'z1'), moves)  17.3 us
    pallas_call x1, Pallas kernels, attention(): pl.pallas_call(attend, out_shape=jax.ShapeDtypeStruct((2 * FAR * NEAR, LI...  3.7 us
  transfers between devices with their start and end apart: 7, of which 5 were waited for; matrix products, arithmetic and copies ran while one was open for 1% of the time, Pallas kernels for 0%

profile of v8, /device:TPU:8, one launch (start us, length us, event | category | flops | bytes accessed | tf_op | source)
XLA Modules:
  0.0 145.4 jit_solution(3090570575486701741)
XLA Ops:
  0.0 3.7 %attend.1 = bf16[24,40,128]{2,1,0:T(8,128)(2,1)} custom-call(s32[4]{0:T(128)} %lengths_ref.1, s32[1]{0:T(128)} %bitcast.1.here_ref, bf16[4,2,4096]{2,1,0:T(2,128)(2,1)} %q_hbm.1, bf16[4,128,512]{2,1,0:T(8,128)(2,1)} %k_hbm.1, bf16[4,128,512]{2,1,0:T(8,128)(2,1)} %v_hbm.1, bf16[4,2,512]{2,1,0:T(2,128)(2,1)} %nk_hbm.1, bf16[4,2,512]{2,1,0:T(2,128)(2,1)} %nv_hbm.1), custom_call_target="tpu_custom_call" | custom-call | flops 100000000 | bytes 1048576 | tf_op jit(solution)/shard_map/attend/pallas_call | solution.py:150
  3.7 18.0 %all-to-all-start = ((bf16[24,40,128]{2,1,0:T(8,128)(2,1)}), bf16[24,40,128]{2,1,0:T(8,128)(2,1)S(1)}, u32[]{:S(2)}, u32[]{:S(2)}) async-start(bf16[24,40,128]{2,1,0:T(8,128)(2,1)} %attend.1), calls=%async_computation | async-start | bytes 491520 | tf_op jit(solution)/shard_map/all_to_all | solution.py:26
  21.9 17.2 %all-to-all-done = bf16[24,40,128]{2,1,0:T(8,128)(2,1)S(1)} async-done(((bf16[24,40,128]{2,1,0:T(8,128)(2,1)}), bf16[24,40,128]{2,1,0:T(8,128)(2,1)S(1)}, u32[]{:S(2)}, u32[]{:S(2)}) %all-to-all-start) | async-done | bytes 245792 | tf_op jit(solution)/shard_map/all_to_all | solution.py:26
  39.9 0.7 reshape.145
  40.7 8.1 %all-to-all-start.1 = ((bf16[64,4,256]{2,1,0:T(4,128)(2,1)}), bf16[64,4,256]{2,1,0:T(4,128)(2,1)S(1)}, u32[]{:S(2)}, u32[]{:S(2)}) async-start(bf16[64,4,256]{2,1,0:T(4,128)(2,1)} %reshape.145), calls=%async_computation.1 | async-start | bytes 262144 | tf_op jit(solution)/shard_map/all_to_all | solution.py:26
  48.9 2.4 %collective-permute-start.1 = (bf16[304,128]{1,0:T(8,128)(2,1)S(1)}, bf16[304,128]{1,0:T(8,128)(2,1)S(1)}, u32[]{:S(2)}, u32[]{:S(2)}) collective-permute-start(bf16[304,128]{1,0:T(8,128)(2,1)S(1)} %get-tuple-element.18), channel_id=1, source_target_pairs={{0,192},{1,240},{2,288},{3,336},{48,0},{49,48},{50,96},{51,144},{9... | collective-permute-start | bytes 233480 | tf_op jit(solution)/shard_map/ppermute | solution.py:52
  51.3 7.2 %collective-permute-start = (bf16[304,128]{1,0:T(8,128)(2,1)S(1)}, bf16[304,128]{1,0:T(8,128)(2,1)S(1)}, u32[]{:S(2)}, u32[]{:S(2)}) collective-permute-start(bf16[304,128]{1,0:T(8,128)(2,1)S(1)} %get-tuple-element.17), channel_id=1, source_target_pairs={{0,0},{1,48},{2,96},{3,144},{48,192},{49,240},{50,288},{51,336},{9... | collective-permute-start | bytes 233480 | tf_op jit(solution)/shard_map/ppermute | solution.py:52
  58.4 0.7 all-to-all-done.1
  59.5 0.2 fusion.1
  59.7 0.2 copy.101
  60.1 8.1 %collective-permute-done = bf16[304,128]{1,0:T(8,128)(2,1)S(1)} collective-permute-done((bf16[304,128]{1,0:T(8,128)(2,1)S(1)}, bf16[304,128]{1,0:T(8,128)(2,1)S(1)}, u32[]{:S(2)}, u32[]{:S(2)}) %collective-permute-start) | collective-permute-done | bytes 77856 | tf_op jit(solution)/shard_map/ppermute | solution.py:52
  68.1 0.2 fusion
  68.6 11.4 %all_to_all.30 = bf16[16,16,306]{2,1,0:T(8,128)(2,1)S(1)} all-to-all(bf16[16,16,306]{2,1,0:T(8,128)(2,1)S(1)} %pad_maximum_fusion), channel_id=1, replica_groups=mesh['xl'=2,'ya'=4,'yb'=2,'c'=2,'xh'=2,'z2'=3,'z1'=4] {'xl','c','z1'}, dimensions={0} | all-to-all | bytes 313344 | tf_op jit(solution)/shard_map/all_to_all | solution.py:26
  80.4 0.7 broadcast_in_dim.7
  81.1 3.9 %all-to-all-start.3 = ((bf16[16,16,304]{2,1,0:T(8,128)(2,1)}), bf16[16,16,304]{2,1,0:T(8,128)(2,1)S(1)}, u32[]{:S(2)}, u32[]{:S(2)}) async-start(bf16[16,16,304]{2,1,0:T(8,128)(2,1)} %broadcast_in_dim.7), calls=%async_computation.3 | async-start | bytes 393216 | tf_op jit(solution)/shard_map/all_to_all | solution.py:26
  85.1 2.0 %collective-permute-start.3 = (bf16[304,128]{1,0:T(8,128)(2,1)S(1)}, bf16[304,128]{1,0:T(8,128)(2,1)S(1)}, u32[]{:S(2)}, u32[]{:S(2)}) collective-permute-start(bf16[304,128]{1,0:T(8,128)(2,1)S(1)} %get-tuple-element.16), channel_id=1, source_target_pairs={{0,192},{1,240},{2,288},{3,336},{48,0},{49,48},{50,96},{51,144},{9... | collective-permute-start | bytes 233480 | tf_op jit(solution)/shard_map/ppermute | solution.py:52
  87.1 5.8 %collective-permute-start.2 = (bf16[304,128]{1,0:T(8,128)(2,1)S(1)}, bf16[304,128]{1,0:T(8,128)(2,1)S(1)}, u32[]{:S(2)}, u32[]{:S(2)}) collective-permute-start(bf16[304,128]{1,0:T(8,128)(2,1)S(1)} %get-tuple-element.15), channel_id=1, source_target_pairs={{0,0},{1,48},{2,96},{3,144},{48,192},{49,240},{50,288},{51,336},{9... | collective-permute-start | bytes 233480 | tf_op jit(solution)/shard_map/ppermute | solution.py:52
  93.0 0.2 collective-permute-done.3
  93.2 0.2 convolution_convert_fusion
  93.4 9.6 %collective-permute-done.2 = bf16[304,128]{1,0:T(8,128)(2,1)S(1)} collective-permute-done((bf16[304,128]{1,0:T(8,128)(2,1)S(1)}, bf16[304,128]{1,0:T(8,128)(2,1)S(1)}, u32[]{:S(2)}, u32[]{:S(2)}) %collective-permute-start.2) | collective-permute-done | bytes 77856 | tf_op jit(solution)/shard_map/ppermute | solution.py:52
  103.0 0.2 convolution_convert_fusion.1
  103.4 20.9 %all_to_all.31 = bf16[64,4,256]{2,1,0:T(4,128)(2,1)S(1)} all-to-all(bf16[64,4,256]{2,1,0:T(4,128)(2,1)S(1)} %reshape.152), channel_id=1, replica_groups=mesh['xl'=2,'ya'=4,'yb'=2,'c'=2,'xh'=2,'z2'=3,'z1'=4] {'xl','ya','yb','c..., dimensions={0} | all-to-all | bytes 262144 | tf_op jit(solution)/shard_map/all_to_all | solution.py:26
  124.8 19.8 %all_to_all.32 = bf16[24,4,1024]{2,1,0:T(4,128)(2,1)S(1)} all-to-all(bf16[24,4,1024]{2,1,0:T(4,128)(2,1)S(1)} %broadcast_in_dim.8), channel_id=1, replica_groups=mesh['xl'=2,'ya'=4,'yb'=2,'c'=2,'xh'=2,'z2'=3,'z1'=4] {'xh','z2','z1'}, dimensions={0} | all-to-all | bytes 393216 | tf_op jit(solution)/shard_map/all_to_all | solution.py:26
  144.8 0.6 reshape.155
  (64 shorter events, 2.8 us)
Async XLA Ops:
  0.0 21.8 %copy-start = (f32[4096]{0:T(1024)S(1)}, f32[4096]{0:T(1024)}, u32[]{:S(2)}) copy-start(f32[4096]{0:T(1024)} %param.17) | copy-start | bytes 49156
  3.7 18.0 %copy-start.3 = (bf16[4,2,4096]{2,1,0:T(2,128)(2,1)S(1)}, bf16[4,2,4096]{2,1,0:T(2,128)(2,1)}, u32[]{:S(2)}) copy-start(bf16[4,2,4096]{2,1,0:T(2,128)(2,1)} %param.16) | copy-start | bytes 196612
  3.7 35.4 %all-to-all-start = ((bf16[24,40,128]{2,1,0:T(8,128)(2,1)}), bf16[24,40,128]{2,1,0:T(8,128)(2,1)S(1)}, u32[]{:S(2)}, u32[]{:S(2)}) async-start(bf16[24,40,128]{2,1,0:T(8,128)(2,1)} %attend.1), calls=%async_computation | async-start | bytes 491520 | tf_op jit(solution)/shard_map/all_to_all | solution.py:26
  39.9 8.9 %copy-start.1 = (f32[128,600]{0,1:T(8,128)S(1)}, f32[128,600]{0,1:T(8,128)}, u32[]{:S(2)}) copy-start(f32[128,600]{0,1:T(8,128)} %param.18) | copy-start | bytes 921604
  40.7 18.5 %all-to-all-start.1 = ((bf16[64,4,256]{2,1,0:T(4,128)(2,1)}), bf16[64,4,256]{2,1,0:T(4,128)(2,1)S(1)}, u32[]{:S(2)}, u32[]{:S(2)}) async-start(bf16[64,4,256]{2,1,0:T(4,128)(2,1)} %reshape.145), calls=%async_computation.1 | async-start | bytes 262144 | tf_op jit(solution)/shard_map/all_to_all | solution.py:26
  48.9 10.6 %collective-permute-start.1 = (bf16[304,128]{1,0:T(8,128)(2,1)S(1)}, bf16[304,128]{1,0:T(8,128)(2,1)S(1)}, u32[]{:S(2)}, u32[]{:S(2)}) collective-permute-start(bf16[304,128]{1,0:T(8,128)(2,1)S(1)} %get-tuple-element.18), channel_id=1, source_target_pairs={{0,192},{1,240},{2,288},{3,336},{48,0},{49,48},{50,96},{51,144},{9... | collective-permute-start | bytes 233480 | tf_op jit(solution)/shard_map/ppermute | solution.py:52
  51.3 16.9 %collective-permute-start = (bf16[304,128]{1,0:T(8,128)(2,1)S(1)}, bf16[304,128]{1,0:T(8,128)(2,1)S(1)}, u32[]{:S(2)}, u32[]{:S(2)}) collective-permute-start(bf16[304,128]{1,0:T(8,128)(2,1)S(1)} %get-tuple-element.17), channel_id=1, source_target_pairs={{0,0},{1,48},{2,96},{3,144},{48,192},{49,240},{50,288},{51,336},{9... | collective-permute-start | bytes 233480 | tf_op jit(solution)/shard_map/ppermute | solution.py:52
  80.4 4.7 %copy-start.2 = (f32[128,600]{0,1:T(8,128)S(1)}, f32[128,600]{0,1:T(8,128)}, u32[]{:S(2)}) copy-start(f32[128,600]{0,1:T(8,128)} %param.19) | copy-start | bytes 921604
  81.1 12.1 %all-to-all-start.3 = ((bf16[16,16,304]{2,1,0:T(8,128)(2,1)}), bf16[16,16,304]{2,1,0:T(8,128)(2,1)S(1)}, u32[]{:S(2)}, u32[]{:S(2)}) async-start(bf16[16,16,304]{2,1,0:T(8,128)(2,1)} %broadcast_in_dim.7), calls=%async_computation.3 | async-start | bytes 393216 | tf_op jit(solution)/shard_map/all_to_all | solution.py:26
  85.1 8.0 %collective-permute-start.3 = (bf16[304,128]{1,0:T(8,128)(2,1)S(1)}, bf16[304,128]{1,0:T(8,128)(2,1)S(1)}, u32[]{:S(2)}, u32[]{:S(2)}) collective-permute-start(bf16[304,128]{1,0:T(8,128)(2,1)S(1)} %get-tuple-element.16), channel_id=1, source_target_pairs={{0,192},{1,240},{2,288},{3,336},{48,0},{49,48},{50,96},{51,144},{9... | collective-permute-start | bytes 233480 | tf_op jit(solution)/shard_map/ppermute | solution.py:52
  87.1 15.9 %collective-permute-start.2 = (bf16[304,128]{1,0:T(8,128)(2,1)S(1)}, bf16[304,128]{1,0:T(8,128)(2,1)S(1)}, u32[]{:S(2)}, u32[]{:S(2)}) collective-permute-start(bf16[304,128]{1,0:T(8,128)(2,1)S(1)} %get-tuple-element.15), channel_id=1, source_target_pairs={{0,0},{1,48},{2,96},{3,144},{48,192},{49,240},{50,288},{51,336},{9... | collective-permute-start | bytes 233480 | tf_op jit(solution)/shard_map/ppermute | solution.py:52

commit v9 on v5

--- a/solution.py
+++ b/solution.py
@@ -48,9 +48,9 @@
     for row in range(NEAR):
         for pair in range(2):
             for deep in range(NEAR):
-                target = (pair ^ over) * 2 + (deep // 2 ^ under)
-                moves.append(((row * 2 + pair) * NEAR + deep, (target * 2 + deep % 2) * NEAR + row))
-    at = (lax.axis_index("yb") ^ over) * 2 + (lax.axis_index("z1") // 2 ^ under)
+                target = (deep // 2 ^ under) * 2 + deep % 2
+                moves.append(((row * 2 + pair) * NEAR + deep, (target * 2 + (pair ^ over)) * NEAR + row))
+    at = (lax.axis_index("z1") // 2 ^ under) * 2 + (lax.axis_index("yb") ^ over)
     sent = lax.dynamic_index_in_dim(pieces, at, 1, False)
     return lax.ppermute(sent, ("ya", "yb", "z1"), moves)
 
@@ -193,7 +193,7 @@
     mine = lax.dynamic_index_in_dim(lax.dynamic_index_in_dim(mine, half, 0, False), deep, 2, False).astype(jnp.float32)
     gain = lax.dynamic_index_in_dim(norm_gain.reshape(2, near, 4, HD), deep, 1, False)
     own_gain = gain.reshape(2, 2, 2, HD)[lax.axis_index("xl"), :, lax.axis_index("c")]
-    own_gain = jnp.where(lax.axis_index("ya") < NEAR // 2, own_gain, own_gain[::-1]).reshape(2 * HD)
+    own_gain = jnp.where(lax.axis_index("yb") == 0, own_gain, own_gain[::-1]).reshape(2 * HD)
     first = (lax.axis_index("z2") == 0).astype(jnp.float32)
     pieces = exchange(sent, TP)
 
@@ -208,7 +208,7 @@
     gained = (summed * gain).astype(jnp.bfloat16).reshape(share, 2, 2, 2, HD)
     gained = jnp.transpose(gained, (1, 3, 0, 2, 4))
     ordered = jnp.stack([gained, gained[:, :, :, ::-1]], axis=1)
-    ordered = jnp.broadcast_to(ordered[:, :, None, :, None], (2, 2, near, 2, halves, share, 2, HD))
+    ordered = jnp.broadcast_to(ordered[:, None, :, :, None], (2, near, 2, 2, halves, share, 2, HD))
     ordered = ordered.reshape(groups * halves, share, 2 * HD)
     kept = summed * first
     ordered, kept, own_gain = lax.optimization_barrier((ordered, kept, own_gain))
@@ -237,7 +237,7 @@
         [jnp.dot(hidden, w, preferred_element_type=jnp.float32).astype(jnp.bfloat16) for w in down_weights], axis=-1
     )
     partial = exchange(terms.reshape(groups * halves, share, 2 * HD), WIDE)
-    partial = partial.reshape(2, 2, near, 2, halves, share, 2, HD).astype(jnp.float32).sum(axis=(2, 4))
+    partial = partial.reshape(2, near, 2, 2, halves, share, 2, HD).astype(jnp.float32).sum(axis=(1, 4))
     mlp = partial[:, 0] + partial[:, 1, :, :, ::-1]
     mlp = jnp.transpose(mlp, (2, 0, 3, 1, 4)).reshape(share, 2, 4, HD)
     mixed = mlp + kept

time: 146 us -> 145 us (level)
  blocking collectives: 65 us -> 69.5 us
  starting transfers between devices: 44.8 us -> 40.7 us
  waiting for transfers between devices: 26.1 us -> 24.4 us
    all_to_all x4, blocking collectives: 65 us -> 69.5 us  [exchange(): return lax.all_to_all(parts, axis, split_axis=0, concat_axis=0, tiled=True)]
    ppermute x4, starting transfers between devices: 18.9 us -> 14.7 us  [traded(): return lax.ppermute(sent, ('ya', 'yb', 'z1'), moves)]
    ppermute x4, waiting for transfers between devices: 9.61 us -> 7.94 us  [traded(): return lax.ppermute(sent, ('ya', 'yb', 'z1'), moves)]
where the time goes in v9:
time: 145 us; the launch traced here: 144 us
  blocking collectives  69.5 us (48%)
  starting transfers between devices  40.7 us (28%)
  waiting for transfers between devices  24.4 us (17%)
  Pallas kernels  3.7 us (3%)
  local copies, waits for them, and re-layouts  3.5 us (2%)
    all_to_all x4, blocking collectives, exchange(): return lax.all_to_all(parts, axis, split_axis=0, concat_axis=0, tiled=True)  69.5 us
    all_to_all x2, starting transfers between devices, exchange(): return lax.all_to_all(parts, axis, split_axis=0, concat_axis=0, tiled=True)  26 us
    all_to_all x2, waiting for transfers between devices, exchange(): return lax.all_to_all(parts, axis, split_axis=0, concat_axis=0, tiled=True)  16.5 us
    ppermute x4, starting transfers between devices, traded(): return lax.ppermute(sent, ('ya', 'yb', 'z1'), moves)  14.7 us
    ppermute x4, waiting for transfers between devices, traded(): return lax.ppermute(sent, ('ya', 'yb', 'z1'), moves)  7.94 us
    pallas_call x1, Pallas kernels, attention(): pl.pallas_call(attend, out_shape=jax.ShapeDtypeStruct((2 * FAR * NEAR, LI...  3.7 us
  transfers between devices with their start and end apart: 6, of which 3 were waited for; matrix products, arithmetic and copies ran while one was open for 0% of the time, Pallas kernels for 0%

profile of v9, /device:TPU:8, one launch (start us, length us, event | category | flops | bytes accessed | tf_op | source)
XLA Modules:
  0.0 144.4 jit_solution(5489745523642071455)
XLA Ops:
  0.0 3.7 %attend.1 = bf16[24,40,128]{2,1,0:T(8,128)(2,1)} custom-call(s32[4]{0:T(128)} %lengths_ref.1, s32[1]{0:T(128)} %bitcast.1.here_ref, bf16[4,2,4096]{2,1,0:T(2,128)(2,1)} %q_hbm.1, bf16[4,128,512]{2,1,0:T(8,128)(2,1)} %k_hbm.1, bf16[4,128,512]{2,1,0:T(8,128)(2,1)} %v_hbm.1, bf16[4,2,512]{2,1,0:T(2,128)(2,1)} %nk_hbm.1, bf16[4,2,512]{2,1,0:T(2,128)(2,1)} %nv_hbm.1), custom_call_target="tpu_custom_call" | custom-call | flops 100000000 | bytes 1048576 | tf_op jit(solution)/shard_map/attend/pallas_call | solution.py:153
  3.7 17.8 %all-to-all-start = ((bf16[24,40,128]{2,1,0:T(8,128)(2,1)}), bf16[24,40,128]{2,1,0:T(8,128)(2,1)S(1)}, u32[]{:S(2)}, u32[]{:S(2)}) async-start(bf16[24,40,128]{2,1,0:T(8,128)(2,1)} %attend.1), calls=%async_computation | async-start | bytes 491520 | tf_op jit(solution)/shard_map/all_to_all | solution.py:27
  21.7 0.7 copy-done.3
  22.5 16.5 %all-to-all-done = bf16[24,40,128]{2,1,0:T(8,128)(2,1)S(1)} async-done(((bf16[24,40,128]{2,1,0:T(8,128)(2,1)}), bf16[24,40,128]{2,1,0:T(8,128)(2,1)S(1)}, u32[]{:S(2)}, u32[]{:S(2)}) %all-to-all-start) | async-done | bytes 245792 | tf_op jit(solution)/shard_map/all_to_all | solution.py:27
  39.3 0.2 multiply_reduce_fusion
  39.8 0.7 reshape.139
  40.5 8.1 %all-to-all-start.1 = ((bf16[64,4,256]{2,1,0:T(4,128)(2,1)}), bf16[64,4,256]{2,1,0:T(4,128)(2,1)S(1)}, u32[]{:S(2)}, u32[]{:S(2)}) async-start(bf16[64,4,256]{2,1,0:T(4,128)(2,1)} %reshape.139), calls=%async_computation.1 | async-start | bytes 262144 | tf_op jit(solution)/shard_map/all_to_all | solution.py:27
  48.9 6.4 %collective-permute-start.3 = (bf16[2,152,128]{2,1,0:T(8,128)(2,1)S(1)}, bf16[2,152,128]{2,1,0:T(8,128)(2,1)S(1)}, u32[]{:S(2)}, u32[]{:S(2)}) collective-permute-start(bf16[2,152,128]{2,1,0:T(8,128)(2,1)S(1)} %get-tuple-element.23), channel_id=1, source_target_pairs={{0,240},{1,336},{2,48},{3,144},{48,192},{49,288},{50,0},{51,96},{9... | collective-permute-start | bytes 233480 | tf_op jit(solution)/shard_map/ppermute | solution.py:55
  55.3 2.5 %collective-permute-start.2 = (bf16[2,152,128]{2,1,0:T(8,128)(2,1)S(1)}, bf16[2,152,128]{2,1,0:T(8,128)(2,1)S(1)}, u32[]{:S(2)}, u32[]{:S(2)}) collective-permute-start(bf16[2,152,128]{2,1,0:T(8,128)(2,1)S(1)} %get-tuple-element.24), channel_id=1, source_target_pairs={{0,48},{1,144},{2,240},{3,336},{48,0},{49,96},{50,192},{51,288},{9... | collective-permute-start | bytes 233480 | tf_op jit(solution)/shard_map/ppermute | solution.py:55
  57.7 5.2 %collective-permute-start.1 = (bf16[2,152,128]{2,1,0:T(8,128)(2,1)S(1)}, bf16[2,152,128]{2,1,0:T(8,128)(2,1)S(1)}, u32[]{:S(2)}, u32[]{:S(2)}) collective-permute-start(bf16[2,152,128]{2,1,0:T(8,128)(2,1)S(1)} %get-tuple-element.25), channel_id=1, source_target_pairs={{0,192},{1,288},{2,0},{3,96},{48,240},{49,336},{50,48},{51,144},{9... | collective-permute-start | bytes 233480 | tf_op jit(solution)/shard_map/ppermute | solution.py:55
  62.9 0.7 collective-permute-start
  63.9 6.8 %collective-permute-done.3 = bf16[2,152,128]{2,1,0:T(8,128)(2,1)S(1)} collective-permute-done((bf16[2,152,128]{2,1,0:T(8,128)(2,1)S(1)}, bf16[2,152,128]{2,1,0:T(8,128)(2,1)S(1)}, u32[]{:S(2)}, u32[]{:S(2)}) %collective-permute-start.3) | collective-permute-done | bytes 77856 | tf_op jit(solution)/shard_map/ppermute | solution.py:55
  70.8 1.1 collective-permute-done.1
  72.0 0.2 fusion.4
  72.2 0.2 fusion
  72.4 0.2 copy.83
  72.6 19.3 %all_to_all.30 = bf16[16,16,306]{2,1,0:T(8,128)(2,1)S(1)} all-to-all(bf16[16,16,306]{2,1,0:T(8,128)(2,1)S(1)} %bitcast.75), channel_id=1, replica_groups=mesh['xl'=2,'ya'=4,'yb'=2,'c'=2,'xh'=2,'z2'=3,'z1'=4] {'xl','c','z1'}, dimensions={0} | all-to-all | bytes 313344 | tf_op jit(solution)/shard_map/all_to_all | solution.py:27
  91.9 0.2 fusion.25
  92.2 11.8 %all_to_all.31 = bf16[16,16,304]{2,1,0:T(8,128)(2,1)S(1)} all-to-all(bf16[16,16,304]{2,1,0:T(8,128)(2,1)S(1)} %broadcast_in_dim.7), channel_id=1, replica_groups=mesh['xl'=2,'ya'=4,'yb'=2,'c'=2,'xh'=2,'z2'=3,'z1'=4] {'xl','c','z1'}, dimensions={0} | all-to-all | bytes 311296 | tf_op jit(solution)/shard_map/all_to_all | solution.py:27
  104.0 0.3 convolution_convert_fusion
  104.2 0.3 convolution_convert_fusion.1
  104.7 17.7 %all_to_all.32 = bf16[64,4,256]{2,1,0:T(4,128)(2,1)S(1)} all-to-all(bf16[64,4,256]{2,1,0:T(4,128)(2,1)S(1)} %reshape.146), channel_id=1, replica_groups=mesh['xl'=2,'ya'=4,'yb'=2,'c'=2,'xh'=2,'z2'=3,'z1'=4] {'xl','ya','yb','c..., dimensions={0} | all-to-all | bytes 262144 | tf_op jit(solution)/shard_map/all_to_all | solution.py:27
  122.8 20.7 %all_to_all.33 = bf16[24,4,1024]{2,1,0:T(4,128)(2,1)S(1)} all-to-all(bf16[24,4,1024]{2,1,0:T(4,128)(2,1)S(1)} %broadcast_in_dim.8), channel_id=1, replica_groups=mesh['xl'=2,'ya'=4,'yb'=2,'c'=2,'xh'=2,'z2'=3,'z1'=4] {'xh','z2','z1'}, dimensions={0} | all-to-all | bytes 393216 | tf_op jit(solution)/shard_map/all_to_all | solution.py:27
  143.7 0.6 reshape.149
  (63 shorter events, 2.1 us)
Async XLA Ops:
  0.0 21.6 %copy-start = (f32[4096]{0:T(1024)S(1)}, f32[4096]{0:T(1024)}, u32[]{:S(2)}) copy-start(f32[4096]{0:T(1024)} %param.17) | copy-start | bytes 49156
  3.7 35.3 %all-to-all-start = ((bf16[24,40,128]{2,1,0:T(8,128)(2,1)}), bf16[24,40,128]{2,1,0:T(8,128)(2,1)S(1)}, u32[]{:S(2)}, u32[]{:S(2)}) async-start(bf16[24,40,128]{2,1,0:T(8,128)(2,1)} %attend.1), calls=%async_computation | async-start | bytes 491520 | tf_op jit(solution)/shard_map/all_to_all | solution.py:27
  21.6 0.8 copy-start.3
  39.7 9.0 %copy-start.1 = (f32[128,600]{0,1:T(8,128)S(1)}, f32[128,600]{0,1:T(8,128)}, u32[]{:S(2)}) copy-start(f32[128,600]{0,1:T(8,128)} %param.19) | copy-start | bytes 921604
  39.7 9.0 %copy-start.2 = (f32[128,600]{0,1:T(8,128)S(1)}, f32[128,600]{0,1:T(8,128)}, u32[]{:S(2)}) copy-start(f32[128,600]{0,1:T(8,128)} %param.18) | copy-start | bytes 921604
  40.5 23.0 %all-to-all-start.1 = ((bf16[64,4,256]{2,1,0:T(4,128)(2,1)}), bf16[64,4,256]{2,1,0:T(4,128)(2,1)S(1)}, u32[]{:S(2)}, u32[]{:S(2)}) async-start(bf16[64,4,256]{2,1,0:T(4,128)(2,1)} %reshape.139), calls=%async_computation.1 | async-start | bytes 262144 | tf_op jit(solution)/shard_map/all_to_all | solution.py:27
  48.9 21.9 %collective-permute-start.3 = (bf16[2,152,128]{2,1,0:T(8,128)(2,1)S(1)}, bf16[2,152,128]{2,1,0:T(8,128)(2,1)S(1)}, u32[]{:S(2)}, u32[]{:S(2)}) collective-permute-start(bf16[2,152,128]{2,1,0:T(8,128)(2,1)S(1)} %get-tuple-element.23), channel_id=1, source_target_pairs={{0,240},{1,336},{2,48},{3,144},{48,192},{49,288},{50,0},{51,96},{9... | collective-permute-start | bytes 233480 | tf_op jit(solution)/shard_map/ppermute | solution.py:55
  55.3 15.5 %collective-permute-start.2 = (bf16[2,152,128]{2,1,0:T(8,128)(2,1)S(1)}, bf16[2,152,128]{2,1,0:T(8,128)(2,1)S(1)}, u32[]{:S(2)}, u32[]{:S(2)}) collective-permute-start(bf16[2,152,128]{2,1,0:T(8,128)(2,1)S(1)} %get-tuple-element.24), channel_id=1, source_target_pairs={{0,48},{1,144},{2,240},{3,336},{48,0},{49,96},{50,192},{51,288},{9... | collective-permute-start | bytes 233480 | tf_op jit(solution)/shard_map/ppermute | solution.py:55
  57.7 14.1 %collective-permute-start.1 = (bf16[2,152,128]{2,1,0:T(8,128)(2,1)S(1)}, bf16[2,152,128]{2,1,0:T(8,128)(2,1)S(1)}, u32[]{:S(2)}, u32[]{:S(2)}) collective-permute-start(bf16[2,152,128]{2,1,0:T(8,128)(2,1)S(1)} %get-tuple-element.25), channel_id=1, source_target_pairs={{0,192},{1,288},{2,0},{3,96},{48,240},{49,336},{50,48},{51,144},{9... | collective-permute-start | bytes 233480 | tf_op jit(solution)/shard_map/ppermute | solution.py:55
  62.9 9.0 %collective-permute-start = (bf16[2,152,128]{2,1,0:T(8,128)(2,1)S(1)}, bf16[2,152,128]{2,1,0:T(8,128)(2,1)S(1)}, u32[]{:S(2)}, u32[]{:S(2)}) collective-permute-start(bf16[2,152,128]{2,1,0:T(8,128)(2,1)S(1)} %get-tuple-element.26), channel_id=1, source_target_pairs={{0,0},{1,96},{2,192},{3,288},{48,48},{49,144},{50,240},{51,336},{9... | collective-permute-start | bytes 233480 | tf_op jit(solution)/shard_map/ppermute | solution.py:55

commit v10 on v7

--- a/solution.py
+++ b/solution.py
@@ -14,9 +14,9 @@
 NEAR = 4
 FAR = 3
 LINES = 32
-GRP = ("xl", "ya", "yb", "c")
+GRP = ("xl", "yb", "ya", "c")
 TP = ("xh", "z2", "z1")
-WIDE = ("xl", "ya", "yb", "c", "xh")
+WIDE = ("xl", "yb", "ya", "c", "xh")
 DEEP = ("xl", "c", "z1")
 HALF = 304
 masked_score = -1e30
@@ -47,9 +47,9 @@
         for pair in range(2):
             for deep in range(NEAR):
                 target = (pair ^ turn) * NEAR + deep
-                moves.append(((row * 2 + pair) * NEAR + deep, target * NEAR + row))
+                moves.append(((pair * NEAR + row) * NEAR + deep, target * NEAR + row))
     sent = lax.dynamic_index_in_dim(halves, lax.axis_index("yb") ^ turn, 1, False)
-    return lax.ppermute(sent, ("ya", "yb", "z1"), moves)
+    return lax.ppermute(sent, ("yb", "ya", "z1"), moves)
 
 
 def attend(lengths_ref, here_ref, q_hbm, k_hbm, v_hbm, nk_hbm, nv_hbm, out_ref, q, k, v, nk, nv, small, large):
@@ -129,9 +129,9 @@
             def lines_to(array):
                 parts = []
                 for r in range(half * rows // 2, (half + 1) * rows // 2):
-                    for side in range(2):
-                        at = (r * KVH + side * 2 + near // 2) * block + near % 2 * 8
-                        parts.append(array[at : at + 8])
+                    for j in range(KVH):
+                        at = (r * KVH + j) * block + near * 4
+                        parts.append(array[at : at + 4])
                 return jnp.concatenate(parts, axis=0)
 
             lead = lines_to(high)
@@ -187,11 +187,12 @@
     sent = attention(queries, cache_keys, cache_values, new_keys, new_values, lengths, here)
 
     half, deep = lax.axis_index("xh"), lax.axis_index("z1")
-    mine = residual.reshape(halves, share, 2, near, 4, HD)
-    mine = lax.dynamic_index_in_dim(lax.dynamic_index_in_dim(mine, half, 0, False), deep, 2, False).astype(jnp.float32)
-    gain = lax.dynamic_index_in_dim(norm_gain.reshape(2, near, 4, HD), deep, 1, False)
+    mine = residual.reshape(halves, share, 2, 2, near, 2, HD)
+    mine = lax.dynamic_index_in_dim(lax.dynamic_index_in_dim(mine, half, 0, False), deep, 3, False).astype(jnp.float32)
+    mine = mine.reshape(share, 2, 4, HD)
+    gain = lax.dynamic_index_in_dim(norm_gain.reshape(2, 2, near, 2, HD), deep, 2, False).reshape(2, 4, HD)
     own_gain = gain.reshape(2, 2, 2, HD)[lax.axis_index("xl"), :, lax.axis_index("c")]
-    own_gain = jnp.where(lax.axis_index("ya") < NEAR // 2, own_gain, own_gain[::-1]).reshape(2 * HD)
+    own_gain = jnp.where(lax.axis_index("yb") == 0, own_gain, own_gain[::-1]).reshape(2 * HD)
     first = (lax.axis_index("z2") == 0).astype(jnp.float32)
     pieces = exchange(sent, TP)
 
@@ -236,13 +237,13 @@
     mlp = jnp.transpose(mlp, (2, 0, 3, 1, 4)).reshape(share, 2, 4, HD)
     mixed = mlp + kept
     mixed = copies(mixed.astype(jnp.bfloat16).reshape(share, 8 * HD), TP)
-    mixed = mixed.reshape(halves, far, near, share, 2, 4, HD).astype(jnp.float32).sum(axis=1)
-    mixed = jnp.transpose(mixed, (0, 2, 3, 1, 4, 5))
+    mixed = mixed.reshape(halves, far, near, share, 2, 2, 2, HD).astype(jnp.float32).sum(axis=1)
+    mixed = jnp.transpose(mixed, (0, 2, 3, 4, 1, 5, 6))
     return mixed.astype(jnp.bfloat16).reshape(rows, steps, features)
 
 
 def solution(mesh):
-    fine = Mesh(mesh.devices.reshape(2, 4, 2, 2, 2, 3, 4), ("xl", "ya", "yb", "c", "xh", "z2", "z1"))
+    fine = Mesh(mesh.devices.reshape(2, 2, 4, 2, 2, 3, 4), ("xl", "yb", "ya", "c", "xh", "z2", "z1"))
     return jax.shard_map(
         layer,
         mesh=fine,

time: 145 us -> 142 us (0.979)
  waiting for transfers between devices: 37.8 us -> 35.3 us
  starting transfers between devices: 34.3 us -> 35.9 us
    ppermute x2, waiting for transfers between devices: 19.5 us -> 17.7 us  [traded(): return lax.ppermute(sent, ('yb', 'ya', 'z1'), moves)]
    ppermute x2, starting transfers between devices: 8.31 us -> 9.76 us  [traded(): return lax.ppermute(sent, ('yb', 'ya', 'z1'), moves)]
where the time goes in v10:
time: 142 us
  blocking collectives  61.3 us (43%)
  starting transfers between devices  35.9 us (25%)
  waiting for transfers between devices  35.3 us (25%)
  Pallas kernels  3.7 us (3%)
  local copies, waits for them, and re-layouts  3.04 us (2%)
    all_to_all x4, blocking collectives, exchange(): return lax.all_to_all(parts, axis, split_axis=0, concat_axis=0, tiled=True)  61.3 us
    all_to_all x2, starting transfers between devices, exchange(): return lax.all_to_all(parts, axis, split_axis=0, concat_axis=0, tiled=True)  26.1 us
    ppermute x2, waiting for transfers between devices, traded(): return lax.ppermute(sent, ('yb', 'ya', 'z1'), moves)  17.7 us
    all_to_all x2, waiting for transfers between devices, exchange(): return lax.all_to_all(parts, axis, split_axis=0, concat_axis=0, tiled=True)  17.6 us
    ppermute x2, starting transfers between devices, traded(): return lax.ppermute(sent, ('yb', 'ya', 'z1'), moves)  9.76 us
    pallas_call x1, Pallas kernels, attention(): pl.pallas_call(attend, out_shape=jax.ShapeDtypeStruct((2 * FAR * NEAR, LI...  3.7 us
  transfers between devices with their start and end apart: 4, of which 3 were waited for; matrix products, arithmetic and copies ran while one was open for 1% of the time, Pallas kernels for 0%

profile of v10, /device:TPU:8, one launch (start us, length us, event | category | flops | bytes accessed | tf_op | source)
XLA Modules:
  0.0 141.8 jit_solution(8520841979857661092)
XLA Ops:
  0.0 3.7 %attend.1 = bf16[24,40,128]{2,1,0:T(8,128)(2,1)} custom-call(s32[4]{0:T(128)} %lengths_ref.1, s32[1]{0:T(128)} %bitcast.1.here_ref, bf16[4,2,4096]{2,1,0:T(2,128)(2,1)} %q_hbm.1, bf16[4,128,512]{2,1,0:T(8,128)(2,1)} %k_hbm.1, bf16[4,128,512]{2,1,0:T(8,128)(2,1)} %v_hbm.1, bf16[4,2,512]{2,1,0:T(2,128)(2,1)} %nk_hbm.1, bf16[4,2,512]{2,1,0:T(2,128)(2,1)} %nv_hbm.1), custom_call_target="tpu_custom_call" | custom-call | flops 100000000 | bytes 1048576 | tf_op jit(solution)/shard_map/attend/pallas_call | solution.py:150
  3.7 18.0 %all-to-all-start = ((bf16[24,40,128]{2,1,0:T(8,128)(2,1)}), bf16[24,40,128]{2,1,0:T(8,128)(2,1)S(1)}, u32[]{:S(2)}, u32[]{:S(2)}) async-start(bf16[24,40,128]{2,1,0:T(8,128)(2,1)} %attend.1), calls=%async_computation | async-start | bytes 491520 | tf_op jit(solution)/shard_map/all_to_all | solution.py:26
  21.9 17.2 %all-to-all-done = bf16[24,40,128]{2,1,0:T(8,128)(2,1)S(1)} async-done(((bf16[24,40,128]{2,1,0:T(8,128)(2,1)}), bf16[24,40,128]{2,1,0:T(8,128)(2,1)S(1)}, u32[]{:S(2)}, u32[]{:S(2)}) %all-to-all-start) | async-done | bytes 245792 | tf_op jit(solution)/shard_map/all_to_all | solution.py:26
  39.4 0.2 multiply_reduce_fusion
  39.9 0.7 reshape.144
  40.6 8.1 %all-to-all-start.1 = ((bf16[64,4,256]{2,1,0:T(4,128)(2,1)}), bf16[64,4,256]{2,1,0:T(4,128)(2,1)S(1)}, u32[]{:S(2)}, u32[]{:S(2)}) async-start(bf16[64,4,256]{2,1,0:T(4,128)(2,1)} %reshape.144), calls=%async_computation.1 | async-start | bytes 262144 | tf_op jit(solution)/shard_map/all_to_all | solution.py:26
  49.0 2.0 %collective-permute-start = (bf16[2,304,128]{2,1,0:T(8,128)(2,1)S(1)}, bf16[2,304,128]{2,1,0:T(8,128)(2,1)S(1)}, u32[]{:S(2)}, u32[]{:S(2)}) collective-permute-start(bf16[2,304,128]{2,1,0:T(8,128)(2,1)S(1)} %get-tuple-element.15), channel_id=1, source_target_pairs={{0,0},{1,48},{2,96},{3,144},{192,192},{193,240},{194,288},{195,336... | collective-permute-start | bytes 466952 | tf_op jit(solution)/shard_map/ppermute | solution.py:52
  51.0 7.7 %collective-permute-start.1 = (bf16[2,304,128]{2,1,0:T(8,128)(2,1)S(1)}, bf16[2,304,128]{2,1,0:T(8,128)(2,1)S(1)}, u32[]{:S(2)}, u32[]{:S(2)}) collective-permute-start(bf16[2,304,128]{2,1,0:T(8,128)(2,1)S(1)} %get-tuple-element.16), channel_id=1, source_target_pairs={{0,192},{1,240},{2,288},{3,336},{192,0},{193,48},{194,96},{195,144... | collective-permute-start | bytes 466952 | tf_op jit(solution)/shard_map/ppermute | solution.py:52
  58.7 0.4 all-to-all-done.1
  59.4 0.2 copy.101
  59.6 0.2 copy.100
  59.8 17.7 %collective-permute-done.1 = bf16[2,304,128]{2,1,0:T(8,128)(2,1)S(1)} collective-permute-done((bf16[2,304,128]{2,1,0:T(8,128)(2,1)S(1)}, bf16[2,304,128]{2,1,0:T(8,128)(2,1)S(1)}, u32[]{:S(2)}, u32[]{:S(2)}) %collective-permute-start.1) | collective-permute-done | bytes 155680 | tf_op jit(solution)/shard_map/ppermute | solution.py:52
  77.6 0.2 fusion.4
  77.8 0.2 fusion
  78.0 0.2 copy.97
  78.3 10.9 %all_to_all.30 = bf16[16,16,306]{2,1,0:T(8,128)(2,1)S(1)} all-to-all(bf16[16,16,306]{2,1,0:T(8,128)(2,1)S(1)} %pad_maximum_fusion), channel_id=1, replica_groups=mesh['xl'=2,'yb'=2,'ya'=4,'c'=2,'xh'=2,'z2'=3,'z1'=4] {'xl','c','z1'}, dimensions={0} | all-to-all | bytes 313344 | tf_op jit(solution)/shard_map/all_to_all | solution.py:26
  89.2 0.2 fusion.15
  89.5 11.8 %all_to_all.31 = bf16[16,16,304]{2,1,0:T(8,128)(2,1)S(1)} all-to-all(bf16[16,16,304]{2,1,0:T(8,128)(2,1)S(1)} %broadcast_in_dim.7), channel_id=1, replica_groups=mesh['xl'=2,'yb'=2,'ya'=4,'c'=2,'xh'=2,'z2'=3,'z1'=4] {'xl','c','z1'}, dimensions={0} | all-to-all | bytes 311296 | tf_op jit(solution)/shard_map/all_to_all | solution.py:26
  101.2 0.2 convolution_convert_fusion
  101.5 0.2 convolution_convert_fusion.1
  101.9 17.8 %all_to_all.32 = bf16[64,4,256]{2,1,0:T(4,128)(2,1)S(1)} all-to-all(bf16[64,4,256]{2,1,0:T(4,128)(2,1)S(1)} %reshape.150), channel_id=1, replica_groups=mesh['xl'=2,'yb'=2,'ya'=4,'c'=2,'xh'=2,'z2'=3,'z1'=4] {'xl','yb','ya','c..., dimensions={0} | all-to-all | bytes 262144 | tf_op jit(solution)/shard_map/all_to_all | solution.py:26
  119.7 0.1 reshape.157
  120.1 20.8 %all_to_all.33 = bf16[24,4,1024]{2,1,0:T(4,128)(2,1)S(1)} all-to-all(bf16[24,4,1024]{2,1,0:T(4,128)(2,1)S(1)} %broadcast_in_dim.8), channel_id=1, replica_groups=mesh['xl'=2,'yb'=2,'ya'=4,'c'=2,'xh'=2,'z2'=3,'z1'=4] {'xh','z2','z1'}, dimensions={0} | all-to-all | bytes 393216 | tf_op jit(solution)/shard_map/all_to_all | solution.py:26
  141.1 0.6 reshape.153
  (54 shorter events, 1.9 us)
Async XLA Ops:
  0.0 21.7 %copy-start = (f32[4096]{0:T(1024)S(1)}, f32[4096]{0:T(1024)}, u32[]{:S(2)}) copy-start(f32[4096]{0:T(1024)} %param.17) | copy-start | bytes 49156
  3.7 18.1 %copy-start.3 = (bf16[4,2,4096]{2,1,0:T(2,128)(2,1)S(1)}, bf16[4,2,4096]{2,1,0:T(2,128)(2,1)}, u32[]{:S(2)}) copy-start(bf16[4,2,4096]{2,1,0:T(2,128)(2,1)} %param.16) | copy-start | bytes 196612
  3.7 35.4 %all-to-all-start = ((bf16[24,40,128]{2,1,0:T(8,128)(2,1)}), bf16[24,40,128]{2,1,0:T(8,128)(2,1)S(1)}, u32[]{:S(2)}, u32[]{:S(2)}) async-start(bf16[24,40,128]{2,1,0:T(8,128)(2,1)} %attend.1), calls=%async_computation | async-start | bytes 491520 | tf_op jit(solution)/shard_map/all_to_all | solution.py:26
  39.8 9.0 %copy-start.2 = (f32[128,600]{0,1:T(8,128)S(1)}, f32[128,600]{0,1:T(8,128)}, u32[]{:S(2)}) copy-start(f32[128,600]{0,1:T(8,128)} %param.18) | copy-start | bytes 921604
  39.9 8.9 %copy-start.1 = (f32[128,600]{0,1:T(8,128)S(1)}, f32[128,600]{0,1:T(8,128)}, u32[]{:S(2)}) copy-start(f32[128,600]{0,1:T(8,128)} %param.19) | copy-start | bytes 921604
  40.6 18.5 %all-to-all-start.1 = ((bf16[64,4,256]{2,1,0:T(4,128)(2,1)}), bf16[64,4,256]{2,1,0:T(4,128)(2,1)S(1)}, u32[]{:S(2)}, u32[]{:S(2)}) async-start(bf16[64,4,256]{2,1,0:T(4,128)(2,1)} %reshape.144), calls=%async_computation.1 | async-start | bytes 262144 | tf_op jit(solution)/shard_map/all_to_all | solution.py:26
  49.0 28.8 %collective-permute-start = (bf16[2,304,128]{2,1,0:T(8,128)(2,1)S(1)}, bf16[2,304,128]{2,1,0:T(8,128)(2,1)S(1)}, u32[]{:S(2)}, u32[]{:S(2)}) collective-permute-start(bf16[2,304,128]{2,1,0:T(8,128)(2,1)S(1)} %get-tuple-element.15), channel_id=1, source_target_pairs={{0,0},{1,48},{2,96},{3,144},{192,192},{193,240},{194,288},{195,336... | collective-permute-start | bytes 466952 | tf_op jit(solution)/shard_map/ppermute | solution.py:52
  51.0 26.6 %collective-permute-start.1 = (bf16[2,304,128]{2,1,0:T(8,128)(2,1)S(1)}, bf16[2,304,128]{2,1,0:T(8,128)(2,1)S(1)}, u32[]{:S(2)}, u32[]{:S(2)}) collective-permute-start(bf16[2,304,128]{2,1,0:T(8,128)(2,1)S(1)} %get-tuple-element.16), channel_id=1, source_target_pairs={{0,192},{1,240},{2,288},{3,336},{192,0},{193,48},{194,96},{195,144... | collective-permute-start | bytes 466952 | tf_op jit(solution)/shard_map/ppermute | solution.py:52
